TPU v7x, 128 devices: a whole 4x4x4 slice. The times are simulated.
128 devices in a mesh: bx: 8 (over y, x_hi), by: 16 (over x_lo, z, core).
Axes of the slice: x: 4 (x_hi: 2, x_lo: 2; x = x_hi * 2 + x_lo), y: 4, z: 4, core: 2. Of those that a mesh axis runs over, the one named last changes fastest.
Arguments:
- speed_vectors: float32 [3, 6, 120, 240, 128], P(None, None, 'bx', 'by'), may hold values from -10 to 10, as said below
- bin_population: int32 [120, 240, 128], P('bx', 'by'), may hold values from 0 to 6, as said below
- spin_choice: int32 [12, 120, 240, 128], P(None, 'bx', 'by'), may hold values from 0 to 5
- approval_flags: int32 [12, 120, 240, 128], P(None, 'bx', 'by'), may hold values 0 or 1
- round_evenness: int32 [12], replicated, may hold values from 0 to 1
- grid_displacements: int32 [12], replicated, may hold values from 0 to 127
- thermostat_heat_level: float32 [12], replicated, may hold values from 0.5 to 2
Outputs:
- final_velocity: float32 [3, 6, 120, 240, 128], P(None, None, 'bx', 'by')
Inputs may be any that keep to these rules, and one draw needn't show every extreme that they name: `bin_population`: A cell's particles fill its first slots. `speed_vectors`: entries in slots at or beyond a cell's occupancy are not read.
All inputs are finite; a program needn't handle non-finite values. No bound on the sum of `approval_flags` on one device may be relied on, other than what follows from the above.
Results may differ from a plain program's by a relative error of at most 0.0003.
Values sent between devices are 32-bit elements; how exact they have to be, the bound alone decides.
No kernel may reach another device: no remote copies, remote signals or barrier semaphores. Data moves between devices by JAX's collectives and lax.ppermute only.
A program may use at most 64 MiB of HBM per device.

v0:
```python
import math

import jax
import jax.numpy as jnp
from jax import lax
from jax.sharding import Mesh
from jax.sharding import PartitionSpec as P

ROUNDS = 6
BX_BY = ("bx_0", "bx_1", "by_0", "by_1", "by_2")
BX = ("bx_0", "bx_1")
BY = ("by_0", "by_1", "by_2")


turn_angle = 130.0 * math.pi / 180.0
drag_gain = 1.0
excess_coupling = 1e-06


def over_axes(array, axes):
    for axis in axes:
        array = lax.psum(array, axis)
    return array


def from_behind(value, axis, steps):
    count = lax.axis_size(axis)
    pairs = [(source, (source + steps) % count) for source in range(count)]
    return lax.ppermute(value, axis, pairs)


def rotate(thermal, spin_choice):
    picked = spin_choice // 2
    unit_axis = [(picked == member).astype(jnp.float32)[None] for member in range(3)]
    sine_term = (math.sin(turn_angle) * (1 - 2 * (spin_choice % 2)).astype(jnp.float32))[None]
    cosine_term = math.cos(turn_angle)
    along_axis = unit_axis[0] * thermal[0] + unit_axis[1] * thermal[1] + unit_axis[2] * thermal[2]
    result = []
    for member in range(3):
        second = (member + 1) % 3
        third_idx = (member + 2) % 3
        cross_term = unit_axis[second] * thermal[third_idx] - unit_axis[third_idx] * thermal[second]
        result.append(
            cosine_term * thermal[member]
            + (1.0 - cosine_term) * unit_axis[member] * along_axis
            + sine_term * cross_term
        )
    return jnp.stack(result)


def per_device(
    speed_vectors,
    bin_population,
    spin_choice,
    approval_flags,
    round_evenness,
    grid_displacements,
    thermostat_heat_level,
):
    slot_count = speed_vectors.shape[1]
    overall_work_sum = over_axes(jnp.sum(bin_population.astype(jnp.float32)), BX_BY)

    def decode(received):
        return (received[1], received[0], received[2])

    def collide_step(
        ensemble_snapshot, bin_tallies, pending, present_round_number, partner_heading
    ):
        slot_rank = lax.broadcasted_iota(jnp.int32, (slot_count,) + bin_tallies.shape, 0)
        occupied = (slot_rank < bin_tallies[None]).astype(jnp.float32)
        moment = jnp.sum(ensemble_snapshot * occupied[None], axis=1)
        cell_mass = bin_tallies.astype(jnp.float32)
        safe_mass = jnp.maximum(cell_mass, 1.0)
        accept_bits = approval_flags[present_round_number].astype(jnp.float32)
        along_moment = moment[partner_heading]
        step_parity = round_evenness[present_round_number]
        stack_parts = (along_moment[None], cell_mass[None], accept_bits[None])
        extent = bin_tallies.shape[partner_heading]
        low_edge = jnp.concatenate(
            [
                lax.slice_in_dim(part_item, 0, 1, axis=partner_heading + 1)
                for part_item in stack_parts
            ],
            0,
        )
        high_edge = jnp.concatenate(
            [
                lax.slice_in_dim(part_item, extent - 1, extent, axis=partner_heading + 1)
                for part_item in stack_parts
            ],
            0,
        )
        if partner_heading == 0:
            start = lax.axis_index(BX) * extent
        else:
            start = lax.axis_index(BY) * extent
        if partner_heading == 0:
            from_above = from_behind(low_edge, BX, -1)
            from_below = from_behind(high_edge, BX, 1)
        else:
            from_above = from_behind(low_edge, BY, -1)
            from_below = from_behind(high_edge, BY, 1)
        above_parts = decode(from_above)
        below_parts = decode(from_below)
        coords = start + lax.broadcasted_iota(jnp.int32, bin_tallies.shape, partner_heading)
        is_lower = (coords - step_parity) % 2 == 0

        def partner(local_values, below_values, above_values):
            extended = jnp.concatenate([below_values, local_values, above_values], partner_heading)
            upper_side = lax.slice_in_dim(extended, 2, extent + 2, axis=partner_heading)
            lower_side = lax.slice_in_dim(extended, 0, extent, axis=partner_heading)
            return jnp.where(is_lower, upper_side, lower_side)

        other_mass = partner(cell_mass, below_parts[0], above_parts[0])
        other_moment = partner(along_moment, below_parts[1], above_parts[1])
        other_bits = partner(accept_bits, below_parts[2], above_parts[2])
        own_speed = pending * along_moment / safe_mass
        other_speed = pending * other_moment / jnp.maximum(other_mass, 1.0)
        closing = jnp.maximum(
            jnp.where(is_lower, own_speed - other_speed, other_speed - own_speed), 0.0
        )
        reduced = cell_mass * other_mass / jnp.maximum(cell_mass + other_mass, 1.0)
        transfer = (
            jnp.maximum(accept_bits, other_bits) * reduced * closing * jnp.tanh(drag_gain * closing)
        )
        new_along = pending * along_moment - jnp.where(is_lower, transfer, -transfer)
        true_moment = jnp.stack(
            [
                new_along if member == partner_heading else pending * moment[member]
                for member in range(3)
            ]
        )
        thermal = (ensemble_snapshot - (moment / safe_mass)[:, None]) * occupied[None]
        kinetic_local = jnp.sum(
            true_moment * true_moment / safe_mass
        ) + pending * pending * jnp.sum(thermal * thermal)
        motion_work_sum = over_axes(kinetic_local, BX_BY)
        speed_multiplier = jnp.sqrt(
            3.0
            * thermostat_heat_level[present_round_number]
            * overall_work_sum
            / (motion_work_sum + excess_coupling)
        )
        turned = rotate(thermal, spin_choice[present_round_number])
        return (
            speed_multiplier
            * ((true_moment / safe_mass)[:, None] * occupied[None] + pending * turned),
            pending,
        )

    def one_round(round_index, carry):
        ensemble_snapshot, bin_tallies, pending = carry
        for displacement_amount in range(2):
            present_round_number = 2 * round_index + displacement_amount
            ensemble_snapshot, pending = collide_step(
                ensemble_snapshot, bin_tallies, pending, present_round_number, displacement_amount
            )
            shift_by = grid_displacements[present_round_number]
            ensemble_snapshot = jnp.roll(ensemble_snapshot, shift_by, axis=4)
            bin_tallies = jnp.roll(bin_tallies, shift_by, axis=2)
        return (ensemble_snapshot, bin_tallies, pending)

    start_scale = jnp.ones((), jnp.float32)
    ensemble_snapshot, bin_tallies, pending = lax.fori_loop(
        0, ROUNDS, one_round, (speed_vectors, bin_population, start_scale)
    )
    return ensemble_snapshot


def solution(mesh):
    split = Mesh(mesh.devices.reshape(4, 2, 2, 4, 2), ("bx_0", "bx_1", "by_0", "by_1", "by_2"))
    return jax.shard_map(
        per_device,
        mesh=split,
        in_specs=(
            P(None, None, BX, BY, None),
            P(BX, BY, None),
            P(None, BX, BY, None),
            P(None, BX, BY, None),
            P(),
            P(),
            P(),
        ),
        out_specs=P(None, None, BX, BY, None),
        check_vma=False,
    )
```

profile of v0, /device:TPU:1, one launch (start us, length us, event | category | flops | bytes accessed | tf_op | source)
XLA Modules:
  0.0 786.2 jit_solution(3658337964983819190)
XLA Ops:
  4.7 10.2 %psum.185 = f32[]{:T(128)} all-reduce(f32[]{:T(128)} %convert_reduce_fusion), channel_id=1, replica_groups=mesh['bx_0'=4,'bx_1'=2,'by_0'=2,'by_1'=4,'by_2'=2] {'bx_0'}, use_global_device_ids=true, to_apply=%region_1.0 | all-reduce | flops 1 | bytes 8 | tf_op jit(solution)/shard_map/psum | solution.py:22
  25.2 10.4 %psum.188 = f32[]{:T(128)} all-reduce(f32[]{:T(128)} %psum.187), channel_id=1, replica_groups=mesh['bx_0'=4,'bx_1'=2,'by_0'=2,'by_1'=4,'by_2'=2] {'by_1'}, use_global_device_ids=true, to_apply=%region_4.0 | all-reduce | flops 1 | bytes 8 | tf_op jit(solution)/shard_map/psum | solution.py:22
  35.6 9.8 %psum.189 = f32[]{:T(128)} all-reduce(f32[]{:T(128)} %psum.188), channel_id=1, replica_groups=mesh['bx_0'=4,'bx_1'=2,'by_0'=2,'by_1'=4,'by_2'=2] {'by_2'}, use_global_device_ids=true, to_apply=%region_5.0 | all-reduce | flops 1 | bytes 8 | tf_op jit(solution)/shard_map/psum | solution.py:22
  45.4 740.8 %while.18 = (s32[]{:T(128)}, f32[3,6,15,15,128]{4,3,2,1,0:T(8,128)}, s32[15,15,128]{2,1,0:T(8,128)S(1)}, f32[12]{0:T(128)}, f32[]{:T(128)}, /*index=5*/s32[12]{0...) while((s32[]{:T(128)}, ...), condition=%wide.region_23.26_spmd, body=%wide.region_6.25_spmd.sunk | while | flops 29883296 | bytes 69046136 | solution.py:164
  101.7 9.4 %psum.204 = f32[]{:T(128)} all-reduce(f32[]{:T(128)} %psum.203), channel_id=1, replica_groups=mesh['bx_0'=4,'bx_1'=2,'by_0'=2,'by_1'=4,'by_2'=2] {'by_2'}, use_global_device_ids=true, to_apply=%region_14.14 | all-reduce | flops 1 | bytes 8 | tf_op jit(solution)/shard_map/while/body/eval_jaxpr/psum | solution.py:22
  142.5 10.0 %psum.208 = f32[]{:T(128)} all-reduce(f32[]{:T(128)} %psum.207), channel_id=1, replica_groups=mesh['bx_0'=4,'bx_1'=2,'by_0'=2,'by_1'=4,'by_2'=2] {'by_1'}, use_global_device_ids=true, to_apply=%region_21.23 | all-reduce | flops 1 | bytes 8 | tf_op jit(solution)/shard_map/while/body/eval_jaxpr/psum | solution.py:22
  152.6 9.6 %psum.209 = f32[]{:T(128)} all-reduce(f32[]{:T(128)} %psum.208), channel_id=1, replica_groups=mesh['bx_0'=4,'bx_1'=2,'by_0'=2,'by_1'=4,'by_2'=2] {'by_2'}, use_global_device_ids=true, to_apply=%region_22.24 | all-reduce | flops 1 | bytes 8 | tf_op jit(solution)/shard_map/while/body/eval_jaxpr/psum | solution.py:22
  205.3 7.6 psum.201
  218.6 8.3 %psum.203 = f32[]{:T(128)} all-reduce(f32[]{:T(128)} %psum.202), channel_id=1, replica_groups=mesh['bx_0'=4,'bx_1'=2,'by_0'=2,'by_1'=4,'by_2'=2] {'by_1'}, use_global_device_ids=true, to_apply=%region_13.13 | all-reduce | flops 1 | bytes 8 | tf_op jit(solution)/shard_map/while/body/eval_jaxpr/psum | solution.py:22
  227.5 9.7 %psum.204 = f32[]{:T(128)} all-reduce(f32[]{:T(128)} %psum.203), channel_id=1, replica_groups=mesh['bx_0'=4,'bx_1'=2,'by_0'=2,'by_1'=4,'by_2'=2] {'by_2'}, use_global_device_ids=true, to_apply=%region_14.14 | all-reduce | flops 1 | bytes 8 | tf_op jit(solution)/shard_map/while/body/eval_jaxpr/psum | solution.py:22
  267.6 8.3 %psum.208 = f32[]{:T(128)} all-reduce(f32[]{:T(128)} %psum.207), channel_id=1, replica_groups=mesh['bx_0'=4,'bx_1'=2,'by_0'=2,'by_1'=4,'by_2'=2] {'by_1'}, use_global_device_ids=true, to_apply=%region_21.23 | all-reduce | flops 1 | bytes 8 | tf_op jit(solution)/shard_map/while/body/eval_jaxpr/psum | solution.py:22
  275.9 9.0 %psum.209 = f32[]{:T(128)} all-reduce(f32[]{:T(128)} %psum.208), channel_id=1, replica_groups=mesh['bx_0'=4,'bx_1'=2,'by_0'=2,'by_1'=4,'by_2'=2] {'by_2'}, use_global_device_ids=true, to_apply=%region_22.24 | all-reduce | flops 1 | bytes 8 | tf_op jit(solution)/shard_map/while/body/eval_jaxpr/psum | solution.py:22
  328.6 8.0 %psum.201 = f32[]{:T(128)} all-reduce(f32[]{:T(128)} %psum.200), channel_id=1, replica_groups=mesh['bx_0'=4,'bx_1'=2,'by_0'=2,'by_1'=4,'by_2'=2] {'bx_1'}, use_global_device_ids=true, to_apply=%region_11.11 | all-reduce | flops 1 | bytes 8 | tf_op jit(solution)/shard_map/while/body/eval_jaxpr/psum | solution.py:22
  342.3 8.3 %psum.203 = f32[]{:T(128)} all-reduce(f32[]{:T(128)} %psum.202), channel_id=1, replica_groups=mesh['bx_0'=4,'bx_1'=2,'by_0'=2,'by_1'=4,'by_2'=2] {'by_1'}, use_global_device_ids=true, to_apply=%region_13.13 | all-reduce | flops 1 | bytes 8 | tf_op jit(solution)/shard_map/while/body/eval_jaxpr/psum | solution.py:22
  351.2 9.7 %psum.204 = f32[]{:T(128)} all-reduce(f32[]{:T(128)} %psum.203), channel_id=1, replica_groups=mesh['bx_0'=4,'bx_1'=2,'by_0'=2,'by_1'=4,'by_2'=2] {'by_2'}, use_global_device_ids=true, to_apply=%region_14.14 | all-reduce | flops 1 | bytes 8 | tf_op jit(solution)/shard_map/while/body/eval_jaxpr/psum | solution.py:22
  391.5 8.1 %psum.208 = f32[]{:T(128)} all-reduce(f32[]{:T(128)} %psum.207), channel_id=1, replica_groups=mesh['bx_0'=4,'bx_1'=2,'by_0'=2,'by_1'=4,'by_2'=2] {'by_1'}, use_global_device_ids=true, to_apply=%region_21.23 | all-reduce | flops 1 | bytes 8 | tf_op jit(solution)/shard_map/while/body/eval_jaxpr/psum | solution.py:22
  399.7 9.4 %psum.209 = f32[]{:T(128)} all-reduce(f32[]{:T(128)} %psum.208), channel_id=1, replica_groups=mesh['bx_0'=4,'bx_1'=2,'by_0'=2,'by_1'=4,'by_2'=2] {'by_2'}, use_global_device_ids=true, to_apply=%region_22.24 | all-reduce | flops 1 | bytes 8 | tf_op jit(solution)/shard_map/while/body/eval_jaxpr/psum | solution.py:22
  452.7 8.0 %psum.201 = f32[]{:T(128)} all-reduce(f32[]{:T(128)} %psum.200), channel_id=1, replica_groups=mesh['bx_0'=4,'bx_1'=2,'by_0'=2,'by_1'=4,'by_2'=2] {'bx_1'}, use_global_device_ids=true, to_apply=%region_11.11 | all-reduce | flops 1 | bytes 8 | tf_op jit(solution)/shard_map/while/body/eval_jaxpr/psum | solution.py:22
  466.4 8.3 %psum.203 = f32[]{:T(128)} all-reduce(f32[]{:T(128)} %psum.202), channel_id=1, replica_groups=mesh['bx_0'=4,'bx_1'=2,'by_0'=2,'by_1'=4,'by_2'=2] {'by_1'}, use_global_device_ids=true, to_apply=%region_13.13 | all-reduce | flops 1 | bytes 8 | tf_op jit(solution)/shard_map/while/body/eval_jaxpr/psum | solution.py:22
  475.3 9.7 %psum.204 = f32[]{:T(128)} all-reduce(f32[]{:T(128)} %psum.203), channel_id=1, replica_groups=mesh['bx_0'=4,'bx_1'=2,'by_0'=2,'by_1'=4,'by_2'=2] {'by_2'}, use_global_device_ids=true, to_apply=%region_14.14 | all-reduce | flops 1 | bytes 8 | tf_op jit(solution)/shard_map/while/body/eval_jaxpr/psum | solution.py:22
  515.4 8.3 %psum.208 = f32[]{:T(128)} all-reduce(f32[]{:T(128)} %psum.207), channel_id=1, replica_groups=mesh['bx_0'=4,'bx_1'=2,'by_0'=2,'by_1'=4,'by_2'=2] {'by_1'}, use_global_device_ids=true, to_apply=%region_21.23 | all-reduce | flops 1 | bytes 8 | tf_op jit(solution)/shard_map/while/body/eval_jaxpr/psum | solution.py:22
  523.8 9.0 %psum.209 = f32[]{:T(128)} all-reduce(f32[]{:T(128)} %psum.208), channel_id=1, replica_groups=mesh['bx_0'=4,'bx_1'=2,'by_0'=2,'by_1'=4,'by_2'=2] {'by_2'}, use_global_device_ids=true, to_apply=%region_22.24 | all-reduce | flops 1 | bytes 8 | tf_op jit(solution)/shard_map/while/body/eval_jaxpr/psum | solution.py:22
  576.5 8.0 %psum.201 = f32[]{:T(128)} all-reduce(f32[]{:T(128)} %psum.200), channel_id=1, replica_groups=mesh['bx_0'=4,'bx_1'=2,'by_0'=2,'by_1'=4,'by_2'=2] {'bx_1'}, use_global_device_ids=true, to_apply=%region_11.11 | all-reduce | flops 1 | bytes 8 | tf_op jit(solution)/shard_map/while/body/eval_jaxpr/psum | solution.py:22
  590.1 8.3 %psum.203 = f32[]{:T(128)} all-reduce(f32[]{:T(128)} %psum.202), channel_id=1, replica_groups=mesh['bx_0'=4,'bx_1'=2,'by_0'=2,'by_1'=4,'by_2'=2] {'by_1'}, use_global_device_ids=true, to_apply=%region_13.13 | all-reduce | flops 1 | bytes 8 | tf_op jit(solution)/shard_map/while/body/eval_jaxpr/psum | solution.py:22
  599.1 9.7 %psum.204 = f32[]{:T(128)} all-reduce(f32[]{:T(128)} %psum.203), channel_id=1, replica_groups=mesh['bx_0'=4,'bx_1'=2,'by_0'=2,'by_1'=4,'by_2'=2] {'by_2'}, use_global_device_ids=true, to_apply=%region_14.14 | all-reduce | flops 1 | bytes 8 | tf_op jit(solution)/shard_map/while/body/eval_jaxpr/psum | solution.py:22
  639.4 8.1 %psum.208 = f32[]{:T(128)} all-reduce(f32[]{:T(128)} %psum.207), channel_id=1, replica_groups=mesh['bx_0'=4,'bx_1'=2,'by_0'=2,'by_1'=4,'by_2'=2] {'by_1'}, use_global_device_ids=true, to_apply=%region_21.23 | all-reduce | flops 1 | bytes 8 | tf_op jit(solution)/shard_map/while/body/eval_jaxpr/psum | solution.py:22
  647.5 9.4 %psum.209 = f32[]{:T(128)} all-reduce(f32[]{:T(128)} %psum.208), channel_id=1, replica_groups=mesh['bx_0'=4,'bx_1'=2,'by_0'=2,'by_1'=4,'by_2'=2] {'by_2'}, use_global_device_ids=true, to_apply=%region_22.24 | all-reduce | flops 1 | bytes 8 | tf_op jit(solution)/shard_map/while/body/eval_jaxpr/psum | solution.py:22
  700.6 8.0 %psum.201 = f32[]{:T(128)} all-reduce(f32[]{:T(128)} %psum.200), channel_id=1, replica_groups=mesh['bx_0'=4,'bx_1'=2,'by_0'=2,'by_1'=4,'by_2'=2] {'bx_1'}, use_global_device_ids=true, to_apply=%region_11.11 | all-reduce | flops 1 | bytes 8 | tf_op jit(solution)/shard_map/while/body/eval_jaxpr/psum | solution.py:22
  714.2 8.3 %psum.203 = f32[]{:T(128)} all-reduce(f32[]{:T(128)} %psum.202), channel_id=1, replica_groups=mesh['bx_0'=4,'bx_1'=2,'by_0'=2,'by_1'=4,'by_2'=2] {'by_1'}, use_global_device_ids=true, to_apply=%region_13.13 | all-reduce | flops 1 | bytes 8 | tf_op jit(solution)/shard_map/while/body/eval_jaxpr/psum | solution.py:22
  723.2 9.7 %psum.204 = f32[]{:T(128)} all-reduce(f32[]{:T(128)} %psum.203), channel_id=1, replica_groups=mesh['bx_0'=4,'bx_1'=2,'by_0'=2,'by_1'=4,'by_2'=2] {'by_2'}, use_global_device_ids=true, to_apply=%region_14.14 | all-reduce | flops 1 | bytes 8 | tf_op jit(solution)/shard_map/while/body/eval_jaxpr/psum | solution.py:22
  763.3 8.3 %psum.208 = f32[]{:T(128)} all-reduce(f32[]{:T(128)} %psum.207), channel_id=1, replica_groups=mesh['bx_0'=4,'bx_1'=2,'by_0'=2,'by_1'=4,'by_2'=2] {'by_1'}, use_global_device_ids=true, to_apply=%region_21.23 | all-reduce | flops 1 | bytes 8 | tf_op jit(solution)/shard_map/while/body/eval_jaxpr/psum | solution.py:22
  771.6 9.0 %psum.209 = f32[]{:T(128)} all-reduce(f32[]{:T(128)} %psum.208), channel_id=1, replica_groups=mesh['bx_0'=4,'bx_1'=2,'by_0'=2,'by_1'=4,'by_2'=2] {'by_2'}, use_global_device_ids=true, to_apply=%region_22.24 | all-reduce | flops 1 | bytes 8 | tf_op jit(solution)/shard_map/while/body/eval_jaxpr/psum | solution.py:22
  (497 shorter events, 445.7 us)
Async XLA Ops:
  0.9 44.5 %copy-start.8 = (s32[12]{0:T(128)S(1)}, s32[12]{0:T(128)}, u32[]{:S(2)}) copy-start(s32[12]{0:T(128)} %param.17) | copy-start | bytes 148
  0.9 44.5 %copy-start.10 = (s32[12]{0:T(128)S(1)}, s32[12]{0:T(128)}, u32[]{:S(2)}) copy-start(s32[12]{0:T(128)} %param.18) | copy-start | bytes 148
  52.0 13.9 %collective-permute-start.1 = (f32[3,1,15,128]{3,2,1,0:T(8,128)}, f32[3,1,15,128]{3,2,1,0:T(8,128)}, u32[]{:S(2)}, u32[]{:S(2)}) collective-permute-start(f32[3,1,15,128]{3,2,1,0:T(8,128)} %pad_maximum_fusion.23), channel_id=1, source_target_pairs={{0,112},{16,0},{32,16},{48,32},{64,48},{80,64},{96,80},{112,96},{1... | collective-permute-start | bytes 69128 | tf_op jit(solution)/shard_map/while/body/eval_jaxpr/ppermute | solution.py:29
  54.5 12.2 %collective-permute-start = (f32[3,1,15,128]{3,2,1,0:T(8,128)}, f32[3,1,15,128]{3,2,1,0:T(8,128)}, u32[]{:S(2)}, u32[]{:S(2)}) collective-permute-start(f32[3,1,15,128]{3,2,1,0:T(8,128)} %pad_maximum_fusion.22), channel_id=1, source_target_pairs={{0,16},{16,32},{32,48},{48,64},{64,80},{80,96},{96,112},{112,0},{1... | collective-permute-start | bytes 69128 | tf_op jit(solution)/shard_map/while/body/eval_jaxpr/ppermute | solution.py:29
  115.8 3.5 collective-permute-start.3
  116.2 3.1 collective-permute-start.2
  174.4 14.6 %collective-permute-start.1 = (f32[3,1,15,128]{3,2,1,0:T(8,128)}, f32[3,1,15,128]{3,2,1,0:T(8,128)}, u32[]{:S(2)}, u32[]{:S(2)}) collective-permute-start(f32[3,1,15,128]{3,2,1,0:T(8,128)} %pad_maximum_fusion.23), channel_id=1, source_target_pairs={{0,112},{16,0},{32,16},{48,32},{64,48},{80,64},{96,80},{112,96},{1... | collective-permute-start | bytes 69128 | tf_op jit(solution)/shard_map/while/body/eval_jaxpr/ppermute | solution.py:29
  178.6 11.2 %collective-permute-start = (f32[3,1,15,128]{3,2,1,0:T(8,128)}, f32[3,1,15,128]{3,2,1,0:T(8,128)}, u32[]{:S(2)}, u32[]{:S(2)}) collective-permute-start(f32[3,1,15,128]{3,2,1,0:T(8,128)} %pad_maximum_fusion.22), channel_id=1, source_target_pairs={{0,16},{16,32},{32,48},{48,64},{64,80},{80,96},{96,112},{112,0},{1... | collective-permute-start | bytes 69128 | tf_op jit(solution)/shard_map/while/body/eval_jaxpr/ppermute | solution.py:29
  193.5 44.5 %copy-start.3 = (f32[15,15,128]{2,1,0:T(8,128)S(1)}, f32[15,15,128]{2,1,0:T(8,128)}, u32[]{:S(2)}) copy-start(f32[15,15,128]{2,1,0:T(8,128)} %get-tuple-element.556) | copy-start | bytes 345604 | tf_op jit(solution)/shard_map/while
  241.9 3.3 collective-permute-start.3
  242.3 2.9 collective-permute-start.2
  297.0 15.6 %collective-permute-start.1 = (f32[3,1,15,128]{3,2,1,0:T(8,128)}, f32[3,1,15,128]{3,2,1,0:T(8,128)}, u32[]{:S(2)}, u32[]{:S(2)}) collective-permute-start(f32[3,1,15,128]{3,2,1,0:T(8,128)} %pad_maximum_fusion.23), channel_id=1, source_target_pairs={{0,112},{16,0},{32,16},{48,32},{64,48},{80,64},{96,80},{112,96},{1... | collective-permute-start | bytes 69128 | tf_op jit(solution)/shard_map/while/body/eval_jaxpr/ppermute | solution.py:29
  302.3 11.2 %collective-permute-start = (f32[3,1,15,128]{3,2,1,0:T(8,128)}, f32[3,1,15,128]{3,2,1,0:T(8,128)}, u32[]{:S(2)}, u32[]{:S(2)}) collective-permute-start(f32[3,1,15,128]{3,2,1,0:T(8,128)} %pad_maximum_fusion.22), channel_id=1, source_target_pairs={{0,16},{16,32},{32,48},{48,64},{64,80},{80,96},{96,112},{112,0},{1... | collective-permute-start | bytes 69128 | tf_op jit(solution)/shard_map/while/body/eval_jaxpr/ppermute | solution.py:29
  317.2 44.5 %copy-start.2 = (f32[15,15,128]{2,1,0:T(8,128)S(1)}, f32[15,15,128]{2,1,0:T(8,128)}, u32[]{:S(2)}) copy-start(f32[15,15,128]{2,1,0:T(8,128)} %get-tuple-element.561) | copy-start | bytes 345604 | tf_op jit(solution)/shard_map/while
  317.2 44.5 %copy-start.3 = (f32[15,15,128]{2,1,0:T(8,128)S(1)}, f32[15,15,128]{2,1,0:T(8,128)}, u32[]{:S(2)}) copy-start(f32[15,15,128]{2,1,0:T(8,128)} %get-tuple-element.556) | copy-start | bytes 345604 | tf_op jit(solution)/shard_map/while
  365.6 3.3 collective-permute-start.3
  366.1 2.9 collective-permute-start.2
  421.1 15.6 %collective-permute-start.1 = (f32[3,1,15,128]{3,2,1,0:T(8,128)}, f32[3,1,15,128]{3,2,1,0:T(8,128)}, u32[]{:S(2)}, u32[]{:S(2)}) collective-permute-start(f32[3,1,15,128]{3,2,1,0:T(8,128)} %pad_maximum_fusion.23), channel_id=1, source_target_pairs={{0,112},{16,0},{32,16},{48,32},{64,48},{80,64},{96,80},{112,96},{1... | collective-permute-start | bytes 69128 | tf_op jit(solution)/shard_map/while/body/eval_jaxpr/ppermute | solution.py:29
  426.5 11.2 %collective-permute-start = (f32[3,1,15,128]{3,2,1,0:T(8,128)}, f32[3,1,15,128]{3,2,1,0:T(8,128)}, u32[]{:S(2)}, u32[]{:S(2)}) collective-permute-start(f32[3,1,15,128]{3,2,1,0:T(8,128)} %pad_maximum_fusion.22), channel_id=1, source_target_pairs={{0,16},{16,32},{32,48},{48,64},{64,80},{80,96},{96,112},{112,0},{1... | collective-permute-start | bytes 69128 | tf_op jit(solution)/shard_map/while/body/eval_jaxpr/ppermute | solution.py:29
  441.3 44.5 %copy-start.3 = (f32[15,15,128]{2,1,0:T(8,128)S(1)}, f32[15,15,128]{2,1,0:T(8,128)}, u32[]{:S(2)}) copy-start(f32[15,15,128]{2,1,0:T(8,128)} %get-tuple-element.556) | copy-start | bytes 345604 | tf_op jit(solution)/shard_map/while
  489.8 3.3 collective-permute-start.3
  490.2 2.9 collective-permute-start.2
  544.9 15.6 %collective-permute-start.1 = (f32[3,1,15,128]{3,2,1,0:T(8,128)}, f32[3,1,15,128]{3,2,1,0:T(8,128)}, u32[]{:S(2)}, u32[]{:S(2)}) collective-permute-start(f32[3,1,15,128]{3,2,1,0:T(8,128)} %pad_maximum_fusion.23), channel_id=1, source_target_pairs={{0,112},{16,0},{32,16},{48,32},{64,48},{80,64},{96,80},{112,96},{1... | collective-permute-start | bytes 69128 | tf_op jit(solution)/shard_map/while/body/eval_jaxpr/ppermute | solution.py:29
  550.2 11.2 %collective-permute-start = (f32[3,1,15,128]{3,2,1,0:T(8,128)}, f32[3,1,15,128]{3,2,1,0:T(8,128)}, u32[]{:S(2)}, u32[]{:S(2)}) collective-permute-start(f32[3,1,15,128]{3,2,1,0:T(8,128)} %pad_maximum_fusion.22), channel_id=1, source_target_pairs={{0,16},{16,32},{32,48},{48,64},{64,80},{80,96},{96,112},{112,0},{1... | collective-permute-start | bytes 69128 | tf_op jit(solution)/shard_map/while/body/eval_jaxpr/ppermute | solution.py:29
  565.0 44.5 %copy-start.3 = (f32[15,15,128]{2,1,0:T(8,128)S(1)}, f32[15,15,128]{2,1,0:T(8,128)}, u32[]{:S(2)}) copy-start(f32[15,15,128]{2,1,0:T(8,128)} %get-tuple-element.556) | copy-start | bytes 345604 | tf_op jit(solution)/shard_map/while
  613.5 3.3 collective-permute-start.3
  613.9 2.9 collective-permute-start.2
  669.0 15.6 %collective-permute-start.1 = (f32[3,1,15,128]{3,2,1,0:T(8,128)}, f32[3,1,15,128]{3,2,1,0:T(8,128)}, u32[]{:S(2)}, u32[]{:S(2)}) collective-permute-start(f32[3,1,15,128]{3,2,1,0:T(8,128)} %pad_maximum_fusion.23), channel_id=1, source_target_pairs={{0,112},{16,0},{32,16},{48,32},{64,48},{80,64},{96,80},{112,96},{1... | collective-permute-start | bytes 69128 | tf_op jit(solution)/shard_map/while/body/eval_jaxpr/ppermute | solution.py:29
  674.3 11.2 %collective-permute-start = (f32[3,1,15,128]{3,2,1,0:T(8,128)}, f32[3,1,15,128]{3,2,1,0:T(8,128)}, u32[]{:S(2)}, u32[]{:S(2)}) collective-permute-start(f32[3,1,15,128]{3,2,1,0:T(8,128)} %pad_maximum_fusion.22), channel_id=1, source_target_pairs={{0,16},{16,32},{32,48},{48,64},{64,80},{80,96},{96,112},{112,0},{1... | collective-permute-start | bytes 69128 | tf_op jit(solution)/shard_map/while/body/eval_jaxpr/ppermute | solution.py:29
  689.2 44.5 %copy-start.3 = (f32[15,15,128]{2,1,0:T(8,128)S(1)}, f32[15,15,128]{2,1,0:T(8,128)}, u32[]{:S(2)}) copy-start(f32[15,15,128]{2,1,0:T(8,128)} %get-tuple-element.556) | copy-start | bytes 345604 | tf_op jit(solution)/shard_map/while
  737.6 3.3 collective-permute-start.3
  738.0 2.9 collective-permute-start.2
  (54 other events, 772.5 us)
where the time goes:
time: 790 us; the launch traced here: 786 us
  blocking collectives  472 us (60%)
  other arithmetic  171 us (22%)
  loops' own time  65 us (8%)
  starting transfers between devices  37 us (5%)
  local copies, waits for them, and re-layouts  33.5 us (4%)
  waiting for transfers between devices  8.4 us (1%)
    psum x65, blocking collectives, over_axes(): array = lax.psum(array, axis)  472 us
    another operation x1, loops' own time, per_device(): lax.fori_loop(0, ROUNDS, one_round, (speed_vectors, bin_population, start...  65 us
    ppermute x24, starting transfers between devices, from_behind(): return lax.ppermute(value, axis, pairs)  37 us
    reduce_sum x12, other arithmetic, collide_step(): jnp.sum(thermal * thermal)  26.1 us
    add x12, other arithmetic, rotate(): cosine_term * thermal[member]  25.3 us
    reduce_sum x12, other arithmetic, collide_step(): moment = jnp.sum(ensemble_snapshot * occupied[None], axis=1)  18.5 us
  transfers between devices with their start and end apart: 24, of which 6 were waited for; matrix products, arithmetic and copies ran while one was open for 8% of the time, Pallas kernels for 0%

commit v1 on v0

v1 whole, which is shorter than its diff:
```python
import math

import jax
import jax.numpy as jnp
from jax import lax
from jax.experimental import pallas as pl
from jax.experimental.pallas import tpu as pltpu
from jax.sharding import PartitionSpec as P

STEPS = 12
HALF = STEPS // 2
SLOTS = 6
EXT = 15
PAD = 16
HALO = HALF
FULL = EXT + 2 * HALO
PAIRS = (FULL - 1) // 2
NZ = 128
DEVICES = 128
EDGE_PLANES = 2 * HALO + HALO * (HALO + 1) // 2
FIELDS = 2 + HALF

turn_angle = 130.0 * math.pi / 180.0
excess_coupling = 1e-06
BIG = 2.0**46
SCALE_CAP = 3e38
HALF_TAN = math.tan(turn_angle / 2.0)
TURN_NORM = math.cos(turn_angle / 2.0) ** (2 * STEPS)

VMEM = pl.BlockSpec(memory_space=pltpu.VMEM)
SMEM = pl.BlockSpec(memory_space=pltpu.SMEM)
f32 = jnp.float32


def shape(*dims):
    return jax.ShapeDtypeStruct(dims, f32)


def later_shifts(shift_ref, step):
    total = jnp.int32(0)
    for later in range(step, STEPS):
        total = total + shift_ref[later]
    return lax.rem(total, jnp.int32(NZ))


def edge_offsets():
    table = []
    place = 0
    for field in range(FIELDS):
        planes = HALO if field < 2 else HALO - (field - 2)
        table.append((field, place, planes))
        place += planes
    return table


def prep_kernel(shift_ref, v_ref, count_ref, flag_ref, sx_ref, sy_ref, xlo_ref, xhi_ref, ylo_ref, yhi_ref, uz_ref, base_ref, turn_ref):
    shift = later_shifts(shift_ref, 0)
    zero_row = jnp.zeros((EXT, 1, NZ), f32)
    for field in range(FIELDS):
        sx_ref[field, :, EXT:PAD, :] = zero_row
        turn_ref[field, EXT * PAD : PAD * PAD, :] = jnp.zeros((PAD, NZ), f32)
    uz_ref[:, EXT:PAD, :] = zero_row

    def plane(i, sums):
        thermal, energy_y, total = sums
        counts = count_ref[i]
        mass = counts.astype(f32)
        safe = jnp.maximum(mass, 1.0)
        inverse = 1.0 / safe
        mean = []
        for member in range(3):
            values = [
                jnp.where(counts > slot, v_ref[member, slot, i] * BIG, 0.0) for slot in range(SLOTS)
            ]
            moment = values[0]
            for slot in range(1, SLOTS):
                moment = moment + values[slot]
            middle = moment * inverse
            mean.append(middle)
            for slot in range(SLOTS):
                rest = jnp.where(counts > slot, values[slot] - middle, 0.0)
                thermal = thermal + rest * rest
        thermal = thermal + mass * mean[2] * mean[2]
        energy_y = energy_y + mass * mean[1] * mean[1]
        total = total + mass
        rolled = pltpu.roll(mass, shift, 1)
        sx_ref[0, i, 0:EXT, :] = pltpu.roll(mean[0], shift, 1)
        sx_ref[1, i, 0:EXT, :] = rolled
        uz_ref[i, 0:EXT, :] = pltpu.roll(mean[2], shift, 1)
        row = pl.multiple_of(i * PAD, PAD)
        turn_ref[0, pl.ds(row, EXT), :] = pltpu.roll(mean[1], shift, 1)
        turn_ref[1, pl.ds(row, EXT), :] = rolled
        return thermal, energy_y, total

    nothing = jnp.zeros((EXT, NZ), f32)
    thermal, energy_y, total = lax.fori_loop(0, EXT, plane, (nothing, nothing, nothing))
    base_ref[...] = jnp.zeros((8, NZ), f32)
    base_ref[0:1, :] = jnp.full((1, NZ), 1.0 / BIG, f32)
    base_ref[2:3, :] = jnp.sum(thermal, axis=0, keepdims=True)
    base_ref[4:5, :] = jnp.sum(energy_y, axis=0, keepdims=True)
    base_ref[5:6, :] = jnp.sum(total, axis=0, keepdims=True)

    for step in range(STEPS):
        later = later_shifts(shift_ref, step)
        field = 2 + step // 2

        def flags(i, carry, step=step, later=later, field=field):
            bits = pltpu.roll(flag_ref[step, i].astype(f32), later, 1)
            if step % 2 == 0:
                sx_ref[field, i, 0:EXT, :] = bits
            else:
                row = pl.multiple_of(i * PAD, PAD)
                turn_ref[field, pl.ds(row, EXT), :] = bits
            return carry

        lax.fori_loop(0, EXT, flags, 0)

    keep = lax.broadcasted_iota(jnp.int32, (PAD, NZ), 0) < EXT
    for field in range(FIELDS):
        for y in range(EXT):
            rows = turn_ref[field, pl.ds(y, PAD, stride=PAD), :]
            sy_ref[field, y] = jnp.where(keep, rows, 0.0)

    for field, place, planes in edge_offsets():
        for k in range(planes):
            xlo_ref[place + k] = sx_ref[field, k]
            xhi_ref[place + k] = sx_ref[field, EXT - planes + k]
            ylo_ref[place + k] = sy_ref[field, k]
            yhi_ref[place + k] = sy_ref[field, EXT - planes + k]


def prep(shifts, v, counts, flags):
    edge = shape(EDGE_PLANES, PAD, NZ)
    own = shape(FIELDS, EXT, PAD, NZ)
    return pl.pallas_call(
        prep_kernel,
        in_specs=[SMEM, VMEM, VMEM, VMEM],
        out_specs=[VMEM] * 8,
        out_shape=[own, own, edge, edge, edge, edge, shape(EXT, PAD, NZ), shape(8, NZ)],
        scratch_shapes=[pltpu.VMEM((FIELDS, PAD * PAD, NZ), f32)],
        name="prep",
    )(shifts, v, counts, flags)


def lower_start(parity_ref, step, brick_axis):
    return lax.rem(parity_ref[step] + lax.axis_index(brick_axis) * EXT, jnp.int32(2))


def join_kernel(parity_ref, own_ref, below_ref, above_ref, u_ref, *rest, first_step, brick_axis):
    weight_refs, (mass_ref, bits_ref) = rest[:HALF], rest[HALF:]
    for field, place, planes in edge_offsets():
        for k in range(planes):
            low, high = below_ref[place + k], above_ref[place + k]
            if field == 0:
                u_ref[HALO - planes + k] = low
                u_ref[HALO + EXT + k] = high
            elif field == 1:
                mass_ref[HALO - planes + k] = low
                mass_ref[HALO + EXT + k] = high
            else:
                bits_ref[field - 2, HALO - planes + k] = low
                bits_ref[field - 2, HALO + EXT + k] = high
        for k in range(HALO - planes):
            bits_ref[field - 2, k] = jnp.zeros((PAD, NZ), f32)
            bits_ref[field - 2, FULL - 1 - k] = jnp.zeros((PAD, NZ), f32)
    for k in range(EXT):
        u_ref[HALO + k] = own_ref[0, k]
        mass_ref[HALO + k] = own_ref[1, k]
        for j in range(HALF):
            bits_ref[j, HALO + k] = own_ref[2 + j, k]
    for j in range(HALF):
        start = lower_start(parity_ref, first_step + 2 * j, brick_axis)
        for k in range(PAIRS):
            plane = start + 2 * k
            mass_low, mass_high = mass_ref[plane], mass_ref[plane + 1]
            allowed = jnp.maximum(bits_ref[j, plane], bits_ref[j, plane + 1])
            reduced = allowed * mass_low * mass_high / jnp.maximum(mass_low + mass_high, 1.0)
            weight_refs[j][0, k] = reduced / jnp.maximum(mass_low, 1.0)
            weight_refs[j][1, k] = reduced / jnp.maximum(mass_high, 1.0)


def join(parity, own, below, above, first_step, brick_axis):
    def body(*refs):
        join_kernel(*refs, first_step=first_step, brick_axis=brick_axis)

    return pl.pallas_call(
        body,
        in_specs=[SMEM, VMEM, VMEM, VMEM],
        out_specs=[VMEM] * (1 + HALF),
        out_shape=[shape(FULL, PAD, NZ)] + [shape(2, PAIRS, PAD, NZ)] * HALF,
        scratch_shapes=[pltpu.VMEM((FULL, PAD, NZ), f32), pltpu.VMEM((HALF, FULL, PAD, NZ), f32)],
        name="join",
    )(parity, own, below, above)


def next_scale(received_ref, carry_ref, heat_ref, step):
    sums = jnp.sum(received_ref[...], axis=0, keepdims=True)
    scale = carry_ref[0:1, :]
    if step == 0:
        lane = lax.broadcasted_iota(jnp.int32, (1, NZ), 1)
        energy = jnp.sum(jnp.where(lane < NZ // 2, sums, 0.0), axis=1, keepdims=True)
        total = jnp.sum(jnp.where(lane < NZ // 2, 0.0, sums), axis=1, keepdims=True)
        total = jnp.broadcast_to(total, (1, NZ))
    else:
        energy = jnp.sum(sums, axis=1, keepdims=True)
        total = carry_ref[1:2, :]
    speed = scale * jnp.sqrt(jnp.broadcast_to(energy, (1, NZ)))
    factor = jnp.sqrt(3.0 * heat_ref[step] * total / (speed * speed + excess_coupling))
    return jnp.minimum(scale * factor, SCALE_CAP), total


def step_kernel(*refs, step, brick_axis):
    if step == 0:
        parity_ref, carry_ref, u_in_ref, weight_ref, own_ref, u_ref, rows_ref, out_ref = refs
        scale, total = carry_ref[0:1, :], jnp.zeros((1, NZ), f32)
    else:
        parity_ref, heat_ref, received_ref, carry_ref, u_in_ref, weight_ref, own_ref, u_ref, rows_ref, out_ref = refs
        scale, total = next_scale(received_ref, carry_ref, heat_ref, step - 1)
    wide = jnp.broadcast_to(scale, (PAD, NZ))
    start = lower_start(parity_ref, step, brick_axis)
    u_ref[0] = u_in_ref[0]
    u_ref[FULL - 1] = u_in_ref[FULL - 1]
    for k in range(PAIRS):
        plane = start + 2 * k
        low, high = u_in_ref[plane], u_in_ref[plane + 1]
        closing = jnp.maximum(low - high, 0.0)
        push = closing * jnp.tanh(wide * closing)
        u_ref[plane] = low - weight_ref[0, k] * push
        u_ref[plane + 1] = high + weight_ref[1, k] * push
    energy = jnp.zeros((PAD, NZ), f32)
    for k in range(EXT):
        u = u_ref[HALO + k]
        energy = energy + own_ref[1, k] * u * u
    mine = jnp.sum(energy, axis=0, keepdims=True)
    other = carry_ref[4:5, :] if step % 2 == 0 else carry_ref[3:4, :]
    local = carry_ref[2:3, :] + mine + other
    if step == 0:
        half = NZ // 2
        lane = lax.broadcasted_iota(jnp.int32, (1, NZ), 1)
        number = carry_ref[5:6, :]
        local = local + pltpu.roll(local, half, 1)
        number = number + pltpu.roll(number, half, 1)
        local = jnp.where(lane < half, local, number)
    out_ref[...] = carry_ref[...]
    out_ref[0:1, :] = scale
    out_ref[1:2, :] = total
    row = 3 if step % 2 == 0 else 4
    out_ref[row : row + 1, :] = mine
    rows_ref[...] = jnp.broadcast_to(local, (DEVICES, NZ))


def collide(step, parity, heat, received, carry, u, weight, own):
    brick_axis = "bx" if step % 2 == 0 else "by"

    def body(*refs):
        step_kernel(*refs, step=step, brick_axis=brick_axis)

    scalars = (parity,) if step == 0 else (parity, heat)
    arrays = (carry, u, weight, own) if step == 0 else (received, carry, u, weight, own)
    return pl.pallas_call(
        body,
        in_specs=[SMEM] * len(scalars) + [VMEM] * len(arrays),
        out_specs=[VMEM] * 3,
        out_shape=[shape(FULL, PAD, NZ), shape(DEVICES, NZ), shape(8, NZ)],
        name="collide",
    )(*scalars, *arrays)


def turn_kernel(shift_ref, v_ref, count_ref, spin_ref, w_ref):
    shifts = [later_shifts(shift_ref, step) for step in range(STEPS)]

    def plane(i, carry):
        real = jnp.ones((EXT, NZ), f32)
        parts = [jnp.zeros((EXT, NZ), f32)] * 3
        for step in range(STEPS):
            spin = pltpu.roll(spin_ref[step, i], shifts[step], 1)
            tangent = jnp.where((spin & 1) == 0, HALF_TAN, -HALF_TAN)
            on_x, on_y = spin < 2, spin < 4
            x, y, z = parts

            def pick(first, second, third):
                return tangent * jnp.where(on_x, first, jnp.where(on_y, second, third))

            real, parts = (
                real - pick(x, y, z),
                [x + pick(real, z, -y), y + pick(-z, real, x), z + pick(y, -x, real)],
            )
        x, y, z = parts
        unit = BIG * TURN_NORM
        xx, yy, zz, rr = x * x, y * y, z * z, real * real
        rows = [
            [(rr + xx) - (yy + zz), 2.0 * (x * y - real * z), 2.0 * (x * z + real * y)],
            [2.0 * (x * y + real * z), (rr + yy) - (xx + zz), 2.0 * (y * z - real * x)],
            [2.0 * (x * z - real * y), 2.0 * (y * z + real * x), (rr + zz) - (xx + yy)],
        ]
        rows = [[unit * value for value in row] for row in rows]
        counts = pltpu.roll(count_ref[i], shifts[0], 1)
        inverse = 1.0 / jnp.maximum(counts.astype(f32), 1.0)
        values = [
            [
                jnp.where(counts > slot, pltpu.roll(v_ref[member, slot, i], shifts[0], 1), 0.0)
                for slot in range(SLOTS)
            ]
            for member in range(3)
        ]
        mean = []
        for member in range(3):
            moment = values[member][0]
            for slot in range(1, SLOTS):
                moment = moment + values[member][slot]
            mean.append(moment * inverse)
        for slot in range(SLOTS):
            rest = [values[member][slot] - mean[member] for member in range(3)]
            for member in range(3):
                turned = rows[member][0] * rest[0] + rows[member][1] * rest[1] + rows[member][2] * rest[2]
                w_ref[member, slot, i] = turned
        return carry

    lax.fori_loop(0, EXT, plane, 0)


def turn(shifts, v, counts, spin):
    return pl.pallas_call(
        turn_kernel,
        in_specs=[SMEM, VMEM, VMEM, VMEM],
        out_specs=VMEM,
        out_shape=shape(3, SLOTS, EXT, EXT, NZ),
        name="turn",
    )(shifts, v, counts, spin)


def finish_kernel(heat_ref, received_ref, carry_ref, ux_ref, uy_ref, uz_ref, own_ref, w_ref, v_ref):
    scale, _ = next_scale(received_ref, carry_ref, heat_ref, STEPS - 1)
    wide = jnp.broadcast_to(scale, (EXT, NZ))
    for i in range(EXT):
        counts = own_ref[1, i, 0:EXT, :]
        mean = [
            ux_ref[HALO + i, 0:EXT, :],
            uy_ref[pl.ds(HALO * PAD + i, EXT, stride=PAD), :],
            uz_ref[i, 0:EXT, :],
        ]
        for member in range(3):
            for slot in range(SLOTS):
                value = wide * (mean[member] + w_ref[member, slot, i])
                v_ref[member, slot, i] = jnp.where(counts > slot, value, 0.0)


def finish(heat, received, carry, ux, uy, uz, own, w):
    return pl.pallas_call(
        finish_kernel,
        in_specs=[SMEM] + [VMEM] * 7,
        out_specs=VMEM,
        out_shape=shape(3, SLOTS, EXT, EXT, NZ),
        name="finish",
    )(heat, received, carry, ux, uy.reshape(FULL * PAD, NZ), uz, own, w)


def exchange(low_edge, high_edge, axis):
    count = lax.axis_size(axis)
    down = [(source, (source - 1) % count) for source in range(count)]
    up = [(source, (source + 1) % count) for source in range(count)]
    return lax.ppermute(low_edge, axis, down), lax.ppermute(high_edge, axis, up)


def per_device(v, counts, spin, flags, parity, shifts, heat):
    sx, sy, xlo, xhi, ylo, yhi, uz, carry = prep(shifts, v, counts, flags)
    x_above, x_below = exchange(xlo, xhi, "bx")
    y_above, y_below = exchange(ylo, yhi, "by")
    w = turn(shifts, v, counts, spin)
    ux, *x_weights = join(parity, sx, x_below, x_above, 0, "bx")
    uy, *y_weights = join(parity, sy, y_below, y_above, 1, "by")
    received = None
    for step in range(STEPS):
        if step % 2 == 0:
            ux, rows, carry = collide(step, parity, heat, received, carry, ux, x_weights[step // 2], sx)
        else:
            uy, rows, carry = collide(step, parity, heat, received, carry, uy, y_weights[step // 2], sy)
        received = lax.all_to_all(rows, ("bx", "by"), 0, 0, tiled=True)
    return finish(heat, received, carry, ux, uy, uz, sx, w)


def solution(mesh):
    return jax.shard_map(
        per_device,
        mesh=mesh,
        in_specs=(
            P(None, None, "bx", "by", None),
            P("bx", "by", None),
            P(None, "bx", "by", None),
            P(None, "bx", "by", None),
            P(),
            P(),
            P(),
        ),
        out_specs=P(None, None, "bx", "by", None),
        check_vma=False,
    )
```

time: 790 us -> 262 us (0.33)
  blocking collectives: 472 us -> 153 us
  other arithmetic: 171 us -> 0 us
  loops' own time: 65 us -> 0 us
  Pallas kernels: 0 us -> 62.4 us
  local copies, waits for them, and re-layouts: 33.5 us -> 2.76 us
  starting transfers between devices: 37 us -> 25.6 us
  waiting for transfers between devices: 8.4 us -> 17.1 us
    psum x65 -> x0, blocking collectives: 472 us -> none  [over_axes(): array = lax.psum(array, axis)]
    all_to_all x0 -> x10, blocking collectives: none -> 153 us  [per_device(): received = lax.all_to_all(rows, ('bx', 'by'), 0, 0, tiled=True)]
    another operation x1 -> x0, loops' own time: 65 us -> none  [per_device(): lax.fori_loop(0, ROUNDS, one_round, (speed_vectors, bin_population, start...]
    pallas_call x0 -> x17, Pallas kernels: none -> 62.4 us  [the longest x12 28.5 us: collide(): pl.pallas_call(body, in_specs=[SMEM] * len(scalars) + [VMEM] * len(arrays...]
    reduce_sum x37 -> x0, other arithmetic: 59.4 us -> none  [the longest x12 26.1 us: collide_step(): jnp.sum(thermal * thermal)]
    mul x48 -> x0, other arithmetic: 32.9 us -> none  [the longest x18 15.5 us: rotate(): (1.0 - cosine_term) * unit_axis[member] * along_axis]
    ppermute x24 -> x4, starting transfers between devices: 37 us -> 8.66 us  [the longest x2 6.13 us: exchange(): lax.ppermute(high_edge, axis, up)]
    add x24 -> x0, other arithmetic: 25.3 us -> none  [the longest x12 25.3 us: rotate(): cosine_term * thermal[member]]
  transfers between devices with their start and end apart: 24 -> 6, of which waited for: 6 -> 4; matrix products, arithmetic and copies ran while one was open for 8% -> 0% of each run, Pallas kernels for 0% -> 5%
where the time goes in v1:
time: 262 us; the launch traced here: 261 us
  blocking collectives  153 us (58%)
  Pallas kernels  62.4 us (24%)
  starting transfers between devices  25.6 us (10%)
  waiting for transfers between devices  17.1 us (7%)
  local copies, waits for them, and re-layouts  2.76 us (1%)
    all_to_all x10, blocking collectives, per_device(): received = lax.all_to_all(rows, ('bx', 'by'), 0, 0, tiled=True)  153 us
    pallas_call x12, Pallas kernels, collide(): pl.pallas_call(body, in_specs=[SMEM] * len(scalars) + [VMEM] * len(arrays...  28.5 us
    pallas_call x1, Pallas kernels, prep(): pl.pallas_call(prep_kernel, in_specs=[SMEM, VMEM, VMEM, VMEM], out_specs=...  18.3 us
    all_to_all x2, starting transfers between devices, per_device(): received = lax.all_to_all(rows, ('bx', 'by'), 0, 0, tiled=True)  16.9 us
    all_to_all x2, waiting for transfers between devices, per_device(): received = lax.all_to_all(rows, ('bx', 'by'), 0, 0, tiled=True)  9.05 us
    pallas_call x1, Pallas kernels, turn(): pl.pallas_call(turn_kernel, in_specs=[SMEM, VMEM, VMEM, VMEM], out_specs=...  6.54 us
    ppermute x2, starting transfers between devices, exchange(): lax.ppermute(high_edge, axis, up)  6.13 us
  transfers between devices with their start and end apart: 6, of which 4 were waited for; matrix products, arithmetic and copies ran while one was open for 0% of the time, Pallas kernels for 5%

profile of v1, /device:TPU:1, one launch (start us, length us, event | category | flops | bytes accessed | tf_op | source)
XLA Modules:
  0.0 261.1 jit_solution(1163772176483573752)
XLA Ops:
  0.0 18.3 %prep.1 = (f32[8,15,16,128]{3,2,1,0:T(8,128)}, f32[8,15,16,128]{3,2,1,0:T(8,128)}, f32[33,16,128]{2,1,0:T(8,128)}, f32[33,16,128]{2,1,0:T(8,128)}, f32[33,16,128...) custom-call(s32[12]{0:T(128)} %shift_ref.3, f32[3,6,15,15,128]{4,3,2,1,0:T(8,128)} %v_ref.3, ...), custom_call_target="tpu_custom_call" | custom-call | tf_op jit(solution)/shard_map/prep/pallas_call | solution.py:135
  18.3 3.6 %collective-permute-start = (f32[33,16,128]{2,1,0:T(8,128)}, f32[33,16,128]{2,1,0:T(8,128)S(1)}, u32[]{:S(2)}, u32[]{:S(2)}) collective-permute-start(f32[33,16,128]{2,1,0:T(8,128)} %get-tuple-element.65), channel_id=1, source_target_pairs={{0,16},{16,32},{32,48},{48,64},{64,80},{80,96},{96,112},{112,0},{1... | collective-permute-start | bytes 811016 | tf_op jit(solution)/shard_map/ppermute | solution.py:362
  21.9 2.5 collective-permute-start.1
  24.4 2.6 collective-permute-start.2
  27.0 3.7 %collective-permute-done.refs_2_ = f32[33,16,128]{2,1,0:T(8,128)S(1)} collective-permute-done((f32[33,16,128]{2,1,0:T(8,128)}, f32[33,16,128]{2,1,0:T(8,128)S(1)}, u32[]{:S(2)}, u32[]{:S(2)}) %collective-permute-start) | collective-permute-done | bytes 270368 | tf_op jit(solution)/shard_map/ppermute | solution.py:362
  30.6 4.4 %collective-permute-done.1.refs_3_ = f32[33,16,128]{2,1,0:T(8,128)S(1)} collective-permute-done((f32[33,16,128]{2,1,0:T(8,128)}, f32[33,16,128]{2,1,0:T(8,128)S(1)}, u32[]{:S(2)}, u32[]{:S(2)}) %collective-permute-start.1) | collective-permute-done | bytes 270368 | tf_op jit(solution)/shard_map/ppermute | solution.py:362
  35.7 2.6 join.2
  40.6 12.4 %all-to-all-start = ((f32[128,1,128]{2,1,0:T(1,128)}), f32[128,1,128]{2,1,0:T(1,128)S(1)}, u32[]{:S(2)}, u32[]{:S(2)}) async-start(f32[128,1,128]{2,1,0:T(1,128)} %bitcast.62), calls=%async_computation | async-start | bytes 131072 | tf_op jit(solution)/shard_map/all_to_all | solution.py:378
  53.8 2.6 join.3
  56.4 6.0 %all-to-all-done = f32[128,1,128]{2,1,0:T(1,128)S(1)} async-done(((f32[128,1,128]{2,1,0:T(1,128)}), f32[128,1,128]{2,1,0:T(1,128)S(1)}, u32[]{:S(2)}, u32[]{:S(2)}) %all-to-all-start) | async-done | bytes 65568 | tf_op jit(solution)/shard_map/all_to_all | solution.py:378
  63.0 2.4 collide.13
  65.4 15.3 %all_to_all.132 = f32[128,1,128]{2,1,0:T(1,128)} all-to-all(f32[128,1,128]{2,1,0:T(1,128)} %bitcast.64), channel_id=1, replica_groups=mesh['bx'=8,'by'=16] {'bx','by'}, dimensions={0} | all-to-all | bytes 131072 | tf_op jit(solution)/shard_map/all_to_all | solution.py:378
  80.7 2.4 collide.14
  83.1 15.2 %all_to_all.133 = f32[128,1,128]{2,1,0:T(1,128)} all-to-all(f32[128,1,128]{2,1,0:T(1,128)} %bitcast.65), channel_id=1, replica_groups=mesh['bx'=8,'by'=16] {'bx','by'}, dimensions={0} | all-to-all | bytes 131072 | tf_op jit(solution)/shard_map/all_to_all | solution.py:378
  98.3 2.4 collide.15
  100.7 15.4 %all_to_all.134 = f32[128,1,128]{2,1,0:T(1,128)} all-to-all(f32[128,1,128]{2,1,0:T(1,128)} %bitcast.66), channel_id=1, replica_groups=mesh['bx'=8,'by'=16] {'bx','by'}, dimensions={0} | all-to-all | bytes 131072 | tf_op jit(solution)/shard_map/all_to_all | solution.py:378
  116.0 2.4 collide.16
  118.4 15.1 %all_to_all.135 = f32[128,1,128]{2,1,0:T(1,128)} all-to-all(f32[128,1,128]{2,1,0:T(1,128)} %bitcast.67), channel_id=1, replica_groups=mesh['bx'=8,'by'=16] {'bx','by'}, dimensions={0} | all-to-all | bytes 131072 | tf_op jit(solution)/shard_map/all_to_all | solution.py:378
  135.9 15.4 %all_to_all.136 = f32[128,1,128]{2,1,0:T(1,128)} all-to-all(f32[128,1,128]{2,1,0:T(1,128)} %bitcast.68), channel_id=1, replica_groups=mesh['bx'=8,'by'=16] {'bx','by'}, dimensions={0} | all-to-all | bytes 131072 | tf_op jit(solution)/shard_map/all_to_all | solution.py:378
  153.6 15.3 %all_to_all.137 = f32[128,1,128]{2,1,0:T(1,128)} all-to-all(f32[128,1,128]{2,1,0:T(1,128)} %bitcast.69), channel_id=1, replica_groups=mesh['bx'=8,'by'=16] {'bx','by'}, dimensions={0} | all-to-all | bytes 131072 | tf_op jit(solution)/shard_map/all_to_all | solution.py:378
  169.0 2.4 collide.19
  171.4 15.3 %all_to_all.138 = f32[128,1,128]{2,1,0:T(1,128)} all-to-all(f32[128,1,128]{2,1,0:T(1,128)} %bitcast.70), channel_id=1, replica_groups=mesh['bx'=8,'by'=16] {'bx','by'}, dimensions={0} | all-to-all | bytes 131072 | tf_op jit(solution)/shard_map/all_to_all | solution.py:378
  189.0 15.4 %all_to_all.139 = f32[128,1,128]{2,1,0:T(1,128)} all-to-all(f32[128,1,128]{2,1,0:T(1,128)} %bitcast.71), channel_id=1, replica_groups=mesh['bx'=8,'by'=16] {'bx','by'}, dimensions={0} | all-to-all | bytes 131072 | tf_op jit(solution)/shard_map/all_to_all | solution.py:378
  204.4 2.4 collide.21
  206.8 15.5 %all_to_all.140 = f32[128,1,128]{2,1,0:T(1,128)} all-to-all(f32[128,1,128]{2,1,0:T(1,128)} %bitcast.72), channel_id=1, replica_groups=mesh['bx'=8,'by'=16] {'bx','by'}, dimensions={0} | all-to-all | bytes 131072 | tf_op jit(solution)/shard_map/all_to_all | solution.py:378
  222.3 2.4 collide.22
  224.7 15.4 %all_to_all.141 = f32[128,1,128]{2,1,0:T(1,128)} all-to-all(f32[128,1,128]{2,1,0:T(1,128)} %bitcast.73), channel_id=1, replica_groups=mesh['bx'=8,'by'=16] {'bx','by'}, dimensions={0} | all-to-all | bytes 131072 | tf_op jit(solution)/shard_map/all_to_all | solution.py:378
  240.0 2.4 collide.23
  242.4 4.5 %all-to-all-start.11 = ((f32[128,1,128]{2,1,0:T(1,128)}), f32[128,1,128]{2,1,0:T(1,128)S(1)}, u32[]{:S(2)}, u32[]{:S(2)}) async-start(f32[128,1,128]{2,1,0:T(1,128)} %bitcast.63), calls=%async_computation.11 | async-start | bytes 131072 | tf_op jit(solution)/shard_map/all_to_all | solution.py:378
  247.0 6.5 %turn.1.w_ref = f32[3,6,15,15,128]{4,3,2,1,0:T(8,128)} custom-call(s32[12]{0:T(128)} %shift_ref.3, f32[3,6,15,15,128]{4,3,2,1,0:T(8,128)} %v_ref.3, s32[15,15,128]{2,1,0:T(8,128)} %count_ref.3, s32[12,15,15,128]{3,2,1,0:T(8,128)} %spin_ref.1), custom_call_target="tpu_custom_call" | custom-call | tf_op jit(solution)/shard_map/turn/pallas_call | solution.py:323
  253.5 3.0 %all-to-all-done.11 = f32[128,1,128]{2,1,0:T(1,128)S(1)} async-done(((f32[128,1,128]{2,1,0:T(1,128)}), f32[128,1,128]{2,1,0:T(1,128)S(1)}, u32[]{:S(2)}, u32[]{:S(2)}) %all-to-all-start.11) | async-done | bytes 65568 | tf_op jit(solution)/shard_map/all_to_all | solution.py:378
  257.2 3.9 %finish.1 = f32[3,6,15,15,128]{4,3,2,1,0:T(8,128)} custom-call(f32[12]{0:T(128)} %heat_ref.1, f32[128,128]{1,0:T(8,128)} %bitcast.49, f32[8,128]{1,0:T(8,128)} %get-tuple-element.117.carry_ref, f32[27,16,128]{2,1,0:T(8,128)} %get-tuple-element.118.ux_ref, f32[432,128]{1,0:T(8,128)} %bitcast.61, f32[15,16,128]{2,1,0:T(8,128)} %get-tuple-element.120.uz_ref, ...), custom_call_target="tpu_custom_call" | custom-call | tf_op jit(solution)/shard_map/finish/pallas_call | solution.py:349
  (19 shorter events, 12.1 us)
Async XLA Ops:
  18.3 12.4 %collective-permute-start = (f32[33,16,128]{2,1,0:T(8,128)}, f32[33,16,128]{2,1,0:T(8,128)S(1)}, u32[]{:S(2)}, u32[]{:S(2)}) collective-permute-start(f32[33,16,128]{2,1,0:T(8,128)} %get-tuple-element.65), channel_id=1, source_target_pairs={{0,16},{16,32},{32,48},{48,64},{64,80},{80,96},{96,112},{112,0},{1... | collective-permute-start | bytes 811016 | tf_op jit(solution)/shard_map/ppermute | solution.py:362
  21.9 13.1 %collective-permute-start.1 = (f32[33,16,128]{2,1,0:T(8,128)}, f32[33,16,128]{2,1,0:T(8,128)S(1)}, u32[]{:S(2)}, u32[]{:S(2)}) collective-permute-start(f32[33,16,128]{2,1,0:T(8,128)} %get-tuple-element.66), channel_id=1, source_target_pairs={{0,112},{16,0},{32,16},{48,32},{64,48},{80,64},{96,80},{112,96},{1... | collective-permute-start | bytes 811016 | tf_op jit(solution)/shard_map/ppermute | solution.py:362
  24.4 28.6 %collective-permute-start.2 = (f32[33,16,128]{2,1,0:T(8,128)}, f32[33,16,128]{2,1,0:T(8,128)S(1)}, u32[]{:S(2)}, u32[]{:S(2)}) collective-permute-start(f32[33,16,128]{2,1,0:T(8,128)} %get-tuple-element.72), channel_id=1, source_target_pairs={{0,1},{1,2},{2,3},{3,4},{4,5},{5,6},{6,7},{7,8},{8,9},{9,10},{10,1... | collective-permute-start | bytes 811016 | tf_op jit(solution)/shard_map/ppermute | solution.py:362
  26.9 26.0 %collective-permute-start.3 = (f32[33,16,128]{2,1,0:T(8,128)}, f32[33,16,128]{2,1,0:T(8,128)S(1)}, u32[]{:S(2)}, u32[]{:S(2)}) collective-permute-start(f32[33,16,128]{2,1,0:T(8,128)} %get-tuple-element.73), channel_id=1, source_target_pairs={{0,15},{1,0},{2,1},{3,2},{4,3},{5,4},{6,5},{7,6},{8,7},{9,8},{10,9... | collective-permute-start | bytes 811016 | tf_op jit(solution)/shard_map/ppermute | solution.py:362
  30.6 4.4 %copy-start.2 = (f32[33,16,128]{2,1,0:T(8,128)}, f32[33,16,128]{2,1,0:T(8,128)S(1)}, u32[]{:S(2)}) copy-start(f32[33,16,128]{2,1,0:T(8,128)S(1)} %collective-permute-done.refs_2_) | copy-start | bytes 811012
  35.0 0.7 copy-start.3
  40.6 21.8 %all-to-all-start = ((f32[128,1,128]{2,1,0:T(1,128)}), f32[128,1,128]{2,1,0:T(1,128)S(1)}, u32[]{:S(2)}, u32[]{:S(2)}) async-start(f32[128,1,128]{2,1,0:T(1,128)} %bitcast.62), calls=%async_computation | async-start | bytes 131072 | tf_op jit(solution)/shard_map/all_to_all | solution.py:378
  53.0 0.7 copy-start
  53.0 0.8 copy-start.1
  62.4 0.6 copy-start.5
  242.4 14.1 %all-to-all-start.11 = ((f32[128,1,128]{2,1,0:T(1,128)}), f32[128,1,128]{2,1,0:T(1,128)S(1)}, u32[]{:S(2)}, u32[]{:S(2)}) async-start(f32[128,1,128]{2,1,0:T(1,128)} %bitcast.63), calls=%async_computation.11 | async-start | bytes 131072 | tf_op jit(solution)/shard_map/all_to_all | solution.py:378
  256.5 0.6 copy-start.4

commit v2 on v1

--- a/solution.py
+++ b/solution.py
@@ -30,6 +30,7 @@
 VMEM = pl.BlockSpec(memory_space=pltpu.VMEM)
 SMEM = pl.BlockSpec(memory_space=pltpu.SMEM)
 f32 = jnp.float32
+GRANT = pltpu.CompilerParams(vmem_limit_bytes=12 * 2**20)
 
 
 def shape(*dims):
@@ -53,20 +54,29 @@
     return table
 
 
-def prep_kernel(shift_ref, v_ref, count_ref, flag_ref, sx_ref, sy_ref, xlo_ref, xhi_ref, ylo_ref, yhi_ref, uz_ref, base_ref, turn_ref):
+def fold(values):
+    return jnp.sum(values, axis=0, keepdims=True)
+
+
+def prep_kernel(
+    shift_ref, v_ref, count_ref, flag_hbm, own_ref, uy_ref, uz_ref, low_ref, high_ref, base_ref, flag_ref, flag_sem
+):
+    fetch = pltpu.make_async_copy(flag_hbm.at[0], flag_ref, flag_sem)
+    fetch.start()
     shift = later_shifts(shift_ref, 0)
     zero_row = jnp.zeros((EXT, 1, NZ), f32)
-    for field in range(FIELDS):
-        sx_ref[field, :, EXT:PAD, :] = zero_row
-        turn_ref[field, EXT * PAD : PAD * PAD, :] = jnp.zeros((PAD, NZ), f32)
-    uz_ref[:, EXT:PAD, :] = zero_row
-
-    def plane(i, sums):
-        thermal, energy_y, total = sums
+    for field in range(3):
+        own_ref[field, :, EXT:PAD, :] = zero_row
+    for array_ref in (uy_ref, uz_ref):
+        array_ref[0:EXT, EXT:PAD, :] = zero_row
+    uy_ref[EXT] = jnp.zeros((PAD, NZ), f32)
+
+    thermal = energy_y = total = jnp.zeros((EXT, NZ), f32)
+    fetch.wait()
+    for i in range(EXT):
         counts = count_ref[i]
         mass = counts.astype(f32)
-        safe = jnp.maximum(mass, 1.0)
-        inverse = 1.0 / safe
+        inverse = 1.0 / jnp.maximum(mass, 1.0)
         mean = []
         for member in range(3):
             values = [
@@ -83,42 +93,57 @@
         thermal = thermal + mass * mean[2] * mean[2]
         energy_y = energy_y + mass * mean[1] * mean[1]
         total = total + mass
-        rolled = pltpu.roll(mass, shift, 1)
-        sx_ref[0, i, 0:EXT, :] = pltpu.roll(mean[0], shift, 1)
-        sx_ref[1, i, 0:EXT, :] = rolled
+        own_ref[0, i, 0:EXT, :] = pltpu.roll(mean[0], shift, 1)
+        own_ref[1, i, 0:EXT, :] = pltpu.roll(mass, shift, 1)
+        own_ref[2, i, 0:EXT, :] = pltpu.roll(flag_ref[i].astype(f32), shift, 1)
+        uy_ref[i, 0:EXT, :] = pltpu.roll(mean[1], shift, 1)
         uz_ref[i, 0:EXT, :] = pltpu.roll(mean[2], shift, 1)
-        row = pl.multiple_of(i * PAD, PAD)
-        turn_ref[0, pl.ds(row, EXT), :] = pltpu.roll(mean[1], shift, 1)
-        turn_ref[1, pl.ds(row, EXT), :] = rolled
-        return thermal, energy_y, total
-
-    nothing = jnp.zeros((EXT, NZ), f32)
-    thermal, energy_y, total = lax.fori_loop(0, EXT, plane, (nothing, nothing, nothing))
     base_ref[...] = jnp.zeros((8, NZ), f32)
     base_ref[0:1, :] = jnp.full((1, NZ), 1.0 / BIG, f32)
-    base_ref[2:3, :] = jnp.sum(thermal, axis=0, keepdims=True)
-    base_ref[4:5, :] = jnp.sum(energy_y, axis=0, keepdims=True)
-    base_ref[5:6, :] = jnp.sum(total, axis=0, keepdims=True)
-
+    base_ref[2:3, :] = fold(thermal)
+    base_ref[4:5, :] = fold(energy_y)
+    base_ref[5:6, :] = fold(total)
+    for field in range(3):
+        low_ref[field] = own_ref[field, 0]
+        high_ref[field] = own_ref[field, EXT - 1]
+
+
+def prep(shifts, v, counts, flags):
+    edge = shape(3, PAD, NZ)
+    return pl.pallas_call(
+        prep_kernel,
+        in_specs=[SMEM, VMEM, VMEM, pl.BlockSpec(memory_space=pl.ANY)],
+        out_specs=[VMEM] * 6,
+        out_shape=[shape(3, EXT, PAD, NZ), shape(PAD, PAD, NZ), shape(EXT, PAD, NZ), edge, edge, shape(8, NZ)],
+        scratch_shapes=[pltpu.VMEM((EXT, EXT, NZ), jnp.int32), pltpu.SemaphoreType.DMA],
+        compiler_params=GRANT,
+        name="prep",
+    )(shifts, v, counts, flags)
+
+
+def spread_kernel(shift_ref, own_ref, uy_ref, flag_ref, sx_ref, sy_ref, xlo_ref, xhi_ref, ylo_ref, yhi_ref, turn_ref):
+    for field in range(HALF):
+        sx_ref[2 + field, :, EXT:PAD, :] = jnp.zeros((EXT, 1, NZ), f32)
+    for i in range(EXT):
+        sx_ref[0, i] = own_ref[0, i]
+        sx_ref[1, i] = own_ref[1, i]
     for step in range(STEPS):
         later = later_shifts(shift_ref, step)
-        field = 2 + step // 2
-
-        def flags(i, carry, step=step, later=later, field=field):
+        for i in range(EXT):
             bits = pltpu.roll(flag_ref[step, i].astype(f32), later, 1)
             if step % 2 == 0:
-                sx_ref[field, i, 0:EXT, :] = bits
+                sx_ref[2 + step // 2, i, 0:EXT, :] = bits
             else:
-                row = pl.multiple_of(i * PAD, PAD)
-                turn_ref[field, pl.ds(row, EXT), :] = bits
-            return carry
-
-        lax.fori_loop(0, EXT, flags, 0)
-
+                turn_ref[step // 2, i * PAD : i * PAD + EXT, :] = bits
     keep = lax.broadcasted_iota(jnp.int32, (PAD, NZ), 0) < EXT
+    for i in range(EXT):
+        turn_ref[HALF, i * PAD : (i + 1) * PAD, :] = own_ref[1, i]
     for field in range(FIELDS):
         for y in range(EXT):
-            rows = turn_ref[field, pl.ds(y, PAD, stride=PAD), :]
+            if field == 0:
+                rows = uy_ref[pl.ds(y, PAD, stride=PAD), :]
+            else:
+                rows = turn_ref[HALF if field == 1 else field - 2, pl.ds(y, PAD, stride=PAD), :]
             sy_ref[field, y] = jnp.where(keep, rows, 0.0)
 
     for field, place, planes in edge_offsets():
@@ -129,25 +154,85 @@
             yhi_ref[place + k] = sy_ref[field, EXT - planes + k]
 
 
-def prep(shifts, v, counts, flags):
+def spread(shifts, own, uy, flags):
     edge = shape(EDGE_PLANES, PAD, NZ)
-    own = shape(FIELDS, EXT, PAD, NZ)
-    return pl.pallas_call(
-        prep_kernel,
+    full = shape(FIELDS, EXT, PAD, NZ)
+    return pl.pallas_call(
+        spread_kernel,
         in_specs=[SMEM, VMEM, VMEM, VMEM],
-        out_specs=[VMEM] * 8,
-        out_shape=[own, own, edge, edge, edge, edge, shape(EXT, PAD, NZ), shape(8, NZ)],
-        scratch_shapes=[pltpu.VMEM((FIELDS, PAD * PAD, NZ), f32)],
-        name="prep",
-    )(shifts, v, counts, flags)
+        out_specs=[VMEM] * 6,
+        out_shape=[full, full, edge, edge, edge, edge],
+        scratch_shapes=[pltpu.VMEM((HALF + 1, PAD * PAD, NZ), f32)],
+        compiler_params=GRANT,
+        name="spread",
+    )(shifts, own, uy.reshape(PAD * PAD, NZ), flags)
+
+
+def first_kernel(parity_ref, own_ref, below_ref, above_ref, carry_ref, rows_ref, out_ref, u_ref, mass_ref, bits_ref):
+    for field, array_ref in enumerate((u_ref, mass_ref, bits_ref)):
+        array_ref[0] = below_ref[field]
+        array_ref[EXT + 1] = above_ref[field]
+        for k in range(EXT):
+            array_ref[1 + k] = own_ref[field, k]
+    start = lax.rem(lower_start(parity_ref, 0, "bx") + 1, jnp.int32(2))
+    wide = jnp.broadcast_to(carry_ref[0:1, :], (PAD, NZ))
+    for k in range((EXT + 1) // 2):
+        plane = start + 2 * k
+        low, high = u_ref[plane], u_ref[plane + 1]
+        weight_low, weight_high = pair_weights(mass_ref[plane], mass_ref[plane + 1])
+        allowed = jnp.maximum(bits_ref[plane], bits_ref[plane + 1])
+        closing = jnp.maximum(low - high, 0.0)
+        push = allowed * closing * jnp.tanh(wide * closing)
+        u_ref[plane] = low - weight_low * push
+        u_ref[plane + 1] = high + weight_high * push
+    energy = jnp.zeros((PAD, NZ), f32)
+    for k in range(EXT):
+        u = u_ref[1 + k]
+        energy = energy + own_ref[1, k] * u * u
+    mine = fold(energy)
+    half = NZ // 2
+    lane = lax.broadcasted_iota(jnp.int32, (1, NZ), 1)
+    local = carry_ref[2:3, :] + mine + carry_ref[4:5, :]
+    number = carry_ref[5:6, :]
+    local = jnp.where(lane < half, local + pltpu.roll(local, half, 1), number + pltpu.roll(number, half, 1))
+    out_ref[...] = carry_ref[...]
+    out_ref[3:4, :] = mine
+    rows_ref[...] = jnp.broadcast_to(local, (DEVICES, NZ))
+
+
+def first(parity, own, below, above, carry):
+    return pl.pallas_call(
+        first_kernel,
+        in_specs=[SMEM] + [VMEM] * 4,
+        out_specs=[VMEM] * 2,
+        out_shape=[shape(DEVICES, NZ), shape(8, NZ)],
+        scratch_shapes=[pltpu.VMEM((EXT + 2, PAD, NZ), f32)] * 3,
+        compiler_params=GRANT,
+        name="first",
+    )(parity, own, below, above, carry)
 
 
 def lower_start(parity_ref, step, brick_axis):
     return lax.rem(parity_ref[step] + lax.axis_index(brick_axis) * EXT, jnp.int32(2))
 
 
+def pair_weights(mass_low, mass_high):
+    reduced = mass_low * mass_high / jnp.maximum(mass_low + mass_high, 1.0)
+    return reduced / jnp.maximum(mass_low, 1.0), reduced / jnp.maximum(mass_high, 1.0)
+
+
+def pairs_step(u_ref, weight_ref, start, wide):
+    for k in range(PAIRS):
+        plane = start + 2 * k
+        low, high = u_ref[plane], u_ref[plane + 1]
+        closing = jnp.maximum(low - high, 0.0)
+        push = closing * jnp.tanh(wide * closing)
+        u_ref[plane] = low - weight_ref[0, k] * push
+        u_ref[plane + 1] = high + weight_ref[1, k] * push
+
+
 def join_kernel(parity_ref, own_ref, below_ref, above_ref, u_ref, *rest, first_step, brick_axis):
-    weight_refs, (mass_ref, bits_ref) = rest[:HALF], rest[HALF:]
+    weight_refs, (own_mass_ref, mass_ref, bits_ref, both_ref) = rest[:HALF], rest[HALF:]
     for field, place, planes in edge_offsets():
         for k in range(planes):
             low, high = below_ref[place + k], above_ref[place + k]
@@ -166,17 +251,21 @@
     for k in range(EXT):
         u_ref[HALO + k] = own_ref[0, k]
         mass_ref[HALO + k] = own_ref[1, k]
+        own_mass_ref[k] = own_ref[1, k]
         for j in range(HALF):
             bits_ref[j, HALO + k] = own_ref[2 + j, k]
+    for plane in range(FULL - 1):
+        both_ref[0, plane], both_ref[1, plane] = pair_weights(mass_ref[plane], mass_ref[plane + 1])
     for j in range(HALF):
         start = lower_start(parity_ref, first_step + 2 * j, brick_axis)
         for k in range(PAIRS):
             plane = start + 2 * k
-            mass_low, mass_high = mass_ref[plane], mass_ref[plane + 1]
             allowed = jnp.maximum(bits_ref[j, plane], bits_ref[j, plane + 1])
-            reduced = allowed * mass_low * mass_high / jnp.maximum(mass_low + mass_high, 1.0)
-            weight_refs[j][0, k] = reduced / jnp.maximum(mass_low, 1.0)
-            weight_refs[j][1, k] = reduced / jnp.maximum(mass_high, 1.0)
+            weight_refs[j][0, k] = allowed * both_ref[0, plane]
+            weight_refs[j][1, k] = allowed * both_ref[1, plane]
+    if first_step == 0:
+        start = lower_start(parity_ref, 0, brick_axis)
+        pairs_step(u_ref, weight_refs[0], start, jnp.full((PAD, NZ), 1.0 / BIG, f32))
 
 
 def join(parity, own, below, above, first_step, brick_axis):
@@ -186,9 +275,14 @@
     return pl.pallas_call(
         body,
         in_specs=[SMEM, VMEM, VMEM, VMEM],
-        out_specs=[VMEM] * (1 + HALF),
-        out_shape=[shape(FULL, PAD, NZ)] + [shape(2, PAIRS, PAD, NZ)] * HALF,
-        scratch_shapes=[pltpu.VMEM((FULL, PAD, NZ), f32), pltpu.VMEM((HALF, FULL, PAD, NZ), f32)],
+        out_specs=[VMEM] * (2 + HALF),
+        out_shape=[shape(FULL, PAD, NZ)] + [shape(2, PAIRS, PAD, NZ)] * HALF + [shape(EXT, PAD, NZ)],
+        scratch_shapes=[
+            pltpu.VMEM((FULL, PAD, NZ), f32),
+            pltpu.VMEM((HALF, FULL, PAD, NZ), f32),
+            pltpu.VMEM((2, FULL, PAD, NZ), f32),
+        ],
+        compiler_params=GRANT,
         name="join",
     )(parity, own, below, above)
 
@@ -209,61 +303,42 @@
     return jnp.minimum(scale * factor, SCALE_CAP), total
 
 
-def step_kernel(*refs, step, brick_axis):
-    if step == 0:
-        parity_ref, carry_ref, u_in_ref, weight_ref, own_ref, u_ref, rows_ref, out_ref = refs
-        scale, total = carry_ref[0:1, :], jnp.zeros((1, NZ), f32)
-    else:
-        parity_ref, heat_ref, received_ref, carry_ref, u_in_ref, weight_ref, own_ref, u_ref, rows_ref, out_ref = refs
-        scale, total = next_scale(received_ref, carry_ref, heat_ref, step - 1)
-    wide = jnp.broadcast_to(scale, (PAD, NZ))
+def step_kernel(
+    parity_ref, heat_ref, received_ref, carry_ref, u_in_ref, weight_ref, mass_ref, u_ref, rows_ref, out_ref, *, step, brick_axis
+):
+    scale, total = next_scale(received_ref, carry_ref, heat_ref, step - 1)
     start = lower_start(parity_ref, step, brick_axis)
-    u_ref[0] = u_in_ref[0]
-    u_ref[FULL - 1] = u_in_ref[FULL - 1]
-    for k in range(PAIRS):
-        plane = start + 2 * k
-        low, high = u_in_ref[plane], u_in_ref[plane + 1]
-        closing = jnp.maximum(low - high, 0.0)
-        push = closing * jnp.tanh(wide * closing)
-        u_ref[plane] = low - weight_ref[0, k] * push
-        u_ref[plane + 1] = high + weight_ref[1, k] * push
+    for k in range(FULL):
+        u_ref[k] = u_in_ref[k]
+    pairs_step(u_ref, weight_ref, start, jnp.broadcast_to(scale, (PAD, NZ)))
     energy = jnp.zeros((PAD, NZ), f32)
     for k in range(EXT):
         u = u_ref[HALO + k]
-        energy = energy + own_ref[1, k] * u * u
-    mine = jnp.sum(energy, axis=0, keepdims=True)
+        energy = energy + mass_ref[k] * u * u
+    mine = fold(energy)
     other = carry_ref[4:5, :] if step % 2 == 0 else carry_ref[3:4, :]
-    local = carry_ref[2:3, :] + mine + other
-    if step == 0:
-        half = NZ // 2
-        lane = lax.broadcasted_iota(jnp.int32, (1, NZ), 1)
-        number = carry_ref[5:6, :]
-        local = local + pltpu.roll(local, half, 1)
-        number = number + pltpu.roll(number, half, 1)
-        local = jnp.where(lane < half, local, number)
     out_ref[...] = carry_ref[...]
     out_ref[0:1, :] = scale
     out_ref[1:2, :] = total
     row = 3 if step % 2 == 0 else 4
     out_ref[row : row + 1, :] = mine
-    rows_ref[...] = jnp.broadcast_to(local, (DEVICES, NZ))
-
-
-def collide(step, parity, heat, received, carry, u, weight, own):
+    rows_ref[...] = jnp.broadcast_to(carry_ref[2:3, :] + mine + other, (DEVICES, NZ))
+
+
+def collide(step, parity, heat, received, carry, u, weight, mass):
     brick_axis = "bx" if step % 2 == 0 else "by"
 
     def body(*refs):
         step_kernel(*refs, step=step, brick_axis=brick_axis)
 
-    scalars = (parity,) if step == 0 else (parity, heat)
-    arrays = (carry, u, weight, own) if step == 0 else (received, carry, u, weight, own)
     return pl.pallas_call(
         body,
-        in_specs=[SMEM] * len(scalars) + [VMEM] * len(arrays),
+        in_specs=[SMEM] * 2 + [VMEM] * 5,
         out_specs=[VMEM] * 3,
         out_shape=[shape(FULL, PAD, NZ), shape(DEVICES, NZ), shape(8, NZ)],
+        compiler_params=GRANT,
         name="collide",
-    )(*scalars, *arrays)
+    )(parity, heat, received, carry, u, weight, mass)
 
 
 def turn_kernel(shift_ref, v_ref, count_ref, spin_ref, w_ref):
@@ -325,32 +400,46 @@
         in_specs=[SMEM, VMEM, VMEM, VMEM],
         out_specs=VMEM,
         out_shape=shape(3, SLOTS, EXT, EXT, NZ),
+        compiler_params=GRANT,
         name="turn",
     )(shifts, v, counts, spin)
 
 
 def finish_kernel(heat_ref, received_ref, carry_ref, ux_ref, uy_ref, uz_ref, own_ref, w_ref, v_ref):
+    member = pl.program_id(0)
     scale, _ = next_scale(received_ref, carry_ref, heat_ref, STEPS - 1)
     wide = jnp.broadcast_to(scale, (EXT, NZ))
-    for i in range(EXT):
-        counts = own_ref[1, i, 0:EXT, :]
-        mean = [
-            ux_ref[HALO + i, 0:EXT, :],
-            uy_ref[pl.ds(HALO * PAD + i, EXT, stride=PAD), :],
-            uz_ref[i, 0:EXT, :],
-        ]
-        for member in range(3):
+
+    def write(mean_of):
+        for i in range(EXT):
+            counts = own_ref[0, i, 0:EXT, :]
+            mean = mean_of(i)
             for slot in range(SLOTS):
-                value = wide * (mean[member] + w_ref[member, slot, i])
-                v_ref[member, slot, i] = jnp.where(counts > slot, value, 0.0)
+                v_ref[0, slot, i] = jnp.where(counts > slot, wide * (mean + w_ref[0, slot, i]), 0.0)
+
+    @pl.when(member == 0)
+    def _():
+        write(lambda i: ux_ref[HALO + i, 0:EXT, :])
+
+    @pl.when(member == 1)
+    def _():
+        write(lambda i: uy_ref[pl.ds(HALO * PAD + i, EXT, stride=PAD), :])
+
+    @pl.when(member == 2)
+    def _():
+        write(lambda i: uz_ref[i, 0:EXT, :])
 
 
 def finish(heat, received, carry, ux, uy, uz, own, w):
+    part = pl.BlockSpec((1, SLOTS, EXT, EXT, NZ), lambda c: (c, 0, 0, 0, 0))
+    mass = pl.BlockSpec((1, EXT, PAD, NZ), lambda c: (1, 0, 0, 0))
     return pl.pallas_call(
         finish_kernel,
-        in_specs=[SMEM] + [VMEM] * 7,
-        out_specs=VMEM,
+        grid=(3,),
+        in_specs=[SMEM] + [VMEM] * 5 + [mass, part],
+        out_specs=part,
         out_shape=shape(3, SLOTS, EXT, EXT, NZ),
+        compiler_params=GRANT,
         name="finish",
     )(heat, received, carry, ux, uy.reshape(FULL * PAD, NZ), uz, own, w)
 
@@ -363,20 +452,23 @@
 
 
 def per_device(v, counts, spin, flags, parity, shifts, heat):
-    sx, sy, xlo, xhi, ylo, yhi, uz, carry = prep(shifts, v, counts, flags)
+    own, uy, uz, low, high, carry = prep(shifts, v, counts, flags)
+    above, below = exchange(low, high, "bx")
+    sx, sy, xlo, xhi, ylo, yhi = spread(shifts, own, uy, flags)
+    y_above, y_below = exchange(ylo, yhi, "by")
     x_above, x_below = exchange(xlo, xhi, "bx")
-    y_above, y_below = exchange(ylo, yhi, "by")
+    rows, carry = first(parity, own, below, above, carry)
+    received = lax.all_to_all(rows, ("bx", "by"), 0, 0, tiled=True)
     w = turn(shifts, v, counts, spin)
-    ux, *x_weights = join(parity, sx, x_below, x_above, 0, "bx")
-    uy, *y_weights = join(parity, sy, y_below, y_above, 1, "by")
-    received = None
-    for step in range(STEPS):
+    uy, *y_weights, y_mass = join(parity, sy, y_below, y_above, 1, "by")
+    ux, *x_weights, x_mass = join(parity, sx, x_below, x_above, 0, "bx")
+    for step in range(1, STEPS):
         if step % 2 == 0:
-            ux, rows, carry = collide(step, parity, heat, received, carry, ux, x_weights[step // 2], sx)
+            ux, rows, carry = collide(step, parity, heat, received, carry, ux, x_weights[step // 2], x_mass)
         else:
-            uy, rows, carry = collide(step, parity, heat, received, carry, uy, y_weights[step // 2], sy)
+            uy, rows, carry = collide(step, parity, heat, received, carry, uy, y_weights[step // 2], y_mass)
         received = lax.all_to_all(rows, ("bx", "by"), 0, 0, tiled=True)
-    return finish(heat, received, carry, ux, uy, uz, sx, w)
+    return finish(heat, received, carry, ux, uy, uz, own, w)
 
 
 def solution(mesh):

time: 262 us -> 228 us (0.87)
  Pallas kernels: 62.4 us -> 23.4 us
  blocking collectives: 153 us -> 125 us
  local copies, waits for them, and re-layouts: 2.76 us -> 19.5 us
  starting transfers between devices: 25.6 us -> 36.5 us
  waiting for transfers between devices: 17.1 us -> 22.7 us
    pallas_call x14 -> x15, Pallas kernels: 50.7 us -> 17.1 us  [the longest x11 9.69 us: collide(): pl.pallas_call(body, in_specs=[SMEM] * 2 + [VMEM] * 5, out_specs=[VMEM] *...]
    all_to_all x10 -> x9, blocking collectives: 153 us -> 125 us  [per_device(): received = lax.all_to_all(rows, ('bx', 'by'), 0, 0, tiled=True)]
    unnamed x12 -> x70, local copies, waits for them, and re-layouts: 2.76 us -> 19.5 us
    ppermute x2 -> x3, waiting for transfers between devices: 3.69 us -> 10.3 us  [exchange(): lax.ppermute(high_edge, axis, up)]
    all_to_all x2 -> x3, starting transfers between devices: 16.9 us -> 22.3 us  [per_device(): received = lax.all_to_all(rows, ('bx', 'by'), 0, 0, tiled=True)]
    ppermute x2 -> x3, starting transfers between devices: 2.53 us -> 7.87 us  [exchange(): lax.ppermute(low_edge, axis, down)]
    ppermute x2 -> x3, waiting for transfers between devices: 4.35 us -> 0.95 us  [exchange(): lax.ppermute(low_edge, axis, down)]
    pallas_call x1, Pallas kernels: 6.54 us -> 3.57 us  [turn(): pl.pallas_call(turn_kernel, in_specs=[SMEM, VMEM, VMEM, VMEM], out_specs=...]
  transfers between devices with their start and end apart: 6 -> 9, of which waited for: 4 -> 5; matrix products, arithmetic and copies ran while one was open for 0% -> 0% of each run, Pallas kernels for 5% -> 4%
where the time goes in v2:
time: 228 us; the launch traced here: 227 us
  blocking collectives  125 us (55%)
  starting transfers between devices  36.5 us (16%)
  Pallas kernels  23.4 us (10%)
  waiting for transfers between devices  22.7 us (10%)
  local copies, waits for them, and re-layouts  19.5 us (9%)
    all_to_all x9, blocking collectives, per_device(): received = lax.all_to_all(rows, ('bx', 'by'), 0, 0, tiled=True)  125 us
    all_to_all x3, starting transfers between devices, per_device(): received = lax.all_to_all(rows, ('bx', 'by'), 0, 0, tiled=True)  22.3 us
    unnamed x70, local copies, waits for them, and re-layouts  19.5 us
    all_to_all x3, waiting for transfers between devices, per_device(): received = lax.all_to_all(rows, ('bx', 'by'), 0, 0, tiled=True)  11.4 us
    ppermute x3, waiting for transfers between devices, exchange(): lax.ppermute(high_edge, axis, up)  10.3 us
    pallas_call x11, Pallas kernels, collide(): pl.pallas_call(body, in_specs=[SMEM] * 2 + [VMEM] * 5, out_specs=[VMEM] *...  9.69 us
    ppermute x3, starting transfers between devices, exchange(): lax.ppermute(low_edge, axis, down)  7.87 us
    ppermute x3, starting transfers between devices, exchange(): lax.ppermute(high_edge, axis, up)  6.28 us
  transfers between devices with their start and end apart: 9, of which 5 were waited for; matrix products, arithmetic and copies ran while one was open for 0% of the time, Pallas kernels for 4%

profile of v2, /device:TPU:1, one launch (start us, length us, event | category | flops | bytes accessed | tf_op | source)
XLA Modules:
  0.0 226.9 jit_solution(15057131774085343517)
XLA Ops:
  0.0 1.6 copy-done
  1.6 1.4 copy-done.2
  4.6 1.3 prep.1
  6.5 2.1 spread.1
  8.5 3.0 %collective-permute-start.2 = (f32[33,16,128]{2,1,0:T(8,128)}, f32[33,16,128]{2,1,0:T(8,128)S(1)}, u32[]{:S(2)}, u32[]{:S(2)}) collective-permute-start(f32[33,16,128]{2,1,0:T(8,128)} %get-tuple-element.75), channel_id=1, source_target_pairs={{0,1},{1,2},{2,3},{3,4},{4,5},{5,6},{6,7},{7,8},{8,9},{9,10},{10,1... | collective-permute-start | bytes 811016 | tf_op jit(solution)/shard_map/ppermute | solution.py:451
  11.6 2.7 %collective-permute-start.4 = (f32[33,16,128]{2,1,0:T(8,128)}, f32[33,16,128]{2,1,0:T(8,128)S(1)}, u32[]{:S(2)}, u32[]{:S(2)}) collective-permute-start(f32[33,16,128]{2,1,0:T(8,128)} %get-tuple-element.83), channel_id=1, source_target_pairs={{0,16},{16,32},{32,48},{48,64},{64,80},{80,96},{96,112},{112,0},{1... | collective-permute-start | bytes 811016 | tf_op jit(solution)/shard_map/ppermute | solution.py:451
  14.3 2.5 %collective-permute-start.5 = (f32[33,16,128]{2,1,0:T(8,128)}, f32[33,16,128]{2,1,0:T(8,128)S(1)}, u32[]{:S(2)}, u32[]{:S(2)}) collective-permute-start(f32[33,16,128]{2,1,0:T(8,128)} %get-tuple-element.84), channel_id=1, source_target_pairs={{0,112},{16,0},{32,16},{48,32},{64,48},{80,64},{96,80},{112,96},{1... | collective-permute-start | bytes 811016 | tf_op jit(solution)/shard_map/ppermute | solution.py:451
  17.3 10.3 %collective-permute-done.below_ref = f32[3,16,128]{2,1,0:T(8,128)S(1)} collective-permute-done((f32[3,16,128]{2,1,0:T(8,128)S(1)}, f32[3,16,128]{2,1,0:T(8,128)S(1)}, u32[]{:S(2)}, u32[]{:S(2)}) %collective-permute-start) | collective-permute-done | bytes 24608 | tf_op jit(solution)/shard_map/ppermute | solution.py:451
  27.6 5.4 %collective-permute-start.1 = (f32[3,16,128]{2,1,0:T(8,128)S(1)}, f32[3,16,128]{2,1,0:T(8,128)S(1)}, u32[]{:S(2)}, u32[]{:S(2)}) collective-permute-start(f32[3,16,128]{2,1,0:T(8,128)S(1)} %get-tuple-element.69), channel_id=1, source_target_pairs={{0,112},{16,0},{32,16},{48,32},{64,48},{80,64},{96,80},{112,96},{1... | collective-permute-start | bytes 73736 | tf_op jit(solution)/shard_map/ppermute | solution.py:451
  33.9 1.4 first.1
  35.3 11.4 %all-to-all-start = ((f32[128,1,128]{2,1,0:T(1,128)}), f32[128,1,128]{2,1,0:T(1,128)S(1)}, u32[]{:S(2)}, u32[]{:S(2)}) async-start(f32[128,1,128]{2,1,0:T(1,128)} %bitcast.1), calls=%async_computation | async-start | bytes 131072 | tf_op jit(solution)/shard_map/all_to_all | solution.py:461
  52.7 3.4 %all-to-all-done = f32[128,1,128]{2,1,0:T(1,128)S(1)} async-done(((f32[128,1,128]{2,1,0:T(1,128)}), f32[128,1,128]{2,1,0:T(1,128)S(1)}, u32[]{:S(2)}, u32[]{:S(2)}) %all-to-all-start) | async-done | bytes 65568 | tf_op jit(solution)/shard_map/all_to_all | solution.py:461
  58.0 1.4 collide.11
  59.4 6.4 %all-to-all-start.1 = ((f32[128,1,128]{2,1,0:T(1,128)}), f32[128,1,128]{2,1,0:T(1,128)S(1)}, u32[]{:S(2)}, u32[]{:S(2)}) async-start(f32[128,1,128]{2,1,0:T(1,128)} %bitcast.5), calls=%async_computation.1 | async-start | bytes 131072 | tf_op jit(solution)/shard_map/all_to_all | solution.py:470
  65.8 1.5 join.3
  70.0 5.2 %all-to-all-done.1 = f32[128,1,128]{2,1,0:T(1,128)S(1)} async-done(((f32[128,1,128]{2,1,0:T(1,128)}), f32[128,1,128]{2,1,0:T(1,128)S(1)}, u32[]{:S(2)}, u32[]{:S(2)}) %all-to-all-start.1) | async-done | bytes 65568 | tf_op jit(solution)/shard_map/all_to_all | solution.py:470
  76.9 13.8 %all_to_all.132 = f32[128,1,128]{2,1,0:T(1,128)S(1)} all-to-all(f32[128,1,128]{2,1,0:T(1,128)S(1)} %bitcast.65), channel_id=1, replica_groups=mesh['bx'=8,'by'=16] {'bx','by'}, dimensions={0} | all-to-all | bytes 131072 | tf_op jit(solution)/shard_map/all_to_all | solution.py:470
  91.6 13.8 %all_to_all.133 = f32[128,1,128]{2,1,0:T(1,128)S(1)} all-to-all(f32[128,1,128]{2,1,0:T(1,128)S(1)} %bitcast.66), channel_id=1, replica_groups=mesh['bx'=8,'by'=16] {'bx','by'}, dimensions={0} | all-to-all | bytes 131072 | tf_op jit(solution)/shard_map/all_to_all | solution.py:470
  107.1 13.8 %all_to_all.134 = f32[128,1,128]{2,1,0:T(1,128)S(1)} all-to-all(f32[128,1,128]{2,1,0:T(1,128)S(1)} %bitcast.67), channel_id=1, replica_groups=mesh['bx'=8,'by'=16] {'bx','by'}, dimensions={0} | all-to-all | bytes 131072 | tf_op jit(solution)/shard_map/all_to_all | solution.py:470
  121.7 13.8 %all_to_all.135 = f32[128,1,128]{2,1,0:T(1,128)S(1)} all-to-all(f32[128,1,128]{2,1,0:T(1,128)S(1)} %bitcast.68), channel_id=1, replica_groups=mesh['bx'=8,'by'=16] {'bx','by'}, dimensions={0} | all-to-all | bytes 131072 | tf_op jit(solution)/shard_map/all_to_all | solution.py:470
  136.4 13.8 %all_to_all.136 = f32[128,1,128]{2,1,0:T(1,128)S(1)} all-to-all(f32[128,1,128]{2,1,0:T(1,128)S(1)} %bitcast.69), channel_id=1, replica_groups=mesh['bx'=8,'by'=16] {'bx','by'}, dimensions={0} | all-to-all | bytes 131072 | tf_op jit(solution)/shard_map/all_to_all | solution.py:470
  151.0 13.8 %all_to_all.137 = f32[128,1,128]{2,1,0:T(1,128)S(1)} all-to-all(f32[128,1,128]{2,1,0:T(1,128)S(1)} %bitcast.70), channel_id=1, replica_groups=mesh['bx'=8,'by'=16] {'bx','by'}, dimensions={0} | all-to-all | bytes 131072 | tf_op jit(solution)/shard_map/all_to_all | solution.py:470
  165.6 13.9 %all_to_all.138 = f32[128,1,128]{2,1,0:T(1,128)S(1)} all-to-all(f32[128,1,128]{2,1,0:T(1,128)S(1)} %bitcast.71), channel_id=1, replica_groups=mesh['bx'=8,'by'=16] {'bx','by'}, dimensions={0} | all-to-all | bytes 131072 | tf_op jit(solution)/shard_map/all_to_all | solution.py:470
  180.3 13.8 %all_to_all.139 = f32[128,1,128]{2,1,0:T(1,128)S(1)} all-to-all(f32[128,1,128]{2,1,0:T(1,128)S(1)} %bitcast.72), channel_id=1, replica_groups=mesh['bx'=8,'by'=16] {'bx','by'}, dimensions={0} | all-to-all | bytes 131072 | tf_op jit(solution)/shard_map/all_to_all | solution.py:470
  194.9 13.8 %all_to_all.140 = f32[128,1,128]{2,1,0:T(1,128)S(1)} all-to-all(f32[128,1,128]{2,1,0:T(1,128)S(1)} %bitcast.64), channel_id=1, replica_groups=mesh['bx'=8,'by'=16] {'bx','by'}, dimensions={0} | all-to-all | bytes 131072 | tf_op jit(solution)/shard_map/all_to_all | solution.py:470
  208.7 1.4 collide.21
  210.1 4.6 %all-to-all-start.11 = ((f32[128,1,128]{2,1,0:T(1,128)}), f32[128,1,128]{2,1,0:T(1,128)S(1)}, u32[]{:S(2)}, u32[]{:S(2)}) async-start(f32[128,1,128]{2,1,0:T(1,128)} %bitcast.35), calls=%async_computation.11 | async-start | bytes 131072 | tf_op jit(solution)/shard_map/all_to_all | solution.py:470
  214.8 1.6 copy-done.1
  216.4 1.4 copy-done.4
  217.8 3.6 %turn.1.w_ref = f32[3,6,15,15,128]{4,3,2,1,0:T(8,128)S(1)} custom-call(s32[12]{0:T(128)S(1)} %copy-done.34, f32[3,6,15,15,128]{4,3,2,1,0:T(8,128)S(1)} %copy-done.1, s32[15,15,128]{2,1,0:T(8,128)S(1)} %copy-done.6, s32[12,15,15,128]{3,2,1,0:T(8,128)S(1)} %copy-done.4), custom_call_target="tpu_custom_call" | custom-call | tf_op jit(solution)/shard_map/turn/pallas_call | solution.py:398
  221.4 2.8 %all-to-all-done.11 = f32[128,1,128]{2,1,0:T(1,128)S(1)} async-done(((f32[128,1,128]{2,1,0:T(1,128)}), f32[128,1,128]{2,1,0:T(1,128)S(1)}, u32[]{:S(2)}, u32[]{:S(2)}) %all-to-all-start.11) | async-done | bytes 65568 | tf_op jit(solution)/shard_map/all_to_all | solution.py:470
  224.2 2.7 %finish.1 = f32[3,6,15,15,128]{4,3,2,1,0:T(8,128)} custom-call(f32[12]{0:T(128)S(1)} %copy-done.32, f32[128,128]{1,0:T(8,128)S(1)} %bitcast.50, f32[8,128]{1,0:T(8,128)S(1)} %get-tuple-element.125.carry_ref, f32[27,16,128]{2,1,0:T(8,128)S(1)} %get-tuple-element.126.ux_ref, f32[432,128]{1,0:T(8,128)S(1)} %bitcast.62, f32[15,16,128]{2,1,0:T(8,128)S(1)} %copy-done.30, ...), custom_call_target="tpu_custom_call" | custom-call | tf_op jit(solution)/shard_map/finish/pallas_call | solution.py:436
  (83 shorter events, 23.1 us)
Async XLA Ops:
  0.0 1.6 copy-start
  1.6 1.4 copy-start.2
  3.0 0.9 copy-start.5
  4.6 1.9 copy-start.3
  4.6 29.4 %copy-start.31 = (s32[12]{0:T(128)S(1)}, s32[12]{0:T(128)}, u32[]{:S(2)}) copy-start(s32[12]{0:T(128)} %refs_0_.25) | copy-start | bytes 148
  6.5 49.6 %copy-start.32 = (f32[12]{0:T(128)S(1)}, f32[12]{0:T(128)}, u32[]{:S(2)}) copy-start(f32[12]{0:T(128)} %heat_ref.1) | copy-start | bytes 148
  8.5 38.1 %collective-permute-start.2 = (f32[33,16,128]{2,1,0:T(8,128)}, f32[33,16,128]{2,1,0:T(8,128)S(1)}, u32[]{:S(2)}, u32[]{:S(2)}) collective-permute-start(f32[33,16,128]{2,1,0:T(8,128)} %get-tuple-element.75), channel_id=1, source_target_pairs={{0,1},{1,2},{2,3},{3,4},{4,5},{5,6},{6,7},{7,8},{8,9},{9,10},{10,1... | collective-permute-start | bytes 811016 | tf_op jit(solution)/shard_map/ppermute | solution.py:451
  11.6 35.1 %collective-permute-start.3 = (f32[33,16,128]{2,1,0:T(8,128)}, f32[33,16,128]{2,1,0:T(8,128)}, u32[]{:S(2)}, u32[]{:S(2)}) collective-permute-start(f32[33,16,128]{2,1,0:T(8,128)} %get-tuple-element.76), channel_id=1, source_target_pairs={{0,15},{1,0},{2,1},{3,2},{4,3},{5,4},{6,5},{7,6},{8,7},{9,8},{10,9... | collective-permute-start | bytes 811016 | tf_op jit(solution)/shard_map/ppermute | solution.py:451
  11.6 54.2 %collective-permute-start.4 = (f32[33,16,128]{2,1,0:T(8,128)}, f32[33,16,128]{2,1,0:T(8,128)S(1)}, u32[]{:S(2)}, u32[]{:S(2)}) collective-permute-start(f32[33,16,128]{2,1,0:T(8,128)} %get-tuple-element.83), channel_id=1, source_target_pairs={{0,16},{16,32},{32,48},{48,64},{64,80},{80,96},{96,112},{112,0},{1... | collective-permute-start | bytes 811016 | tf_op jit(solution)/shard_map/ppermute | solution.py:451
  14.3 51.5 %collective-permute-start.5 = (f32[33,16,128]{2,1,0:T(8,128)}, f32[33,16,128]{2,1,0:T(8,128)S(1)}, u32[]{:S(2)}, u32[]{:S(2)}) collective-permute-start(f32[33,16,128]{2,1,0:T(8,128)} %get-tuple-element.84), channel_id=1, source_target_pairs={{0,112},{16,0},{32,16},{48,32},{64,48},{80,64},{96,80},{112,96},{1... | collective-permute-start | bytes 811016 | tf_op jit(solution)/shard_map/ppermute | solution.py:451
  16.8 10.8 %collective-permute-start = (f32[3,16,128]{2,1,0:T(8,128)S(1)}, f32[3,16,128]{2,1,0:T(8,128)S(1)}, u32[]{:S(2)}, u32[]{:S(2)}) collective-permute-start(f32[3,16,128]{2,1,0:T(8,128)S(1)} %get-tuple-element.68), channel_id=1, source_target_pairs={{0,16},{16,32},{32,48},{48,64},{64,80},{80,96},{96,112},{112,0},{1... | collective-permute-start | bytes 73736 | tf_op jit(solution)/shard_map/ppermute | solution.py:451
  27.6 6.4 %collective-permute-start.1 = (f32[3,16,128]{2,1,0:T(8,128)S(1)}, f32[3,16,128]{2,1,0:T(8,128)S(1)}, u32[]{:S(2)}, u32[]{:S(2)}) collective-permute-start(f32[3,16,128]{2,1,0:T(8,128)S(1)} %get-tuple-element.69), channel_id=1, source_target_pairs={{0,112},{16,0},{32,16},{48,32},{64,48},{80,64},{96,80},{112,96},{1... | collective-permute-start | bytes 73736 | tf_op jit(solution)/shard_map/ppermute | solution.py:451
  35.3 20.8 %all-to-all-start = ((f32[128,1,128]{2,1,0:T(1,128)}), f32[128,1,128]{2,1,0:T(1,128)S(1)}, u32[]{:S(2)}, u32[]{:S(2)}) async-start(f32[128,1,128]{2,1,0:T(1,128)} %bitcast.1), calls=%async_computation | async-start | bytes 131072 | tf_op jit(solution)/shard_map/all_to_all | solution.py:461
  47.9 0.7 copy-start.7
  56.1 0.9 copy-start.8
  57.0 0.9 copy-start.26
  58.0 32.8 %copy-start.20 = (f32[2,13,16,128]{3,2,1,0:T(8,128)S(1)}, f32[2,13,16,128]{3,2,1,0:T(8,128)}, u32[]{:S(2)}) copy-start(f32[2,13,16,128]{3,2,1,0:T(8,128)} %copy-done.19) | copy-start | bytes 638980
  58.0 63.0 %copy-start.16 = (f32[2,13,16,128]{3,2,1,0:T(8,128)S(1)}, f32[2,13,16,128]{3,2,1,0:T(8,128)}, u32[]{:S(2)}) copy-start(f32[2,13,16,128]{3,2,1,0:T(8,128)} %copy-done.15) | copy-start | bytes 638980
  59.4 15.8 %all-to-all-start.1 = ((f32[128,1,128]{2,1,0:T(1,128)}), f32[128,1,128]{2,1,0:T(1,128)S(1)}, u32[]{:S(2)}, u32[]{:S(2)}) async-start(f32[128,1,128]{2,1,0:T(1,128)} %bitcast.5), calls=%async_computation.1 | async-start | bytes 131072 | tf_op jit(solution)/shard_map/all_to_all | solution.py:470
  70.0 80.2 %copy-start.14 = (f32[2,13,16,128]{3,2,1,0:T(8,128)S(1)}, f32[2,13,16,128]{3,2,1,0:T(8,128)}, u32[]{:S(2)}) copy-start(f32[2,13,16,128]{3,2,1,0:T(8,128)} %copy-done.13) | copy-start | bytes 638980
  75.2 60.4 %copy-start.22 = (f32[2,13,16,128]{3,2,1,0:T(8,128)S(1)}, f32[2,13,16,128]{3,2,1,0:T(8,128)}, u32[]{:S(2)}) copy-start(f32[2,13,16,128]{3,2,1,0:T(8,128)} %copy-done.21) | copy-start | bytes 638980
  75.2 1.0 copy-start.28
  76.2 88.7 %copy-start.18 = (f32[2,13,16,128]{3,2,1,0:T(8,128)S(1)}, f32[2,13,16,128]{3,2,1,0:T(8,128)}, u32[]{:S(2)}) copy-start(f32[2,13,16,128]{3,2,1,0:T(8,128)} %copy-done.17) | copy-start | bytes 638980
  90.8 88.7 %copy-start.12 = (f32[2,13,16,128]{3,2,1,0:T(8,128)S(1)}, f32[2,13,16,128]{3,2,1,0:T(8,128)}, u32[]{:S(2)}) copy-start(f32[2,13,16,128]{3,2,1,0:T(8,128)} %copy-done.11) | copy-start | bytes 638980
  105.4 0.9 copy-start.24
  121.0 87.8 %copy-start.10 = (f32[2,13,16,128]{3,2,1,0:T(8,128)S(1)}, f32[2,13,16,128]{3,2,1,0:T(8,128)}, u32[]{:S(2)}) copy-start(f32[2,13,16,128]{3,2,1,0:T(8,128)} %copy-done.9) | copy-start | bytes 638980
  135.6 79.2 %copy-start.6 = (s32[15,15,128]{2,1,0:T(8,128)S(1)}, s32[15,15,128]{2,1,0:T(8,128)}, u32[]{:S(2)}) copy-start(s32[15,15,128]{2,1,0:T(8,128)} %count_ref.3) | copy-start | bytes 345604
  135.6 79.2 %copy-start.34 = (s32[12]{0:T(128)S(1)}, s32[12]{0:T(128)}, u32[]{:S(2)}) copy-start(s32[12]{0:T(128)} %shift_ref.5) | copy-start | bytes 148
  210.1 14.1 %all-to-all-start.11 = ((f32[128,1,128]{2,1,0:T(1,128)}), f32[128,1,128]{2,1,0:T(1,128)S(1)}, u32[]{:S(2)}, u32[]{:S(2)}) async-start(f32[128,1,128]{2,1,0:T(1,128)} %bitcast.35), calls=%async_computation.11 | async-start | bytes 131072 | tf_op jit(solution)/shard_map/all_to_all | solution.py:470
  214.8 1.6 copy-start.1
  216.4 1.4 copy-start.4
  217.8 6.4 %copy-start.30 = (f32[15,16,128]{2,1,0:T(8,128)S(1)}, f32[15,16,128]{2,1,0:T(8,128)}, u32[]{:S(2)}) copy-start(f32[15,16,128]{2,1,0:T(8,128)} %copy-done.29) | copy-start | bytes 368644
  (12 other events, 8.1 us)

commit v3 on v2

--- a/solution.py
+++ b/solution.py
@@ -12,13 +12,11 @@
 SLOTS = 6
 EXT = 15
 PAD = 16
-HALO = HALF
-FULL = EXT + 2 * HALO
-PAIRS = (FULL - 1) // 2
+CHUNK = 3
 NZ = 128
 DEVICES = 128
-EDGE_PLANES = 2 * HALO + HALO * (HALO + 1) // 2
-FIELDS = 2 + HALF
+X_LEFT = HALF - 1
+Y_LEFT = HALF
 
 turn_angle = 130.0 * math.pi / 180.0
 excess_coupling = 1e-06
@@ -29,6 +27,7 @@
 
 VMEM = pl.BlockSpec(memory_space=pltpu.VMEM)
 SMEM = pl.BlockSpec(memory_space=pltpu.SMEM)
+ANY = pl.BlockSpec(memory_space=pl.ANY)
 f32 = jnp.float32
 GRANT = pltpu.CompilerParams(vmem_limit_bytes=12 * 2**20)
 
@@ -44,14 +43,18 @@
     return lax.rem(total, jnp.int32(NZ))
 
 
-def edge_offsets():
-    table = []
-    place = 0
-    for field in range(FIELDS):
-        planes = HALO if field < 2 else HALO - (field - 2)
-        table.append((field, place, planes))
-        place += planes
-    return table
+def edge_layout(left):
+    counts = [left, left] + [left - k for k in range(left)]
+    starts = [sum(counts[:k]) for k in range(len(counts))]
+    return list(zip(starts, counts)), sum(counts)
+
+
+def full_planes(left):
+    return EXT + 2 * left
+
+
+def pair_count(left):
+    return (full_planes(left) - 1) // 2
 
 
 def fold(values):
@@ -59,10 +62,24 @@
 
 
 def prep_kernel(
-    shift_ref, v_ref, count_ref, flag_hbm, own_ref, uy_ref, uz_ref, low_ref, high_ref, base_ref, flag_ref, flag_sem
+    shift_hbm, v_hbm, count_hbm, flag_hbm, own_ref, uy_ref, uz_ref, low_ref, high_ref, base_ref,
+    shift_ref, v_ref, count_ref, flag_ref, sems, chunk_sems,
 ):
-    fetch = pltpu.make_async_copy(flag_hbm.at[0], flag_ref, flag_sem)
-    fetch.start()
+    fetches = [
+        pltpu.make_async_copy(shift_hbm, shift_ref, sems.at[0]),
+        pltpu.make_async_copy(count_hbm, count_ref, sems.at[1]),
+        pltpu.make_async_copy(flag_hbm.at[0], flag_ref, sems.at[2]),
+    ]
+    chunks = [
+        pltpu.make_async_copy(
+            v_hbm.at[:, :, pl.ds(CHUNK * c, CHUNK)], v_ref.at[:, :, pl.ds(CHUNK * c, CHUNK)], chunk_sems.at[c]
+        )
+        for c in range(EXT // CHUNK)
+    ]
+    for fetch in fetches + chunks:
+        fetch.start()
+    for fetch in fetches:
+        fetch.wait()
     shift = later_shifts(shift_ref, 0)
     zero_row = jnp.zeros((EXT, 1, NZ), f32)
     for field in range(3):
@@ -72,8 +89,9 @@
     uy_ref[EXT] = jnp.zeros((PAD, NZ), f32)
 
     thermal = energy_y = total = jnp.zeros((EXT, NZ), f32)
-    fetch.wait()
     for i in range(EXT):
+        if i % CHUNK == 0:
+            chunks[i // CHUNK].wait()
         counts = count_ref[i]
         mass = counts.astype(f32)
         inverse = 1.0 / jnp.maximum(mass, 1.0)
@@ -112,75 +130,81 @@
     edge = shape(3, PAD, NZ)
     return pl.pallas_call(
         prep_kernel,
-        in_specs=[SMEM, VMEM, VMEM, pl.BlockSpec(memory_space=pl.ANY)],
+        in_specs=[ANY] * 4,
         out_specs=[VMEM] * 6,
         out_shape=[shape(3, EXT, PAD, NZ), shape(PAD, PAD, NZ), shape(EXT, PAD, NZ), edge, edge, shape(8, NZ)],
-        scratch_shapes=[pltpu.VMEM((EXT, EXT, NZ), jnp.int32), pltpu.SemaphoreType.DMA],
+        scratch_shapes=[
+            pltpu.SMEM((STEPS,), jnp.int32),
+            pltpu.VMEM((3, SLOTS, EXT, EXT, NZ), f32),
+            pltpu.VMEM((EXT, EXT, NZ), jnp.int32),
+            pltpu.VMEM((EXT, EXT, NZ), jnp.int32),
+            pltpu.SemaphoreType.DMA((3,)),
+            pltpu.SemaphoreType.DMA((EXT // CHUNK,)),
+        ],
         compiler_params=GRANT,
         name="prep",
-    )(shifts, v, counts, flags)
-
-
-def spread_kernel(shift_ref, own_ref, uy_ref, flag_ref, sx_ref, sy_ref, xlo_ref, xhi_ref, ylo_ref, yhi_ref, turn_ref):
-    for field in range(HALF):
-        sx_ref[2 + field, :, EXT:PAD, :] = jnp.zeros((EXT, 1, NZ), f32)
-    for i in range(EXT):
-        sx_ref[0, i] = own_ref[0, i]
-        sx_ref[1, i] = own_ref[1, i]
-    for step in range(STEPS):
+    )(*[pltpu.with_memory_space_constraint(array, pltpu.HBM) for array in (shifts, v, counts, flags)])
+
+
+def spread_kernel(shift_ref, own_ref, uy_ref, flag_ref, bits_ref, sy_ref, low_ref, high_ref, turn_ref):
+    bits_ref[:, :, EXT:PAD, :] = jnp.zeros((X_LEFT, EXT, 1, NZ), f32)
+    for step in range(1, STEPS):
         later = later_shifts(shift_ref, step)
         for i in range(EXT):
             bits = pltpu.roll(flag_ref[step, i].astype(f32), later, 1)
             if step % 2 == 0:
-                sx_ref[2 + step // 2, i, 0:EXT, :] = bits
+                bits_ref[step // 2 - 1, i, 0:EXT, :] = bits
             else:
                 turn_ref[step // 2, i * PAD : i * PAD + EXT, :] = bits
     keep = lax.broadcasted_iota(jnp.int32, (PAD, NZ), 0) < EXT
     for i in range(EXT):
         turn_ref[HALF, i * PAD : (i + 1) * PAD, :] = own_ref[1, i]
-    for field in range(FIELDS):
+    for field in range(2 + Y_LEFT):
         for y in range(EXT):
             if field == 0:
                 rows = uy_ref[pl.ds(y, PAD, stride=PAD), :]
             else:
                 rows = turn_ref[HALF if field == 1 else field - 2, pl.ds(y, PAD, stride=PAD), :]
             sy_ref[field, y] = jnp.where(keep, rows, 0.0)
-
-    for field, place, planes in edge_offsets():
+    for field, (place, planes) in enumerate(edge_layout(Y_LEFT)[0]):
         for k in range(planes):
-            xlo_ref[place + k] = sx_ref[field, k]
-            xhi_ref[place + k] = sx_ref[field, EXT - planes + k]
-            ylo_ref[place + k] = sy_ref[field, k]
-            yhi_ref[place + k] = sy_ref[field, EXT - planes + k]
+            low_ref[place + k] = sy_ref[field, k]
+            high_ref[place + k] = sy_ref[field, EXT - planes + k]
 
 
 def spread(shifts, own, uy, flags):
-    edge = shape(EDGE_PLANES, PAD, NZ)
-    full = shape(FIELDS, EXT, PAD, NZ)
+    edge = shape(edge_layout(Y_LEFT)[1], PAD, NZ)
     return pl.pallas_call(
         spread_kernel,
         in_specs=[SMEM, VMEM, VMEM, VMEM],
-        out_specs=[VMEM] * 6,
-        out_shape=[full, full, edge, edge, edge, edge],
+        out_specs=[VMEM] * 4,
+        out_shape=[shape(X_LEFT, EXT, PAD, NZ), shape(2 + Y_LEFT, EXT, PAD, NZ), edge, edge],
         scratch_shapes=[pltpu.VMEM((HALF + 1, PAD * PAD, NZ), f32)],
         compiler_params=GRANT,
         name="spread",
     )(shifts, own, uy.reshape(PAD * PAD, NZ), flags)
 
 
-def first_kernel(parity_ref, own_ref, below_ref, above_ref, carry_ref, rows_ref, out_ref, u_ref, mass_ref, bits_ref):
-    for field, array_ref in enumerate((u_ref, mass_ref, bits_ref)):
+def lower_start(parity_ref, step, brick_axis, halo):
+    return lax.rem(parity_ref[step] + lax.axis_index(brick_axis) * EXT + halo, jnp.int32(2))
+
+
+def first_kernel(
+    parity_ref, own_ref, bits_ref, below_ref, above_ref, carry_ref,
+    rows_ref, out_ref, sx_ref, xlo_ref, xhi_ref, u_ref, mass_ref, allow_ref,
+):
+    for field, array_ref in enumerate((u_ref, mass_ref, allow_ref)):
         array_ref[0] = below_ref[field]
         array_ref[EXT + 1] = above_ref[field]
         for k in range(EXT):
             array_ref[1 + k] = own_ref[field, k]
-    start = lax.rem(lower_start(parity_ref, 0, "bx") + 1, jnp.int32(2))
+    start = lower_start(parity_ref, 0, "bx", 1)
     wide = jnp.broadcast_to(carry_ref[0:1, :], (PAD, NZ))
     for k in range((EXT + 1) // 2):
         plane = start + 2 * k
         low, high = u_ref[plane], u_ref[plane + 1]
         weight_low, weight_high = pair_weights(mass_ref[plane], mass_ref[plane + 1])
-        allowed = jnp.maximum(bits_ref[plane], bits_ref[plane + 1])
+        allowed = jnp.maximum(allow_ref[plane], allow_ref[plane + 1])
         closing = jnp.maximum(low - high, 0.0)
         push = allowed * closing * jnp.tanh(wide * closing)
         u_ref[plane] = low - weight_low * push
@@ -189,6 +213,14 @@
     for k in range(EXT):
         u = u_ref[1 + k]
         energy = energy + own_ref[1, k] * u * u
+        sx_ref[0, k] = u
+        sx_ref[1, k] = own_ref[1, k]
+        for j in range(X_LEFT):
+            sx_ref[2 + j, k] = bits_ref[j, k]
+    for field, (place, planes) in enumerate(edge_layout(X_LEFT)[0]):
+        for k in range(planes):
+            xlo_ref[place + k] = sx_ref[field, k]
+            xhi_ref[place + k] = sx_ref[field, EXT - planes + k]
     mine = fold(energy)
     half = NZ // 2
     lane = lax.broadcasted_iota(jnp.int32, (1, NZ), 1)
@@ -200,20 +232,17 @@
     rows_ref[...] = jnp.broadcast_to(local, (DEVICES, NZ))
 
 
-def first(parity, own, below, above, carry):
+def first(parity, own, bits, below, above, carry):
+    edge = shape(edge_layout(X_LEFT)[1], PAD, NZ)
     return pl.pallas_call(
         first_kernel,
-        in_specs=[SMEM] + [VMEM] * 4,
-        out_specs=[VMEM] * 2,
-        out_shape=[shape(DEVICES, NZ), shape(8, NZ)],
+        in_specs=[SMEM] + [VMEM] * 5,
+        out_specs=[VMEM] * 5,
+        out_shape=[shape(DEVICES, NZ), shape(8, NZ), shape(2 + X_LEFT, EXT, PAD, NZ), edge, edge],
         scratch_shapes=[pltpu.VMEM((EXT + 2, PAD, NZ), f32)] * 3,
         compiler_params=GRANT,
         name="first",
-    )(parity, own, below, above, carry)
-
-
-def lower_start(parity_ref, step, brick_axis):
-    return lax.rem(parity_ref[step] + lax.axis_index(brick_axis) * EXT, jnp.int32(2))
+    )(parity, own, bits, below, above, carry)
 
 
 def pair_weights(mass_low, mass_high):
@@ -221,66 +250,52 @@
     return reduced / jnp.maximum(mass_low, 1.0), reduced / jnp.maximum(mass_high, 1.0)
 
 
-def pairs_step(u_ref, weight_ref, start, wide):
-    for k in range(PAIRS):
-        plane = start + 2 * k
-        low, high = u_ref[plane], u_ref[plane + 1]
-        closing = jnp.maximum(low - high, 0.0)
-        push = closing * jnp.tanh(wide * closing)
-        u_ref[plane] = low - weight_ref[0, k] * push
-        u_ref[plane + 1] = high + weight_ref[1, k] * push
-
-
-def join_kernel(parity_ref, own_ref, below_ref, above_ref, u_ref, *rest, first_step, brick_axis):
-    weight_refs, (own_mass_ref, mass_ref, bits_ref, both_ref) = rest[:HALF], rest[HALF:]
-    for field, place, planes in edge_offsets():
+def join_kernel(parity_ref, own_ref, below_ref, above_ref, u_ref, weight_ref, mass_ref, all_mass_ref, bits_ref, both_ref, *, left, brick_axis):
+    for field, (place, planes) in enumerate(edge_layout(left)[0]):
         for k in range(planes):
             low, high = below_ref[place + k], above_ref[place + k]
+            below, above = left - planes + k, left + EXT + k
             if field == 0:
-                u_ref[HALO - planes + k] = low
-                u_ref[HALO + EXT + k] = high
+                u_ref[below], u_ref[above] = low, high
             elif field == 1:
-                mass_ref[HALO - planes + k] = low
-                mass_ref[HALO + EXT + k] = high
+                all_mass_ref[below], all_mass_ref[above] = low, high
             else:
-                bits_ref[field - 2, HALO - planes + k] = low
-                bits_ref[field - 2, HALO + EXT + k] = high
-        for k in range(HALO - planes):
+                bits_ref[field - 2, below], bits_ref[field - 2, above] = low, high
+        for k in range(left - planes):
             bits_ref[field - 2, k] = jnp.zeros((PAD, NZ), f32)
-            bits_ref[field - 2, FULL - 1 - k] = jnp.zeros((PAD, NZ), f32)
+            bits_ref[field - 2, full_planes(left) - 1 - k] = jnp.zeros((PAD, NZ), f32)
     for k in range(EXT):
-        u_ref[HALO + k] = own_ref[0, k]
-        mass_ref[HALO + k] = own_ref[1, k]
-        own_mass_ref[k] = own_ref[1, k]
-        for j in range(HALF):
-            bits_ref[j, HALO + k] = own_ref[2 + j, k]
-    for plane in range(FULL - 1):
-        both_ref[0, plane], both_ref[1, plane] = pair_weights(mass_ref[plane], mass_ref[plane + 1])
-    for j in range(HALF):
-        start = lower_start(parity_ref, first_step + 2 * j, brick_axis)
-        for k in range(PAIRS):
+        u_ref[left + k] = own_ref[0, k]
+        all_mass_ref[left + k] = own_ref[1, k]
+        mass_ref[k] = own_ref[1, k]
+        for j in range(left):
+            bits_ref[j, left + k] = own_ref[2 + j, k]
+    for plane in range(full_planes(left) - 1):
+        both_ref[0, plane], both_ref[1, plane] = pair_weights(all_mass_ref[plane], all_mass_ref[plane + 1])
+    for j in range(left):
+        step = STEPS - 2 * (left - j) + (0 if brick_axis == "bx" else 1)
+        start = lower_start(parity_ref, step, brick_axis, left)
+        for k in range(pair_count(left)):
             plane = start + 2 * k
             allowed = jnp.maximum(bits_ref[j, plane], bits_ref[j, plane + 1])
-            weight_refs[j][0, k] = allowed * both_ref[0, plane]
-            weight_refs[j][1, k] = allowed * both_ref[1, plane]
-    if first_step == 0:
-        start = lower_start(parity_ref, 0, brick_axis)
-        pairs_step(u_ref, weight_refs[0], start, jnp.full((PAD, NZ), 1.0 / BIG, f32))
-
-
-def join(parity, own, below, above, first_step, brick_axis):
+            weight_ref[j, 0, k] = allowed * both_ref[0, plane]
+            weight_ref[j, 1, k] = allowed * both_ref[1, plane]
+
+
+def join(parity, own, below, above, left, brick_axis):
     def body(*refs):
-        join_kernel(*refs, first_step=first_step, brick_axis=brick_axis)
-
+        join_kernel(*refs, left=left, brick_axis=brick_axis)
+
+    full, pairs = full_planes(left), pair_count(left)
     return pl.pallas_call(
         body,
         in_specs=[SMEM, VMEM, VMEM, VMEM],
-        out_specs=[VMEM] * (2 + HALF),
-        out_shape=[shape(FULL, PAD, NZ)] + [shape(2, PAIRS, PAD, NZ)] * HALF + [shape(EXT, PAD, NZ)],
+        out_specs=[VMEM] * 3,
+        out_shape=[shape(full, PAD, NZ), shape(left, 2, pairs, PAD, NZ), shape(EXT, PAD, NZ)],
         scratch_shapes=[
-            pltpu.VMEM((FULL, PAD, NZ), f32),
-            pltpu.VMEM((HALF, FULL, PAD, NZ), f32),
-            pltpu.VMEM((2, FULL, PAD, NZ), f32),
+            pltpu.VMEM((full, PAD, NZ), f32),
+            pltpu.VMEM((left, full, PAD, NZ), f32),
+            pltpu.VMEM((2, full, PAD, NZ), f32),
         ],
         compiler_params=GRANT,
         name="join",
@@ -304,16 +319,24 @@
 
 
 def step_kernel(
-    parity_ref, heat_ref, received_ref, carry_ref, u_in_ref, weight_ref, mass_ref, u_ref, rows_ref, out_ref, *, step, brick_axis
+    parity_ref, heat_ref, received_ref, carry_ref, u_in_ref, weight_ref, mass_ref, u_ref, rows_ref, out_ref, *, step, left, brick_axis
 ):
     scale, total = next_scale(received_ref, carry_ref, heat_ref, step - 1)
-    start = lower_start(parity_ref, step, brick_axis)
-    for k in range(FULL):
+    start = lower_start(parity_ref, step, brick_axis, left)
+    wide = jnp.broadcast_to(scale, (PAD, NZ))
+    turn = left - (STEPS + 1 - step) // 2
+    for k in range(full_planes(left)):
         u_ref[k] = u_in_ref[k]
-    pairs_step(u_ref, weight_ref, start, jnp.broadcast_to(scale, (PAD, NZ)))
+    for k in range(pair_count(left)):
+        plane = start + 2 * k
+        low, high = u_ref[plane], u_ref[plane + 1]
+        closing = jnp.maximum(low - high, 0.0)
+        push = closing * jnp.tanh(wide * closing)
+        u_ref[plane] = low - weight_ref[turn, 0, k] * push
+        u_ref[plane + 1] = high + weight_ref[turn, 1, k] * push
     energy = jnp.zeros((PAD, NZ), f32)
     for k in range(EXT):
-        u = u_ref[HALO + k]
+        u = u_ref[left + k]
         energy = energy + mass_ref[k] * u * u
     mine = fold(energy)
     other = carry_ref[4:5, :] if step % 2 == 0 else carry_ref[3:4, :]
@@ -326,16 +349,16 @@
 
 
 def collide(step, parity, heat, received, carry, u, weight, mass):
-    brick_axis = "bx" if step % 2 == 0 else "by"
+    left, brick_axis = (X_LEFT, "bx") if step % 2 == 0 else (Y_LEFT, "by")
 
     def body(*refs):
-        step_kernel(*refs, step=step, brick_axis=brick_axis)
+        step_kernel(*refs, step=step, left=left, brick_axis=brick_axis)
 
     return pl.pallas_call(
         body,
         in_specs=[SMEM] * 2 + [VMEM] * 5,
         out_specs=[VMEM] * 3,
-        out_shape=[shape(FULL, PAD, NZ), shape(DEVICES, NZ), shape(8, NZ)],
+        out_shape=[shape(full_planes(left), PAD, NZ), shape(DEVICES, NZ), shape(8, NZ)],
         compiler_params=GRANT,
         name="collide",
     )(parity, heat, received, carry, u, weight, mass)
@@ -419,11 +442,11 @@
 
     @pl.when(member == 0)
     def _():
-        write(lambda i: ux_ref[HALO + i, 0:EXT, :])
+        write(lambda i: ux_ref[X_LEFT + i, 0:EXT, :])
 
     @pl.when(member == 1)
     def _():
-        write(lambda i: uy_ref[pl.ds(HALO * PAD + i, EXT, stride=PAD), :])
+        write(lambda i: uy_ref[pl.ds(Y_LEFT * PAD + i, EXT, stride=PAD), :])
 
     @pl.when(member == 2)
     def _():
@@ -441,7 +464,7 @@
         out_shape=shape(3, SLOTS, EXT, EXT, NZ),
         compiler_params=GRANT,
         name="finish",
-    )(heat, received, carry, ux, uy.reshape(FULL * PAD, NZ), uz, own, w)
+    )(heat, received, carry, ux, uy.reshape(full_planes(Y_LEFT) * PAD, NZ), uz, own, w)
 
 
 def exchange(low_edge, high_edge, axis):
@@ -451,23 +474,27 @@
     return lax.ppermute(low_edge, axis, down), lax.ppermute(high_edge, axis, up)
 
 
+def sum_over_devices(rows):
+    return lax.all_to_all(rows, ("bx", "by"), 0, 0, tiled=True)
+
+
 def per_device(v, counts, spin, flags, parity, shifts, heat):
     own, uy, uz, low, high, carry = prep(shifts, v, counts, flags)
     above, below = exchange(low, high, "bx")
-    sx, sy, xlo, xhi, ylo, yhi = spread(shifts, own, uy, flags)
+    bits, sy, ylo, yhi = spread(shifts, own, uy, flags)
     y_above, y_below = exchange(ylo, yhi, "by")
+    rows, carry, sx, xlo, xhi = first(parity, own, bits, below, above, carry)
+    received = sum_over_devices(rows)
     x_above, x_below = exchange(xlo, xhi, "bx")
-    rows, carry = first(parity, own, below, above, carry)
-    received = lax.all_to_all(rows, ("bx", "by"), 0, 0, tiled=True)
     w = turn(shifts, v, counts, spin)
-    uy, *y_weights, y_mass = join(parity, sy, y_below, y_above, 1, "by")
-    ux, *x_weights, x_mass = join(parity, sx, x_below, x_above, 0, "bx")
+    uy, y_weights, y_mass = join(parity, sy, y_below, y_above, Y_LEFT, "by")
+    ux, x_weights, x_mass = join(parity, sx, x_below, x_above, X_LEFT, "bx")
     for step in range(1, STEPS):
         if step % 2 == 0:
-            ux, rows, carry = collide(step, parity, heat, received, carry, ux, x_weights[step // 2], x_mass)
+            ux, rows, carry = collide(step, parity, heat, received, carry, ux, x_weights, x_mass)
         else:
-            uy, rows, carry = collide(step, parity, heat, received, carry, uy, y_weights[step // 2], y_mass)
-        received = lax.all_to_all(rows, ("bx", "by"), 0, 0, tiled=True)
+            uy, rows, carry = collide(step, parity, heat, received, carry, uy, y_weights, y_mass)
+        received = sum_over_devices(rows)
     return finish(heat, received, carry, ux, uy, uz, own, w)
 
 

time: 228 us -> 207 us (0.908)
  local copies, waits for them, and re-layouts: 19.5 us -> 7.34 us
  starting transfers between devices: 36.5 us -> 32.4 us
  waiting for transfers between devices: 22.7 us -> 19.3 us
    unnamed x70 -> x24, local copies, waits for them, and re-layouts: 19.5 us -> 7.34 us
    ppermute x3, waiting for transfers between devices: 10.3 us -> 1.22 us  [exchange(): lax.ppermute(high_edge, axis, up)]
    all_to_all x3, waiting for transfers between devices: 11.4 us -> 17.3 us  [sum_over_devices(): return lax.all_to_all(rows, ('bx', 'by'), 0, 0, tiled=True)]
    all_to_all x3, starting transfers between devices: 22.3 us -> 19.1 us  [sum_over_devices(): return lax.all_to_all(rows, ('bx', 'by'), 0, 0, tiled=True)]
    ppermute x3, starting transfers between devices: 7.87 us -> 5.39 us  [exchange(): lax.ppermute(low_edge, axis, down)]
where the time goes in v3:
time: 207 us
  blocking collectives  125 us (60%)
  starting transfers between devices  32.4 us (16%)
  Pallas kernels  22.9 us (11%)
  waiting for transfers between devices  19.3 us (9%)
  local copies, waits for them, and re-layouts  7.34 us (4%)
    all_to_all x9, blocking collectives, sum_over_devices(): return lax.all_to_all(rows, ('bx', 'by'), 0, 0, tiled=True)  125 us
    all_to_all x3, starting transfers between devices, sum_over_devices(): return lax.all_to_all(rows, ('bx', 'by'), 0, 0, tiled=True)  19.1 us
    all_to_all x3, waiting for transfers between devices, sum_over_devices(): return lax.all_to_all(rows, ('bx', 'by'), 0, 0, tiled=True)  17.3 us
    pallas_call x11, Pallas kernels, collide(): pl.pallas_call(body, in_specs=[SMEM] * 2 + [VMEM] * 5, out_specs=[VMEM] *...  9.66 us
    ppermute x3, starting transfers between devices, exchange(): lax.ppermute(high_edge, axis, up)  7.97 us
    unnamed x24, local copies, waits for them, and re-layouts  7.34 us
    ppermute x3, starting transfers between devices, exchange(): lax.ppermute(low_edge, axis, down)  5.39 us
  transfers between devices with their start and end apart: 9, of which 5 were waited for; matrix products, arithmetic and copies ran while one was open for 0% of the time, Pallas kernels for 4%

profile of v3, /device:TPU:1, one launch (start us, length us, event | category | flops | bytes accessed | tf_op | source)
XLA Modules:
  0.0 206.8 jit_solution(6282898365386176653)
XLA Ops:
  0.0 2.2 %prep.1 = (f32[3,15,16,128]{3,2,1,0:T(8,128)S(1)}, f32[16,16,128]{2,1,0:T(8,128)S(1)}, f32[15,16,128]{2,1,0:T(8,128)S(1)}, f32[3,16,128]{2,1,0:T(8,128)S(1)}, f3...) custom-call(s32[12]{0:T(128)} %shift_ref.3, f32[3,6,15,15,128]{4,3,2,1,0:T(8,128)} %v_ref.1, s32[15,15,128]{2,1,0:T(8,128)} %count_ref.1, ...), custom_call_target="tpu_custom_call" | custom-call | tf_op jit(solution)/shard_map/prep/pallas_call | solution.py:131
  2.3 1.1 spread.1
  3.4 3.1 %collective-permute-start.2 = (f32[33,16,128]{2,1,0:T(8,128)S(1)}, f32[33,16,128]{2,1,0:T(8,128)S(1)}, u32[]{:S(2)}, u32[]{:S(2)}) collective-permute-start(f32[33,16,128]{2,1,0:T(8,128)S(1)} %get-tuple-element.68), channel_id=1, source_target_pairs={{0,1},{1,2},{2,3},{3,4},{4,5},{5,6},{6,7},{7,8},{8,9},{9,10},{10,1... | collective-permute-start | bytes 811016 | tf_op jit(solution)/shard_map/ppermute | solution.py:474
  6.5 2.7 %collective-permute-start = (f32[3,16,128]{2,1,0:T(8,128)S(1)}, f32[3,16,128]{2,1,0:T(8,128)S(1)}, u32[]{:S(2)}, u32[]{:S(2)}) collective-permute-start(f32[3,16,128]{2,1,0:T(8,128)S(1)} %get-tuple-element.62), channel_id=1, source_target_pairs={{0,16},{16,32},{32,48},{48,64},{64,80},{80,96},{96,112},{112,0},{1... | collective-permute-start | bytes 73736 | tf_op jit(solution)/shard_map/ppermute | solution.py:474
  9.2 2.5 %collective-permute-start.1 = (f32[3,16,128]{2,1,0:T(8,128)S(1)}, f32[3,16,128]{2,1,0:T(8,128)S(1)}, u32[]{:S(2)}, u32[]{:S(2)}) collective-permute-start(f32[3,16,128]{2,1,0:T(8,128)S(1)} %get-tuple-element.63), channel_id=1, source_target_pairs={{0,112},{16,0},{32,16},{48,32},{64,48},{80,64},{96,80},{112,96},{1... | collective-permute-start | bytes 73736 | tf_op jit(solution)/shard_map/ppermute | solution.py:474
  11.7 1.2 collective-permute-done.below_ref
  13.7 1.5 first.1
  16.1 2.1 %collective-permute-start.4 = (f32[25,16,128]{2,1,0:T(8,128)}, f32[25,16,128]{2,1,0:T(8,128)}, u32[]{:S(2)}, u32[]{:S(2)}) collective-permute-start(f32[25,16,128]{2,1,0:T(8,128)} %get-tuple-element.76), channel_id=1, source_target_pairs={{0,16},{16,32},{32,48},{48,64},{64,80},{80,96},{96,112},{112,0},{1... | collective-permute-start | bytes 614408 | tf_op jit(solution)/shard_map/ppermute | solution.py:474
  18.2 2.9 %collective-permute-start.5 = (f32[25,16,128]{2,1,0:T(8,128)}, f32[25,16,128]{2,1,0:T(8,128)}, u32[]{:S(2)}, u32[]{:S(2)}) collective-permute-start(f32[25,16,128]{2,1,0:T(8,128)} %get-tuple-element.77), channel_id=1, source_target_pairs={{0,112},{16,0},{32,16},{48,32},{64,48},{80,64},{96,80},{112,96},{1... | collective-permute-start | bytes 614408 | tf_op jit(solution)/shard_map/ppermute | solution.py:474
  21.1 9.9 %all-to-all-start = ((f32[128,1,128]{2,1,0:T(1,128)}), f32[128,1,128]{2,1,0:T(1,128)S(1)}, u32[]{:S(2)}, u32[]{:S(2)}) async-start(f32[128,1,128]{2,1,0:T(1,128)} %bitcast.2), calls=%async_computation | async-start | bytes 131072 | tf_op jit(solution)/shard_map/all_to_all | solution.py:478
  32.5 8.0 %all-to-all-done = f32[128,1,128]{2,1,0:T(1,128)S(1)} async-done(((f32[128,1,128]{2,1,0:T(1,128)}), f32[128,1,128]{2,1,0:T(1,128)S(1)}, u32[]{:S(2)}, u32[]{:S(2)}) %all-to-all-start) | async-done | bytes 65568 | tf_op jit(solution)/shard_map/all_to_all | solution.py:478
  41.5 1.4 collide.11
  42.9 4.6 %all-to-all-start.1 = ((f32[128,1,128]{2,1,0:T(1,128)}), f32[128,1,128]{2,1,0:T(1,128)S(1)}, u32[]{:S(2)}, u32[]{:S(2)}) async-start(f32[128,1,128]{2,1,0:T(1,128)} %bitcast.5), calls=%async_computation.1 | async-start | bytes 131072 | tf_op jit(solution)/shard_map/all_to_all | solution.py:478
  47.6 1.1 copy-done.4
  48.7 1.3 join.3
  50.0 7.1 %all-to-all-done.1 = f32[128,1,128]{2,1,0:T(1,128)S(1)} async-done(((f32[128,1,128]{2,1,0:T(1,128)}), f32[128,1,128]{2,1,0:T(1,128)S(1)}, u32[]{:S(2)}, u32[]{:S(2)}) %all-to-all-start.1) | async-done | bytes 65568 | tf_op jit(solution)/shard_map/all_to_all | solution.py:478
  57.8 13.9 %all_to_all.132 = f32[128,1,128]{2,1,0:T(1,128)S(1)} all-to-all(f32[128,1,128]{2,1,0:T(1,128)S(1)} %bitcast.65), channel_id=1, replica_groups=mesh['bx'=8,'by'=16] {'bx','by'}, dimensions={0} | all-to-all | bytes 131072 | tf_op jit(solution)/shard_map/all_to_all | solution.py:478
  72.5 13.9 %all_to_all.133 = f32[128,1,128]{2,1,0:T(1,128)S(1)} all-to-all(f32[128,1,128]{2,1,0:T(1,128)S(1)} %bitcast.66), channel_id=1, replica_groups=mesh['bx'=8,'by'=16] {'bx','by'}, dimensions={0} | all-to-all | bytes 131072 | tf_op jit(solution)/shard_map/all_to_all | solution.py:478
  87.1 13.8 %all_to_all.134 = f32[128,1,128]{2,1,0:T(1,128)S(1)} all-to-all(f32[128,1,128]{2,1,0:T(1,128)S(1)} %bitcast.67), channel_id=1, replica_groups=mesh['bx'=8,'by'=16] {'bx','by'}, dimensions={0} | all-to-all | bytes 131072 | tf_op jit(solution)/shard_map/all_to_all | solution.py:478
  101.7 13.8 %all_to_all.135 = f32[128,1,128]{2,1,0:T(1,128)S(1)} all-to-all(f32[128,1,128]{2,1,0:T(1,128)S(1)} %bitcast.68), channel_id=1, replica_groups=mesh['bx'=8,'by'=16] {'bx','by'}, dimensions={0} | all-to-all | bytes 131072 | tf_op jit(solution)/shard_map/all_to_all | solution.py:478
  116.3 13.9 %all_to_all.136 = f32[128,1,128]{2,1,0:T(1,128)S(1)} all-to-all(f32[128,1,128]{2,1,0:T(1,128)S(1)} %bitcast.69), channel_id=1, replica_groups=mesh['bx'=8,'by'=16] {'bx','by'}, dimensions={0} | all-to-all | bytes 131072 | tf_op jit(solution)/shard_map/all_to_all | solution.py:478
  130.9 13.8 %all_to_all.137 = f32[128,1,128]{2,1,0:T(1,128)S(1)} all-to-all(f32[128,1,128]{2,1,0:T(1,128)S(1)} %bitcast.70), channel_id=1, replica_groups=mesh['bx'=8,'by'=16] {'bx','by'}, dimensions={0} | all-to-all | bytes 131072 | tf_op jit(solution)/shard_map/all_to_all | solution.py:478
  145.5 13.8 %all_to_all.138 = f32[128,1,128]{2,1,0:T(1,128)S(1)} all-to-all(f32[128,1,128]{2,1,0:T(1,128)S(1)} %bitcast.71), channel_id=1, replica_groups=mesh['bx'=8,'by'=16] {'bx','by'}, dimensions={0} | all-to-all | bytes 131072 | tf_op jit(solution)/shard_map/all_to_all | solution.py:478
  160.2 13.8 %all_to_all.139 = f32[128,1,128]{2,1,0:T(1,128)S(1)} all-to-all(f32[128,1,128]{2,1,0:T(1,128)S(1)} %bitcast.72), channel_id=1, replica_groups=mesh['bx'=8,'by'=16] {'bx','by'}, dimensions={0} | all-to-all | bytes 131072 | tf_op jit(solution)/shard_map/all_to_all | solution.py:478
  174.8 13.8 %all_to_all.140 = f32[128,1,128]{2,1,0:T(1,128)S(1)} all-to-all(f32[128,1,128]{2,1,0:T(1,128)S(1)} %bitcast.64), channel_id=1, replica_groups=mesh['bx'=8,'by'=16] {'bx','by'}, dimensions={0} | all-to-all | bytes 131072 | tf_op jit(solution)/shard_map/all_to_all | solution.py:478
  188.6 1.4 collide.21
  190.0 4.6 %all-to-all-start.11 = ((f32[128,1,128]{2,1,0:T(1,128)}), f32[128,1,128]{2,1,0:T(1,128)S(1)}, u32[]{:S(2)}, u32[]{:S(2)}) async-start(f32[128,1,128]{2,1,0:T(1,128)} %bitcast.35), calls=%async_computation.11 | async-start | bytes 131072 | tf_op jit(solution)/shard_map/all_to_all | solution.py:478
  194.7 1.6 copy-done
  196.3 1.4 copy-done.2
  198.3 3.6 %turn.1.w_ref = f32[3,6,15,15,128]{4,3,2,1,0:T(8,128)S(1)} custom-call(s32[12]{0:T(128)S(1)} %copy-done.11, f32[3,6,15,15,128]{4,3,2,1,0:T(8,128)S(1)} %copy-done, s32[15,15,128]{2,1,0:T(8,128)S(1)} %copy-done.5, s32[12,15,15,128]{3,2,1,0:T(8,128)S(1)} %copy-done.2), custom_call_target="tpu_custom_call" | custom-call | tf_op jit(solution)/shard_map/turn/pallas_call | solution.py:421
  201.9 2.2 %all-to-all-done.11 = f32[128,1,128]{2,1,0:T(1,128)S(1)} async-done(((f32[128,1,128]{2,1,0:T(1,128)}), f32[128,1,128]{2,1,0:T(1,128)S(1)}, u32[]{:S(2)}, u32[]{:S(2)}) %all-to-all-start.11) | async-done | bytes 65568 | tf_op jit(solution)/shard_map/all_to_all | solution.py:478
  204.1 2.7 %finish.1 = f32[3,6,15,15,128]{4,3,2,1,0:T(8,128)} custom-call(f32[12]{0:T(128)S(1)} %copy-done.9, f32[128,128]{1,0:T(8,128)S(1)} %bitcast.50, f32[8,128]{1,0:T(8,128)S(1)} %get-tuple-element.109.carry_ref, f32[25,16,128]{2,1,0:T(8,128)S(1)} %get-tuple-element.110.ux_ref, f32[432,128]{1,0:T(8,128)S(1)} %bitcast.62, ...), custom_call_target="tpu_custom_call" | custom-call | tf_op jit(solution)/shard_map/finish/pallas_call | solution.py:459
  (37 shorter events, 11.7 us)
Async XLA Ops:
  0.0 2.2 %copy-start.10 = (s32[12]{0:T(128)S(1)}, s32[12]{0:T(128)}, u32[]{:S(2)}) copy-start(s32[12]{0:T(128)} %shift_ref.3) | copy-start | bytes 148
  0.0 2.3 %copy-start.1 = (s32[12,15,15,128]{3,2,1,0:T(8,128)S(1)}, s32[12,15,15,128]{3,2,1,0:T(8,128)}, u32[]{:S(2)}) copy-start(s32[12,15,15,128]{3,2,1,0:T(8,128)} %flag_ref.1) | copy-start | bytes 4147204
  0.0 13.7 %copy-start.8 = (s32[12]{0:T(128)S(1)}, s32[12]{0:T(128)}, u32[]{:S(2)}) copy-start(s32[12]{0:T(128)} %refs_0_.25) | copy-start | bytes 148
  2.3 38.3 %copy-start.9 = (f32[12]{0:T(128)S(1)}, f32[12]{0:T(128)}, u32[]{:S(2)}) copy-start(f32[12]{0:T(128)} %heat_ref.1) | copy-start | bytes 148
  3.4 27.6 %collective-permute-start.2 = (f32[33,16,128]{2,1,0:T(8,128)S(1)}, f32[33,16,128]{2,1,0:T(8,128)S(1)}, u32[]{:S(2)}, u32[]{:S(2)}) collective-permute-start(f32[33,16,128]{2,1,0:T(8,128)S(1)} %get-tuple-element.68), channel_id=1, source_target_pairs={{0,1},{1,2},{2,3},{3,4},{4,5},{5,6},{6,7},{7,8},{8,9},{9,10},{10,1... | collective-permute-start | bytes 811016 | tf_op jit(solution)/shard_map/ppermute | solution.py:474
  6.5 24.5 %collective-permute-start.3 = (f32[33,16,128]{2,1,0:T(8,128)S(1)}, f32[33,16,128]{2,1,0:T(8,128)S(1)}, u32[]{:S(2)}, u32[]{:S(2)}) collective-permute-start(f32[33,16,128]{2,1,0:T(8,128)S(1)} %get-tuple-element.69), channel_id=1, source_target_pairs={{0,15},{1,0},{2,1},{3,2},{4,3},{5,4},{6,5},{7,6},{8,7},{9,8},{10,9... | collective-permute-start | bytes 811016 | tf_op jit(solution)/shard_map/ppermute | solution.py:474
  6.5 6.4 %collective-permute-start = (f32[3,16,128]{2,1,0:T(8,128)S(1)}, f32[3,16,128]{2,1,0:T(8,128)S(1)}, u32[]{:S(2)}, u32[]{:S(2)}) collective-permute-start(f32[3,16,128]{2,1,0:T(8,128)S(1)} %get-tuple-element.62), channel_id=1, source_target_pairs={{0,16},{16,32},{32,48},{48,64},{64,80},{80,96},{96,112},{112,0},{1... | collective-permute-start | bytes 73736 | tf_op jit(solution)/shard_map/ppermute | solution.py:474
  9.2 4.4 %collective-permute-start.1 = (f32[3,16,128]{2,1,0:T(8,128)S(1)}, f32[3,16,128]{2,1,0:T(8,128)S(1)}, u32[]{:S(2)}, u32[]{:S(2)}) collective-permute-start(f32[3,16,128]{2,1,0:T(8,128)S(1)} %get-tuple-element.63), channel_id=1, source_target_pairs={{0,112},{16,0},{32,16},{48,32},{64,48},{80,64},{96,80},{112,96},{1... | collective-permute-start | bytes 73736 | tf_op jit(solution)/shard_map/ppermute | solution.py:474
  15.2 0.9 copy-start.3
  16.1 31.5 %collective-permute-start.4 = (f32[25,16,128]{2,1,0:T(8,128)}, f32[25,16,128]{2,1,0:T(8,128)}, u32[]{:S(2)}, u32[]{:S(2)}) collective-permute-start(f32[25,16,128]{2,1,0:T(8,128)} %get-tuple-element.76), channel_id=1, source_target_pairs={{0,16},{16,32},{32,48},{48,64},{64,80},{80,96},{96,112},{112,0},{1... | collective-permute-start | bytes 614408 | tf_op jit(solution)/shard_map/ppermute | solution.py:474
  18.2 29.3 %collective-permute-start.5 = (f32[25,16,128]{2,1,0:T(8,128)}, f32[25,16,128]{2,1,0:T(8,128)}, u32[]{:S(2)}, u32[]{:S(2)}) collective-permute-start(f32[25,16,128]{2,1,0:T(8,128)} %get-tuple-element.77), channel_id=1, source_target_pairs={{0,112},{16,0},{32,16},{48,32},{64,48},{80,64},{96,80},{112,96},{1... | collective-permute-start | bytes 614408 | tf_op jit(solution)/shard_map/ppermute | solution.py:474
  21.1 19.4 %all-to-all-start = ((f32[128,1,128]{2,1,0:T(1,128)}), f32[128,1,128]{2,1,0:T(1,128)S(1)}, u32[]{:S(2)}, u32[]{:S(2)}) async-start(f32[128,1,128]{2,1,0:T(1,128)} %bitcast.2), calls=%async_computation | async-start | bytes 131072 | tf_op jit(solution)/shard_map/all_to_all | solution.py:478
  31.9 0.7 copy-start.6
  40.6 0.9 copy-start.7
  42.9 14.1 %all-to-all-start.1 = ((f32[128,1,128]{2,1,0:T(1,128)}), f32[128,1,128]{2,1,0:T(1,128)S(1)}, u32[]{:S(2)}, u32[]{:S(2)}) async-start(f32[128,1,128]{2,1,0:T(1,128)} %bitcast.5), calls=%async_computation.1 | async-start | bytes 131072 | tf_op jit(solution)/shard_map/all_to_all | solution.py:478
  47.6 1.2 copy-start.4
  159.4 35.3 %copy-start.5 = (s32[15,15,128]{2,1,0:T(8,128)S(1)}, s32[15,15,128]{2,1,0:T(8,128)}, u32[]{:S(2)}) copy-start(s32[15,15,128]{2,1,0:T(8,128)} %count_ref.1) | copy-start | bytes 345604
  190.0 14.1 %all-to-all-start.11 = ((f32[128,1,128]{2,1,0:T(1,128)}), f32[128,1,128]{2,1,0:T(1,128)S(1)}, u32[]{:S(2)}, u32[]{:S(2)}) async-start(f32[128,1,128]{2,1,0:T(1,128)} %bitcast.35), calls=%async_computation.11 | async-start | bytes 131072 | tf_op jit(solution)/shard_map/all_to_all | solution.py:478
  194.7 1.6 copy-start
  196.3 1.4 copy-start.2
  197.7 0.7 copy-start.11

commit v4 on v3

--- a/solution.py
+++ b/solution.py
@@ -13,10 +13,14 @@
 EXT = 15
 PAD = 16
 CHUNK = 3
+TURN_STEP = 5
 NZ = 128
 DEVICES = 128
 X_LEFT = HALF - 1
 Y_LEFT = HALF
+HEAT_ROW = 8
+START_ROW = HEAT_ROW + PAD
+CARRY = START_ROW + PAD
 
 turn_angle = 130.0 * math.pi / 180.0
 excess_coupling = 1e-06
@@ -57,18 +61,24 @@
     return (full_planes(left) - 1) // 2
 
 
+def place_of(step):
+    return (X_LEFT, "bx") if step % 2 == 0 else (Y_LEFT, "by")
+
+
 def fold(values):
     return jnp.sum(values, axis=0, keepdims=True)
 
 
 def prep_kernel(
-    shift_hbm, v_hbm, count_hbm, flag_hbm, own_ref, uy_ref, uz_ref, low_ref, high_ref, base_ref,
-    shift_ref, v_ref, count_ref, flag_ref, sems, chunk_sems,
+    shift_hbm, parity_hbm, heat_hbm, v_hbm, count_hbm, flag_hbm, own_ref, uy_ref, uz_ref, low_ref, high_ref, base_ref,
+    shift_ref, parity_ref, heat_ref, v_ref, count_ref, flag_ref, sems, chunk_sems,
 ):
     fetches = [
         pltpu.make_async_copy(shift_hbm, shift_ref, sems.at[0]),
         pltpu.make_async_copy(count_hbm, count_ref, sems.at[1]),
         pltpu.make_async_copy(flag_hbm.at[0], flag_ref, sems.at[2]),
+        pltpu.make_async_copy(parity_hbm, parity_ref, sems.at[3]),
+        pltpu.make_async_copy(heat_hbm, heat_ref, sems.at[4]),
     ]
     chunks = [
         pltpu.make_async_copy(
@@ -116,7 +126,12 @@
         own_ref[2, i, 0:EXT, :] = pltpu.roll(flag_ref[i].astype(f32), shift, 1)
         uy_ref[i, 0:EXT, :] = pltpu.roll(mean[1], shift, 1)
         uz_ref[i, 0:EXT, :] = pltpu.roll(mean[2], shift, 1)
-    base_ref[...] = jnp.zeros((8, NZ), f32)
+    base_ref[...] = jnp.zeros((CARRY, NZ), f32)
+    for step in range(STEPS):
+        left, brick_axis = place_of(step)
+        start = lower_start(parity_ref, step, brick_axis, left)
+        base_ref[HEAT_ROW + step : HEAT_ROW + step + 1, :] = jnp.full((1, NZ), 3.0 * heat_ref[step], f32)
+        base_ref[START_ROW + step : START_ROW + step + 1, :] = jnp.full((1, NZ), start.astype(f32), f32)
     base_ref[0:1, :] = jnp.full((1, NZ), 1.0 / BIG, f32)
     base_ref[2:3, :] = fold(thermal)
     base_ref[4:5, :] = fold(energy_y)
@@ -126,24 +141,26 @@
         high_ref[field] = own_ref[field, EXT - 1]
 
 
-def prep(shifts, v, counts, flags):
+def prep(shifts, parity, heat, v, counts, flags):
     edge = shape(3, PAD, NZ)
     return pl.pallas_call(
         prep_kernel,
-        in_specs=[ANY] * 4,
+        in_specs=[ANY] * 6,
         out_specs=[VMEM] * 6,
-        out_shape=[shape(3, EXT, PAD, NZ), shape(PAD, PAD, NZ), shape(EXT, PAD, NZ), edge, edge, shape(8, NZ)],
+        out_shape=[shape(3, EXT, PAD, NZ), shape(PAD, PAD, NZ), shape(EXT, PAD, NZ), edge, edge, shape(CARRY, NZ)],
         scratch_shapes=[
             pltpu.SMEM((STEPS,), jnp.int32),
+            pltpu.SMEM((STEPS,), jnp.int32),
+            pltpu.SMEM((STEPS,), f32),
             pltpu.VMEM((3, SLOTS, EXT, EXT, NZ), f32),
             pltpu.VMEM((EXT, EXT, NZ), jnp.int32),
             pltpu.VMEM((EXT, EXT, NZ), jnp.int32),
-            pltpu.SemaphoreType.DMA((3,)),
+            pltpu.SemaphoreType.DMA((5,)),
             pltpu.SemaphoreType.DMA((EXT // CHUNK,)),
         ],
         compiler_params=GRANT,
         name="prep",
-    )(*[pltpu.with_memory_space_constraint(array, pltpu.HBM) for array in (shifts, v, counts, flags)])
+    )(*[pltpu.with_memory_space_constraint(array, pltpu.HBM) for array in (shifts, parity, heat, v, counts, flags)])
 
 
 def spread_kernel(shift_ref, own_ref, uy_ref, flag_ref, bits_ref, sy_ref, low_ref, high_ref, turn_ref):
@@ -238,7 +255,7 @@
         first_kernel,
         in_specs=[SMEM] + [VMEM] * 5,
         out_specs=[VMEM] * 5,
-        out_shape=[shape(DEVICES, NZ), shape(8, NZ), shape(2 + X_LEFT, EXT, PAD, NZ), edge, edge],
+        out_shape=[shape(DEVICES, NZ), shape(CARRY, NZ), shape(2 + X_LEFT, EXT, PAD, NZ), edge, edge],
         scratch_shapes=[pltpu.VMEM((EXT + 2, PAD, NZ), f32)] * 3,
         compiler_params=GRANT,
         name="first",
@@ -302,7 +319,7 @@
     )(parity, own, below, above)
 
 
-def next_scale(received_ref, carry_ref, heat_ref, step):
+def next_scale(received_ref, carry_ref, step):
     sums = jnp.sum(received_ref[...], axis=0, keepdims=True)
     scale = carry_ref[0:1, :]
     if step == 0:
@@ -314,22 +331,20 @@
         energy = jnp.sum(sums, axis=1, keepdims=True)
         total = carry_ref[1:2, :]
     speed = scale * jnp.sqrt(jnp.broadcast_to(energy, (1, NZ)))
-    factor = jnp.sqrt(3.0 * heat_ref[step] * total / (speed * speed + excess_coupling))
+    factor = jnp.sqrt(carry_ref[HEAT_ROW + step : HEAT_ROW + step + 1, :] * total / (speed * speed + excess_coupling))
     return jnp.minimum(scale * factor, SCALE_CAP), total
 
 
-def step_kernel(
-    parity_ref, heat_ref, received_ref, carry_ref, u_in_ref, weight_ref, mass_ref, u_ref, rows_ref, out_ref, *, step, left, brick_axis
-):
-    scale, total = next_scale(received_ref, carry_ref, heat_ref, step - 1)
-    start = lower_start(parity_ref, step, brick_axis, left)
+def step_kernel(received_ref, carry_ref, u_in_ref, weight_ref, mass_ref, u_ref, rows_ref, out_ref, *, step, left):
+    start = carry_ref[START_ROW + step : START_ROW + step + 1, :][0, 0].astype(jnp.int32)
+    scale, total = next_scale(received_ref, carry_ref, step - 1)
     wide = jnp.broadcast_to(scale, (PAD, NZ))
     turn = left - (STEPS + 1 - step) // 2
-    for k in range(full_planes(left)):
-        u_ref[k] = u_in_ref[k]
+    u_ref[0] = u_in_ref[0]
+    u_ref[full_planes(left) - 1] = u_in_ref[full_planes(left) - 1]
     for k in range(pair_count(left)):
         plane = start + 2 * k
-        low, high = u_ref[plane], u_ref[plane + 1]
+        low, high = u_in_ref[plane], u_in_ref[plane + 1]
         closing = jnp.maximum(low - high, 0.0)
         push = closing * jnp.tanh(wide * closing)
         u_ref[plane] = low - weight_ref[turn, 0, k] * push
@@ -348,20 +363,20 @@
     rows_ref[...] = jnp.broadcast_to(carry_ref[2:3, :] + mine + other, (DEVICES, NZ))
 
 
-def collide(step, parity, heat, received, carry, u, weight, mass):
-    left, brick_axis = (X_LEFT, "bx") if step % 2 == 0 else (Y_LEFT, "by")
+def collide(step, received, carry, u, weight, mass):
+    left, _ = place_of(step)
 
     def body(*refs):
-        step_kernel(*refs, step=step, left=left, brick_axis=brick_axis)
+        step_kernel(*refs, step=step, left=left)
 
     return pl.pallas_call(
         body,
-        in_specs=[SMEM] * 2 + [VMEM] * 5,
+        in_specs=[VMEM] * 5,
         out_specs=[VMEM] * 3,
-        out_shape=[shape(full_planes(left), PAD, NZ), shape(DEVICES, NZ), shape(8, NZ)],
+        out_shape=[shape(full_planes(left), PAD, NZ), shape(DEVICES, NZ), shape(CARRY, NZ)],
         compiler_params=GRANT,
         name="collide",
-    )(parity, heat, received, carry, u, weight, mass)
+    )(received, carry, u, weight, mass)
 
 
 def turn_kernel(shift_ref, v_ref, count_ref, spin_ref, w_ref):
@@ -428,9 +443,9 @@
     )(shifts, v, counts, spin)
 
 
-def finish_kernel(heat_ref, received_ref, carry_ref, ux_ref, uy_ref, uz_ref, own_ref, w_ref, v_ref):
+def finish_kernel(received_ref, carry_ref, ux_ref, uy_ref, uz_ref, own_ref, w_ref, v_ref):
     member = pl.program_id(0)
-    scale, _ = next_scale(received_ref, carry_ref, heat_ref, STEPS - 1)
+    scale, _ = next_scale(received_ref, carry_ref, STEPS - 1)
     wide = jnp.broadcast_to(scale, (EXT, NZ))
 
     def write(mean_of):
@@ -453,18 +468,18 @@
         write(lambda i: uz_ref[i, 0:EXT, :])
 
 
-def finish(heat, received, carry, ux, uy, uz, own, w):
+def finish(received, carry, ux, uy, uz, own, w):
     part = pl.BlockSpec((1, SLOTS, EXT, EXT, NZ), lambda c: (c, 0, 0, 0, 0))
     mass = pl.BlockSpec((1, EXT, PAD, NZ), lambda c: (1, 0, 0, 0))
     return pl.pallas_call(
         finish_kernel,
         grid=(3,),
-        in_specs=[SMEM] + [VMEM] * 5 + [mass, part],
+        in_specs=[VMEM] * 5 + [mass, part],
         out_specs=part,
         out_shape=shape(3, SLOTS, EXT, EXT, NZ),
         compiler_params=GRANT,
         name="finish",
-    )(heat, received, carry, ux, uy.reshape(full_planes(Y_LEFT) * PAD, NZ), uz, own, w)
+    )(received, carry, ux, uy.reshape(full_planes(Y_LEFT) * PAD, NZ), uz, own, w)
 
 
 def exchange(low_edge, high_edge, axis):
@@ -479,23 +494,26 @@
 
 
 def per_device(v, counts, spin, flags, parity, shifts, heat):
-    own, uy, uz, low, high, carry = prep(shifts, v, counts, flags)
+    own, uy, uz, low, high, carry = prep(shifts, parity, heat, v, counts, flags)
     above, below = exchange(low, high, "bx")
     bits, sy, ylo, yhi = spread(shifts, own, uy, flags)
     y_above, y_below = exchange(ylo, yhi, "by")
     rows, carry, sx, xlo, xhi = first(parity, own, bits, below, above, carry)
     received = sum_over_devices(rows)
     x_above, x_below = exchange(xlo, xhi, "bx")
-    w = turn(shifts, v, counts, spin)
     uy, y_weights, y_mass = join(parity, sy, y_below, y_above, Y_LEFT, "by")
     ux, x_weights, x_mass = join(parity, sx, x_below, x_above, X_LEFT, "bx")
     for step in range(1, STEPS):
         if step % 2 == 0:
-            ux, rows, carry = collide(step, parity, heat, received, carry, ux, x_weights, x_mass)
+            ux, rows, carry = collide(step, received, carry, ux, x_weights, x_mass)
         else:
-            uy, rows, carry = collide(step, parity, heat, received, carry, uy, y_weights, y_mass)
+            uy, rows, carry = collide(step, received, carry, uy, y_weights, y_mass)
         received = sum_over_devices(rows)
-    return finish(heat, received, carry, ux, uy, uz, own, w)
+        if step == TURN_STEP:
+            received, shifts = lax.optimization_barrier((received, shifts))
+            w = turn(shifts, v, counts, spin)
+            received, w = lax.optimization_barrier((received, w))
+    return finish(received, carry, ux, uy, uz, own, w)
 
 
 def solution(mesh):

time: 207 us -> 203 us (0.981)
  blocking collectives: 125 us -> 138 us
  Pallas kernels: 22.9 us -> 15.4 us
  starting transfers between devices: 32.4 us -> 27.8 us
  local copies, waits for them, and re-layouts: 7.34 us -> 3.69 us
  waiting for transfers between devices: 19.3 us -> 17.1 us
    all_to_all x9 -> x10, blocking collectives: 125 us -> 138 us  [sum_over_devices(): return lax.all_to_all(rows, ('bx', 'by'), 0, 0, tiled=True)]
    pallas_call x13, Pallas kernels: 14.6 us -> 7.16 us  [the longest x11 2.72 us: collide(): pl.pallas_call(body, in_specs=[VMEM] * 5, out_specs=[VMEM] * 3, out_shape...]
    all_to_all x3 -> x2, starting transfers between devices: 19.1 us -> 14.4 us  [sum_over_devices(): return lax.all_to_all(rows, ('bx', 'by'), 0, 0, tiled=True)]
    unnamed x24 -> x20, local copies, waits for them, and re-layouts: 7.34 us -> 3.69 us
    all_to_all x3 -> x2, waiting for transfers between devices: 17.3 us -> 15.1 us  [sum_over_devices(): return lax.all_to_all(rows, ('bx', 'by'), 0, 0, tiled=True)]
  transfers between devices with their start and end apart: 9 -> 8, of which waited for: 5 -> 4; matrix products, arithmetic and copies ran while one was open for 0% -> 0% of each run, Pallas kernels for 4% -> 2%
where the time goes in v4:
time: 203 us
  blocking collectives  138 us (68%)
  starting transfers between devices  27.8 us (14%)
  waiting for transfers between devices  17.1 us (8%)
  Pallas kernels  15.4 us (8%)
  local copies, waits for them, and re-layouts  3.69 us (2%)
    all_to_all x10, blocking collectives, sum_over_devices(): return lax.all_to_all(rows, ('bx', 'by'), 0, 0, tiled=True)  138 us
    all_to_all x2, waiting for transfers between devices, sum_over_devices(): return lax.all_to_all(rows, ('bx', 'by'), 0, 0, tiled=True)  15.1 us
    all_to_all x2, starting transfers between devices, sum_over_devices(): return lax.all_to_all(rows, ('bx', 'by'), 0, 0, tiled=True)  14.4 us
    ppermute x3, starting transfers between devices, exchange(): lax.ppermute(high_edge, axis, up)  7.97 us
    ppermute x3, starting transfers between devices, exchange(): lax.ppermute(low_edge, axis, down)  5.39 us
  transfers between devices with their start and end apart: 8, of which 4 were waited for; matrix products, arithmetic and copies ran while one was open for 0% of the time, Pallas kernels for 2%

profile of v4, /device:TPU:1, one launch (start us, length us, event | category | flops | bytes accessed | tf_op | source)
XLA Modules:
  0.0 202.6 jit_solution(4416735865966869770)
XLA Ops:
  0.0 2.3 %prep.1 = (f32[3,15,16,128]{3,2,1,0:T(8,128)S(1)}, f32[16,16,128]{2,1,0:T(8,128)S(1)}, f32[15,16,128]{2,1,0:T(8,128)S(1)}, f32[3,16,128]{2,1,0:T(8,128)S(1)}, f3...) custom-call(s32[12]{0:T(128)} %shift_ref.2, s32[12]{0:T(128)} %refs_0_.3, f32[12]{0:T(128)} %heat_hbm.1, ...), custom_call_target="tpu_custom_call" | custom-call | tf_op jit(solution)/shard_map/prep/pallas_call | solution.py:146
  2.3 1.1 spread.1
  3.4 3.1 %collective-permute-start.2 = (f32[33,16,128]{2,1,0:T(8,128)S(1)}, f32[33,16,128]{2,1,0:T(8,128)S(1)}, u32[]{:S(2)}, u32[]{:S(2)}) collective-permute-start(f32[33,16,128]{2,1,0:T(8,128)S(1)} %get-tuple-element.72), channel_id=1, source_target_pairs={{0,1},{1,2},{2,3},{3,4},{4,5},{5,6},{6,7},{7,8},{8,9},{9,10},{10,1... | collective-permute-start | bytes 811016 | tf_op jit(solution)/shard_map/ppermute | solution.py:489
  6.5 2.7 %collective-permute-start = (f32[3,16,128]{2,1,0:T(8,128)S(1)}, f32[3,16,128]{2,1,0:T(8,128)S(1)}, u32[]{:S(2)}, u32[]{:S(2)}) collective-permute-start(f32[3,16,128]{2,1,0:T(8,128)S(1)} %get-tuple-element.66), channel_id=1, source_target_pairs={{0,16},{16,32},{32,48},{48,64},{64,80},{80,96},{96,112},{112,0},{1... | collective-permute-start | bytes 73736 | tf_op jit(solution)/shard_map/ppermute | solution.py:489
  9.3 2.5 %collective-permute-start.1 = (f32[3,16,128]{2,1,0:T(8,128)S(1)}, f32[3,16,128]{2,1,0:T(8,128)S(1)}, u32[]{:S(2)}, u32[]{:S(2)}) collective-permute-start(f32[3,16,128]{2,1,0:T(8,128)S(1)} %get-tuple-element.67), channel_id=1, source_target_pairs={{0,112},{16,0},{32,16},{48,32},{64,48},{80,64},{96,80},{112,96},{1... | collective-permute-start | bytes 73736 | tf_op jit(solution)/shard_map/ppermute | solution.py:489
  11.7 1.2 collective-permute-done.below_ref
  12.9 0.8 collective-permute-done.1.above_ref
  13.7 1.5 first.1
  15.2 0.9 copy-done.3
  16.1 2.1 %collective-permute-start.4 = (f32[25,16,128]{2,1,0:T(8,128)}, f32[25,16,128]{2,1,0:T(8,128)}, u32[]{:S(2)}, u32[]{:S(2)}) collective-permute-start(f32[25,16,128]{2,1,0:T(8,128)} %get-tuple-element.80), channel_id=1, source_target_pairs={{0,16},{16,32},{32,48},{48,64},{64,80},{80,96},{96,112},{112,0},{1... | collective-permute-start | bytes 614408 | tf_op jit(solution)/shard_map/ppermute | solution.py:489
  18.2 2.9 %collective-permute-start.5 = (f32[25,16,128]{2,1,0:T(8,128)}, f32[25,16,128]{2,1,0:T(8,128)}, u32[]{:S(2)}, u32[]{:S(2)}) collective-permute-start(f32[25,16,128]{2,1,0:T(8,128)} %get-tuple-element.81), channel_id=1, source_target_pairs={{0,112},{16,0},{32,16},{48,32},{64,48},{80,64},{96,80},{112,96},{1... | collective-permute-start | bytes 614408 | tf_op jit(solution)/shard_map/ppermute | solution.py:489
  21.2 9.8 %all-to-all-start = ((f32[128,1,128]{2,1,0:T(1,128)}), f32[128,1,128]{2,1,0:T(1,128)S(1)}, u32[]{:S(2)}, u32[]{:S(2)}) async-start(f32[128,1,128]{2,1,0:T(1,128)} %bitcast.2), calls=%async_computation | async-start | bytes 131072 | tf_op jit(solution)/shard_map/all_to_all | solution.py:493
  31.0 0.8 join.2
  32.5 8.0 %all-to-all-done = f32[128,1,128]{2,1,0:T(1,128)S(1)} async-done(((f32[128,1,128]{2,1,0:T(1,128)}), f32[128,1,128]{2,1,0:T(1,128)S(1)}, u32[]{:S(2)}, u32[]{:S(2)}) %all-to-all-start) | async-done | bytes 65568 | tf_op jit(solution)/shard_map/all_to_all | solution.py:493
  40.6 0.9 copy-done.7
  41.5 0.8 collide.11
  42.3 4.6 %all-to-all-start.1 = ((f32[128,1,128]{2,1,0:T(1,128)}), f32[128,1,128]{2,1,0:T(1,128)S(1)}, u32[]{:S(2)}, u32[]{:S(2)}) async-start(f32[128,1,128]{2,1,0:T(1,128)} %bitcast.5), calls=%async_computation.1 | async-start | bytes 131072 | tf_op jit(solution)/shard_map/all_to_all | solution.py:493
  46.9 1.1 copy-done.4
  48.1 1.3 join.3
  49.4 7.0 %all-to-all-done.1 = f32[128,1,128]{2,1,0:T(1,128)S(1)} async-done(((f32[128,1,128]{2,1,0:T(1,128)}), f32[128,1,128]{2,1,0:T(1,128)S(1)}, u32[]{:S(2)}, u32[]{:S(2)}) %all-to-all-start.1) | async-done | bytes 65568 | tf_op jit(solution)/shard_map/all_to_all | solution.py:493
  56.6 13.8 %all_to_all.133 = f32[128,1,128]{2,1,0:T(1,128)S(1)} all-to-all(f32[128,1,128]{2,1,0:T(1,128)S(1)} %bitcast.66), channel_id=1, replica_groups=mesh['bx'=8,'by'=16] {'bx','by'}, dimensions={0} | all-to-all | bytes 131072 | tf_op jit(solution)/shard_map/all_to_all | solution.py:493
  70.6 13.8 %all_to_all.134 = f32[128,1,128]{2,1,0:T(1,128)S(1)} all-to-all(f32[128,1,128]{2,1,0:T(1,128)S(1)} %bitcast.67), channel_id=1, replica_groups=mesh['bx'=8,'by'=16] {'bx','by'}, dimensions={0} | all-to-all | bytes 131072 | tf_op jit(solution)/shard_map/all_to_all | solution.py:493
  84.7 13.8 %all_to_all.135 = f32[128,1,128]{2,1,0:T(1,128)S(1)} all-to-all(f32[128,1,128]{2,1,0:T(1,128)S(1)} %bitcast.68), channel_id=1, replica_groups=mesh['bx'=8,'by'=16] {'bx','by'}, dimensions={0} | all-to-all | bytes 131072 | tf_op jit(solution)/shard_map/all_to_all | solution.py:493
  98.7 13.8 %all_to_all.136 = f32[128,1,128]{2,1,0:T(1,128)S(1)} all-to-all(f32[128,1,128]{2,1,0:T(1,128)S(1)} %bitcast.69), channel_id=1, replica_groups=mesh['bx'=8,'by'=16] {'bx','by'}, dimensions={0} | all-to-all | bytes 131072 | tf_op jit(solution)/shard_map/all_to_all | solution.py:493
  112.6 3.6 %turn.1.w_ref = f32[3,6,15,15,128]{4,3,2,1,0:T(8,128)S(1)} custom-call(s32[12]{0:T(128)S(1)} %copy-done.9, f32[3,6,15,15,128]{4,3,2,1,0:T(8,128)S(1)} %copy-done, s32[15,15,128]{2,1,0:T(8,128)S(1)} %copy-done.5, s32[12,15,15,128]{3,2,1,0:T(8,128)S(1)} %copy-done.2), custom_call_target="tpu_custom_call" | custom-call | tf_op jit(solution)/shard_map/turn/pallas_call | solution.py:436
  116.3 13.8 %all_to_all.137 = f32[128,1,128]{2,1,0:T(1,128)S(1)} all-to-all(f32[128,1,128]{2,1,0:T(1,128)S(1)} %bitcast.70), channel_id=1, replica_groups=mesh['bx'=8,'by'=16] {'bx','by'}, dimensions={0} | all-to-all | bytes 131072 | tf_op jit(solution)/shard_map/all_to_all | solution.py:493
  130.4 13.8 %all_to_all.138 = f32[128,1,128]{2,1,0:T(1,128)S(1)} all-to-all(f32[128,1,128]{2,1,0:T(1,128)S(1)} %bitcast.71), channel_id=1, replica_groups=mesh['bx'=8,'by'=16] {'bx','by'}, dimensions={0} | all-to-all | bytes 131072 | tf_op jit(solution)/shard_map/all_to_all | solution.py:493
  144.4 13.8 %all_to_all.139 = f32[128,1,128]{2,1,0:T(1,128)S(1)} all-to-all(f32[128,1,128]{2,1,0:T(1,128)S(1)} %bitcast.72), channel_id=1, replica_groups=mesh['bx'=8,'by'=16] {'bx','by'}, dimensions={0} | all-to-all | bytes 131072 | tf_op jit(solution)/shard_map/all_to_all | solution.py:493
  158.5 13.8 %all_to_all.140 = f32[128,1,128]{2,1,0:T(1,128)S(1)} all-to-all(f32[128,1,128]{2,1,0:T(1,128)S(1)} %bitcast.73), channel_id=1, replica_groups=mesh['bx'=8,'by'=16] {'bx','by'}, dimensions={0} | all-to-all | bytes 131072 | tf_op jit(solution)/shard_map/all_to_all | solution.py:493
  172.5 13.8 %all_to_all.141 = f32[128,1,128]{2,1,0:T(1,128)S(1)} all-to-all(f32[128,1,128]{2,1,0:T(1,128)S(1)} %bitcast.64), channel_id=1, replica_groups=mesh['bx'=8,'by'=16] {'bx','by'}, dimensions={0} | all-to-all | bytes 131072 | tf_op jit(solution)/shard_map/all_to_all | solution.py:493
  186.6 13.8 %all_to_all.142 = f32[128,1,128]{2,1,0:T(1,128)S(1)} all-to-all(f32[128,1,128]{2,1,0:T(1,128)S(1)} %bitcast.65), channel_id=1, replica_groups=mesh['bx'=8,'by'=16] {'bx','by'}, dimensions={0} | all-to-all | bytes 131072 | tf_op jit(solution)/shard_map/all_to_all | solution.py:493
  200.4 2.2 %finish.1 = f32[3,6,15,15,128]{4,3,2,1,0:T(8,128)} custom-call(f32[128,128]{1,0:T(8,128)S(1)} %bitcast.50, f32[40,128]{1,0:T(8,128)S(1)} %get-tuple-element.116.carry_ref, f32[25,16,128]{2,1,0:T(8,128)S(1)} %get-tuple-element.117.ux_ref, f32[432,128]{1,0:T(8,128)S(1)} %bitcast.62, f32[15,16,128]{2,1,0:T(8,128)S(1)} %get-tuple-element.119.uz_ref, ...), custom_call_target="tpu_custom_call" | custom-call | tf_op jit(solution)/shard_map/finish/pallas_call | solution.py:474
  (32 shorter events, 2.6 us)
Async XLA Ops:
  0.0 13.7 %copy-start.8 = (s32[12]{0:T(128)S(1)}, s32[12]{0:T(128)}, u32[]{:S(2)}) copy-start(s32[12]{0:T(128)} %refs_0_.3) | copy-start | bytes 148
  0.0 2.3 %copy-start.9 = (s32[12]{0:T(128)S(1)}, s32[12]{0:T(128)}, u32[]{:S(2)}) copy-start(s32[12]{0:T(128)} %shift_ref.2) | copy-start | bytes 148
  0.0 2.3 %copy-start.1 = (s32[12,15,15,128]{3,2,1,0:T(8,128)S(1)}, s32[12,15,15,128]{3,2,1,0:T(8,128)}, u32[]{:S(2)}) copy-start(s32[12,15,15,128]{3,2,1,0:T(8,128)} %flag_ref.1) | copy-start | bytes 4147204
  3.4 27.6 %collective-permute-start.2 = (f32[33,16,128]{2,1,0:T(8,128)S(1)}, f32[33,16,128]{2,1,0:T(8,128)S(1)}, u32[]{:S(2)}, u32[]{:S(2)}) collective-permute-start(f32[33,16,128]{2,1,0:T(8,128)S(1)} %get-tuple-element.72), channel_id=1, source_target_pairs={{0,1},{1,2},{2,3},{3,4},{4,5},{5,6},{6,7},{7,8},{8,9},{9,10},{10,1... | collective-permute-start | bytes 811016 | tf_op jit(solution)/shard_map/ppermute | solution.py:489
  6.5 24.5 %collective-permute-start.3 = (f32[33,16,128]{2,1,0:T(8,128)S(1)}, f32[33,16,128]{2,1,0:T(8,128)S(1)}, u32[]{:S(2)}, u32[]{:S(2)}) collective-permute-start(f32[33,16,128]{2,1,0:T(8,128)S(1)} %get-tuple-element.73), channel_id=1, source_target_pairs={{0,15},{1,0},{2,1},{3,2},{4,3},{5,4},{6,5},{7,6},{8,7},{9,8},{10,9... | collective-permute-start | bytes 811016 | tf_op jit(solution)/shard_map/ppermute | solution.py:489
  6.5 6.4 %collective-permute-start = (f32[3,16,128]{2,1,0:T(8,128)S(1)}, f32[3,16,128]{2,1,0:T(8,128)S(1)}, u32[]{:S(2)}, u32[]{:S(2)}) collective-permute-start(f32[3,16,128]{2,1,0:T(8,128)S(1)} %get-tuple-element.66), channel_id=1, source_target_pairs={{0,16},{16,32},{32,48},{48,64},{64,80},{80,96},{96,112},{112,0},{1... | collective-permute-start | bytes 73736 | tf_op jit(solution)/shard_map/ppermute | solution.py:489
  9.3 4.4 %collective-permute-start.1 = (f32[3,16,128]{2,1,0:T(8,128)S(1)}, f32[3,16,128]{2,1,0:T(8,128)S(1)}, u32[]{:S(2)}, u32[]{:S(2)}) collective-permute-start(f32[3,16,128]{2,1,0:T(8,128)S(1)} %get-tuple-element.67), channel_id=1, source_target_pairs={{0,112},{16,0},{32,16},{48,32},{64,48},{80,64},{96,80},{112,96},{1... | collective-permute-start | bytes 73736 | tf_op jit(solution)/shard_map/ppermute | solution.py:489
  15.2 0.9 copy-start.3
  16.1 30.8 %collective-permute-start.4 = (f32[25,16,128]{2,1,0:T(8,128)}, f32[25,16,128]{2,1,0:T(8,128)}, u32[]{:S(2)}, u32[]{:S(2)}) collective-permute-start(f32[25,16,128]{2,1,0:T(8,128)} %get-tuple-element.80), channel_id=1, source_target_pairs={{0,16},{16,32},{32,48},{48,64},{64,80},{80,96},{96,112},{112,0},{1... | collective-permute-start | bytes 614408 | tf_op jit(solution)/shard_map/ppermute | solution.py:489
  18.2 28.7 %collective-permute-start.5 = (f32[25,16,128]{2,1,0:T(8,128)}, f32[25,16,128]{2,1,0:T(8,128)}, u32[]{:S(2)}, u32[]{:S(2)}) collective-permute-start(f32[25,16,128]{2,1,0:T(8,128)} %get-tuple-element.81), channel_id=1, source_target_pairs={{0,112},{16,0},{32,16},{48,32},{64,48},{80,64},{96,80},{112,96},{1... | collective-permute-start | bytes 614408 | tf_op jit(solution)/shard_map/ppermute | solution.py:489
  21.2 19.4 %all-to-all-start = ((f32[128,1,128]{2,1,0:T(1,128)}), f32[128,1,128]{2,1,0:T(1,128)S(1)}, u32[]{:S(2)}, u32[]{:S(2)}) async-start(f32[128,1,128]{2,1,0:T(1,128)} %bitcast.2), calls=%async_computation | async-start | bytes 131072 | tf_op jit(solution)/shard_map/all_to_all | solution.py:493
  31.8 0.7 copy-start.6
  40.6 0.9 copy-start.7
  42.3 14.1 %all-to-all-start.1 = ((f32[128,1,128]{2,1,0:T(1,128)}), f32[128,1,128]{2,1,0:T(1,128)S(1)}, u32[]{:S(2)}, u32[]{:S(2)}) async-start(f32[128,1,128]{2,1,0:T(1,128)} %bitcast.5), calls=%async_computation.1 | async-start | bytes 131072 | tf_op jit(solution)/shard_map/all_to_all | solution.py:493
  46.9 1.2 copy-start.4
  70.4 42.1 %copy-start = (f32[3,6,15,15,128]{4,3,2,1,0:T(8,128)S(1)}, f32[3,6,15,15,128]{4,3,2,1,0:T(8,128)}, u32[]{:S(2)}) copy-start(f32[3,6,15,15,128]{4,3,2,1,0:T(8,128)} %v_ref.1) | copy-start | bytes 6220804
  70.4 42.1 %copy-start.2 = (s32[12,15,15,128]{3,2,1,0:T(8,128)S(1)}, s32[12,15,15,128]{3,2,1,0:T(8,128)}, u32[]{:S(2)}) copy-start(s32[12,15,15,128]{3,2,1,0:T(8,128)} %spin_ref.1) | copy-start | bytes 4147204
  70.4 42.1 %copy-start.5 = (s32[15,15,128]{2,1,0:T(8,128)S(1)}, s32[15,15,128]{2,1,0:T(8,128)}, u32[]{:S(2)}) copy-start(s32[15,15,128]{2,1,0:T(8,128)} %count_ref.1) | copy-start | bytes 345604

commit v5 on v4

--- a/solution.py
+++ b/solution.py
@@ -20,7 +20,8 @@
 Y_LEFT = HALF
 HEAT_ROW = 8
 START_ROW = HEAT_ROW + PAD
-CARRY = START_ROW + PAD
+SHIFT_ROW = START_ROW + PAD
+CARRY = SHIFT_ROW + PAD
 
 turn_angle = 130.0 * math.pi / 180.0
 excess_coupling = 1e-06
@@ -61,6 +62,10 @@
     return (full_planes(left) - 1) // 2
 
 
+def whole(carry_ref, row):
+    return carry_ref[row : row + 1, :][0, 0].astype(jnp.int32)
+
+
 def place_of(step):
     return (X_LEFT, "bx") if step % 2 == 0 else (Y_LEFT, "by")
 
@@ -70,7 +75,8 @@
 
 
 def prep_kernel(
-    shift_hbm, parity_hbm, heat_hbm, v_hbm, count_hbm, flag_hbm, own_ref, uy_ref, uz_ref, low_ref, high_ref, base_ref,
+    shift_hbm, parity_hbm, heat_hbm, v_hbm, count_hbm, flag_hbm,
+    ux_ref, mass_ref, allow_ref, uy_ref, uz_ref, low_ref, high_ref, base_ref,
     shift_ref, parity_ref, heat_ref, v_ref, count_ref, flag_ref, sems, chunk_sems,
 ):
     fetches = [
@@ -92,9 +98,7 @@
         fetch.wait()
     shift = later_shifts(shift_ref, 0)
     zero_row = jnp.zeros((EXT, 1, NZ), f32)
-    for field in range(3):
-        own_ref[field, :, EXT:PAD, :] = zero_row
-    for array_ref in (uy_ref, uz_ref):
+    for array_ref in (ux_ref, mass_ref, allow_ref, uy_ref, uz_ref):
         array_ref[0:EXT, EXT:PAD, :] = zero_row
     uy_ref[EXT] = jnp.zeros((PAD, NZ), f32)
 
@@ -121,9 +125,9 @@
         thermal = thermal + mass * mean[2] * mean[2]
         energy_y = energy_y + mass * mean[1] * mean[1]
         total = total + mass
-        own_ref[0, i, 0:EXT, :] = pltpu.roll(mean[0], shift, 1)
-        own_ref[1, i, 0:EXT, :] = pltpu.roll(mass, shift, 1)
-        own_ref[2, i, 0:EXT, :] = pltpu.roll(flag_ref[i].astype(f32), shift, 1)
+        ux_ref[i, 0:EXT, :] = pltpu.roll(mean[0], shift, 1)
+        mass_ref[i, 0:EXT, :] = pltpu.roll(mass, shift, 1)
+        allow_ref[i, 0:EXT, :] = pltpu.roll(flag_ref[i].astype(f32), shift, 1)
         uy_ref[i, 0:EXT, :] = pltpu.roll(mean[1], shift, 1)
         uz_ref[i, 0:EXT, :] = pltpu.roll(mean[2], shift, 1)
     base_ref[...] = jnp.zeros((CARRY, NZ), f32)
@@ -132,13 +136,15 @@
         start = lower_start(parity_ref, step, brick_axis, left)
         base_ref[HEAT_ROW + step : HEAT_ROW + step + 1, :] = jnp.full((1, NZ), 3.0 * heat_ref[step], f32)
         base_ref[START_ROW + step : START_ROW + step + 1, :] = jnp.full((1, NZ), start.astype(f32), f32)
+        later = later_shifts(shift_ref, step)
+        base_ref[SHIFT_ROW + step : SHIFT_ROW + step + 1, :] = jnp.full((1, NZ), later.astype(f32), f32)
     base_ref[0:1, :] = jnp.full((1, NZ), 1.0 / BIG, f32)
     base_ref[2:3, :] = fold(thermal)
     base_ref[4:5, :] = fold(energy_y)
     base_ref[5:6, :] = fold(total)
-    for field in range(3):
-        low_ref[field] = own_ref[field, 0]
-        high_ref[field] = own_ref[field, EXT - 1]
+    for field, array_ref in enumerate((ux_ref, mass_ref, allow_ref)):
+        low_ref[field] = array_ref[0]
+        high_ref[field] = array_ref[EXT - 1]
 
 
 def prep(shifts, parity, heat, v, counts, flags):
@@ -146,8 +152,8 @@
     return pl.pallas_call(
         prep_kernel,
         in_specs=[ANY] * 6,
-        out_specs=[VMEM] * 6,
-        out_shape=[shape(3, EXT, PAD, NZ), shape(PAD, PAD, NZ), shape(EXT, PAD, NZ), edge, edge, shape(CARRY, NZ)],
+        out_specs=[VMEM] * 8,
+        out_shape=[shape(EXT, PAD, NZ)] * 3 + [shape(PAD, PAD, NZ), shape(EXT, PAD, NZ), edge, edge, shape(CARRY, NZ)],
         scratch_shapes=[
             pltpu.SMEM((STEPS,), jnp.int32),
             pltpu.SMEM((STEPS,), jnp.int32),
@@ -163,10 +169,10 @@
     )(*[pltpu.with_memory_space_constraint(array, pltpu.HBM) for array in (shifts, parity, heat, v, counts, flags)])
 
 
-def spread_kernel(shift_ref, own_ref, uy_ref, flag_ref, bits_ref, sy_ref, low_ref, high_ref, turn_ref):
+def spread_kernel(carry_ref, mass_ref, uy_ref, flag_ref, bits_ref, own_ref, y_mass_ref, y_bits_ref, low_ref, high_ref, turn_ref):
     bits_ref[:, :, EXT:PAD, :] = jnp.zeros((X_LEFT, EXT, 1, NZ), f32)
     for step in range(1, STEPS):
-        later = later_shifts(shift_ref, step)
+        later = whole(carry_ref, SHIFT_ROW + step)
         for i in range(EXT):
             bits = pltpu.roll(flag_ref[step, i].astype(f32), later, 1)
             if step % 2 == 0:
@@ -175,31 +181,34 @@
                 turn_ref[step // 2, i * PAD : i * PAD + EXT, :] = bits
     keep = lax.broadcasted_iota(jnp.int32, (PAD, NZ), 0) < EXT
     for i in range(EXT):
-        turn_ref[HALF, i * PAD : (i + 1) * PAD, :] = own_ref[1, i]
-    for field in range(2 + Y_LEFT):
+        turn_ref[HALF, i * PAD : (i + 1) * PAD, :] = mass_ref[i]
+    for field, (place, planes) in enumerate(edge_layout(Y_LEFT)[0]):
         for y in range(EXT):
+            line = pl.ds(y, PAD, stride=PAD)
             if field == 0:
-                rows = uy_ref[pl.ds(y, PAD, stride=PAD), :]
+                rows = own_ref[y] = jnp.where(keep, uy_ref[line, :], 0.0)
+            elif field == 1:
+                rows = y_mass_ref[y] = jnp.where(keep, turn_ref[HALF, line, :], 0.0)
             else:
-                rows = turn_ref[HALF if field == 1 else field - 2, pl.ds(y, PAD, stride=PAD), :]
-            sy_ref[field, y] = jnp.where(keep, rows, 0.0)
-    for field, (place, planes) in enumerate(edge_layout(Y_LEFT)[0]):
-        for k in range(planes):
-            low_ref[place + k] = sy_ref[field, k]
-            high_ref[place + k] = sy_ref[field, EXT - planes + k]
-
-
-def spread(shifts, own, uy, flags):
+                rows = y_bits_ref[field - 2, y] = jnp.where(keep, turn_ref[field - 2, line, :], 0.0)
+            if y < planes:
+                low_ref[place + y] = rows
+            if y >= EXT - planes:
+                high_ref[place + y - (EXT - planes)] = rows
+
+
+def spread(carry, mass, uy, flags):
     edge = shape(edge_layout(Y_LEFT)[1], PAD, NZ)
+    plane = shape(EXT, PAD, NZ)
     return pl.pallas_call(
         spread_kernel,
-        in_specs=[SMEM, VMEM, VMEM, VMEM],
-        out_specs=[VMEM] * 4,
-        out_shape=[shape(X_LEFT, EXT, PAD, NZ), shape(2 + Y_LEFT, EXT, PAD, NZ), edge, edge],
+        in_specs=[VMEM] * 4,
+        out_specs=[VMEM] * 6,
+        out_shape=[shape(X_LEFT, EXT, PAD, NZ), plane, plane, shape(Y_LEFT, EXT, PAD, NZ), edge, edge],
         scratch_shapes=[pltpu.VMEM((HALF + 1, PAD * PAD, NZ), f32)],
         compiler_params=GRANT,
         name="spread",
-    )(shifts, own, uy.reshape(PAD * PAD, NZ), flags)
+    )(carry, mass, uy.reshape(PAD * PAD, NZ), flags)
 
 
 def lower_start(parity_ref, step, brick_axis, halo):
@@ -207,15 +216,17 @@
 
 
 def first_kernel(
-    parity_ref, own_ref, bits_ref, below_ref, above_ref, carry_ref,
-    rows_ref, out_ref, sx_ref, xlo_ref, xhi_ref, u_ref, mass_ref, allow_ref,
+    carry_ref, own_ref, own_mass_ref, own_allow_ref, bits_ref, below_ref, above_ref,
+    rows_ref, out_ref, next_ref, xlo_ref, xhi_ref, u_ref, mass_ref, allow_ref,
 ):
-    for field, array_ref in enumerate((u_ref, mass_ref, allow_ref)):
-        array_ref[0] = below_ref[field]
-        array_ref[EXT + 1] = above_ref[field]
+    for field, (all_ref, mine_ref) in enumerate(
+        ((u_ref, own_ref), (mass_ref, own_mass_ref), (allow_ref, own_allow_ref))
+    ):
+        all_ref[0] = below_ref[field]
+        all_ref[EXT + 1] = above_ref[field]
         for k in range(EXT):
-            array_ref[1 + k] = own_ref[field, k]
-    start = lower_start(parity_ref, 0, "bx", 1)
+            all_ref[1 + k] = mine_ref[k]
+    start = whole(carry_ref, START_ROW)
     wide = jnp.broadcast_to(carry_ref[0:1, :], (PAD, NZ))
     for k in range((EXT + 1) // 2):
         plane = start + 2 * k
@@ -229,15 +240,17 @@
     energy = jnp.zeros((PAD, NZ), f32)
     for k in range(EXT):
         u = u_ref[1 + k]
-        energy = energy + own_ref[1, k] * u * u
-        sx_ref[0, k] = u
-        sx_ref[1, k] = own_ref[1, k]
-        for j in range(X_LEFT):
-            sx_ref[2 + j, k] = bits_ref[j, k]
+        energy = energy + own_mass_ref[k] * u * u
+        next_ref[k] = u
     for field, (place, planes) in enumerate(edge_layout(X_LEFT)[0]):
         for k in range(planes):
-            xlo_ref[place + k] = sx_ref[field, k]
-            xhi_ref[place + k] = sx_ref[field, EXT - planes + k]
+            for edge_ref, plane in ((xlo_ref, k), (xhi_ref, EXT - planes + k)):
+                if field == 0:
+                    edge_ref[place + k] = next_ref[plane]
+                elif field == 1:
+                    edge_ref[place + k] = own_mass_ref[plane]
+                else:
+                    edge_ref[place + k] = bits_ref[field - 2, plane]
     mine = fold(energy)
     half = NZ // 2
     lane = lax.broadcasted_iota(jnp.int32, (1, NZ), 1)
@@ -249,17 +262,17 @@
     rows_ref[...] = jnp.broadcast_to(local, (DEVICES, NZ))
 
 
-def first(parity, own, bits, below, above, carry):
+def first(carry, own, mass, allow, bits, below, above):
     edge = shape(edge_layout(X_LEFT)[1], PAD, NZ)
     return pl.pallas_call(
         first_kernel,
-        in_specs=[SMEM] + [VMEM] * 5,
+        in_specs=[VMEM] * 7,
         out_specs=[VMEM] * 5,
-        out_shape=[shape(DEVICES, NZ), shape(CARRY, NZ), shape(2 + X_LEFT, EXT, PAD, NZ), edge, edge],
+        out_shape=[shape(DEVICES, NZ), shape(CARRY, NZ), shape(EXT, PAD, NZ), edge, edge],
         scratch_shapes=[pltpu.VMEM((EXT + 2, PAD, NZ), f32)] * 3,
         compiler_params=GRANT,
         name="first",
-    )(parity, own, bits, below, above, carry)
+    )(carry, own, mass, allow, bits, below, above)
 
 
 def pair_weights(mass_low, mass_high):
@@ -267,7 +280,9 @@
     return reduced / jnp.maximum(mass_low, 1.0), reduced / jnp.maximum(mass_high, 1.0)
 
 
-def join_kernel(parity_ref, own_ref, below_ref, above_ref, u_ref, weight_ref, mass_ref, all_mass_ref, bits_ref, both_ref, *, left, brick_axis):
+def join_kernel(
+    carry_ref, own_ref, mass_ref, own_bits_ref, below_ref, above_ref, u_ref, weight_ref, all_mass_ref, bits_ref, both_ref, *, left, first_step
+):
     for field, (place, planes) in enumerate(edge_layout(left)[0]):
         for k in range(planes):
             low, high = below_ref[place + k], above_ref[place + k]
@@ -282,16 +297,14 @@
             bits_ref[field - 2, k] = jnp.zeros((PAD, NZ), f32)
             bits_ref[field - 2, full_planes(left) - 1 - k] = jnp.zeros((PAD, NZ), f32)
     for k in range(EXT):
-        u_ref[left + k] = own_ref[0, k]
-        all_mass_ref[left + k] = own_ref[1, k]
-        mass_ref[k] = own_ref[1, k]
+        u_ref[left + k] = own_ref[k]
+        all_mass_ref[left + k] = mass_ref[k]
         for j in range(left):
-            bits_ref[j, left + k] = own_ref[2 + j, k]
+            bits_ref[j, left + k] = own_bits_ref[j, k]
     for plane in range(full_planes(left) - 1):
         both_ref[0, plane], both_ref[1, plane] = pair_weights(all_mass_ref[plane], all_mass_ref[plane + 1])
     for j in range(left):
-        step = STEPS - 2 * (left - j) + (0 if brick_axis == "bx" else 1)
-        start = lower_start(parity_ref, step, brick_axis, left)
+        start = whole(carry_ref, START_ROW + first_step + 2 * j)
         for k in range(pair_count(left)):
             plane = start + 2 * k
             allowed = jnp.maximum(bits_ref[j, plane], bits_ref[j, plane + 1])
@@ -299,16 +312,16 @@
             weight_ref[j, 1, k] = allowed * both_ref[1, plane]
 
 
-def join(parity, own, below, above, left, brick_axis):
+def join(carry, own, mass, bits, below, above, left, first_step):
     def body(*refs):
-        join_kernel(*refs, left=left, brick_axis=brick_axis)
+        join_kernel(*refs, left=left, first_step=first_step)
 
     full, pairs = full_planes(left), pair_count(left)
     return pl.pallas_call(
         body,
-        in_specs=[SMEM, VMEM, VMEM, VMEM],
-        out_specs=[VMEM] * 3,
-        out_shape=[shape(full, PAD, NZ), shape(left, 2, pairs, PAD, NZ), shape(EXT, PAD, NZ)],
+        in_specs=[VMEM] * 6,
+        out_specs=[VMEM] * 2,
+        out_shape=[shape(full, PAD, NZ), shape(left, 2, pairs, PAD, NZ)],
         scratch_shapes=[
             pltpu.VMEM((full, PAD, NZ), f32),
             pltpu.VMEM((left, full, PAD, NZ), f32),
@@ -316,7 +329,7 @@
         ],
         compiler_params=GRANT,
         name="join",
-    )(parity, own, below, above)
+    )(carry, own, mass, bits, below, above)
 
 
 def next_scale(received_ref, carry_ref, step):
@@ -336,7 +349,7 @@
 
 
 def step_kernel(received_ref, carry_ref, u_in_ref, weight_ref, mass_ref, u_ref, rows_ref, out_ref, *, step, left):
-    start = carry_ref[START_ROW + step : START_ROW + step + 1, :][0, 0].astype(jnp.int32)
+    start = whole(carry_ref, START_ROW + step)
     scale, total = next_scale(received_ref, carry_ref, step - 1)
     wide = jnp.broadcast_to(scale, (PAD, NZ))
     turn = left - (STEPS + 1 - step) // 2
@@ -379,8 +392,8 @@
     )(received, carry, u, weight, mass)
 
 
-def turn_kernel(shift_ref, v_ref, count_ref, spin_ref, w_ref):
-    shifts = [later_shifts(shift_ref, step) for step in range(STEPS)]
+def turn_kernel(carry_ref, v_ref, count_ref, spin_ref, w_ref):
+    shifts = [whole(carry_ref, SHIFT_ROW + step) for step in range(STEPS)]
 
     def plane(i, carry):
         real = jnp.ones((EXT, NZ), f32)
@@ -432,25 +445,25 @@
     lax.fori_loop(0, EXT, plane, 0)
 
 
-def turn(shifts, v, counts, spin):
+def turn(carry, v, counts, spin):
     return pl.pallas_call(
         turn_kernel,
-        in_specs=[SMEM, VMEM, VMEM, VMEM],
+        in_specs=[VMEM] * 4,
         out_specs=VMEM,
         out_shape=shape(3, SLOTS, EXT, EXT, NZ),
         compiler_params=GRANT,
         name="turn",
-    )(shifts, v, counts, spin)
-
-
-def finish_kernel(received_ref, carry_ref, ux_ref, uy_ref, uz_ref, own_ref, w_ref, v_ref):
+    )(carry, v, counts, spin)
+
+
+def finish_kernel(received_ref, carry_ref, ux_ref, uy_ref, uz_ref, mass_ref, w_ref, v_ref):
     member = pl.program_id(0)
     scale, _ = next_scale(received_ref, carry_ref, STEPS - 1)
     wide = jnp.broadcast_to(scale, (EXT, NZ))
 
     def write(mean_of):
         for i in range(EXT):
-            counts = own_ref[0, i, 0:EXT, :]
+            counts = mass_ref[i, 0:EXT, :]
             mean = mean_of(i)
             for slot in range(SLOTS):
                 v_ref[0, slot, i] = jnp.where(counts > slot, wide * (mean + w_ref[0, slot, i]), 0.0)
@@ -468,18 +481,17 @@
         write(lambda i: uz_ref[i, 0:EXT, :])
 
 
-def finish(received, carry, ux, uy, uz, own, w):
+def finish(received, carry, ux, uy, uz, mass, w):
     part = pl.BlockSpec((1, SLOTS, EXT, EXT, NZ), lambda c: (c, 0, 0, 0, 0))
-    mass = pl.BlockSpec((1, EXT, PAD, NZ), lambda c: (1, 0, 0, 0))
     return pl.pallas_call(
         finish_kernel,
         grid=(3,),
-        in_specs=[VMEM] * 5 + [mass, part],
+        in_specs=[VMEM] * 6 + [part],
         out_specs=part,
         out_shape=shape(3, SLOTS, EXT, EXT, NZ),
         compiler_params=GRANT,
         name="finish",
-    )(received, carry, ux, uy.reshape(full_planes(Y_LEFT) * PAD, NZ), uz, own, w)
+    )(received, carry, ux, uy.reshape(full_planes(Y_LEFT) * PAD, NZ), uz, mass, w)
 
 
 def exchange(low_edge, high_edge, axis):
@@ -494,26 +506,29 @@
 
 
 def per_device(v, counts, spin, flags, parity, shifts, heat):
-    own, uy, uz, low, high, carry = prep(shifts, parity, heat, v, counts, flags)
+    ux, mass, allow, uy, uz, low, high, carry = prep(shifts, parity, heat, v, counts, flags)
     above, below = exchange(low, high, "bx")
-    bits, sy, ylo, yhi = spread(shifts, own, uy, flags)
+    bits, uy, y_mass, y_bits, ylo, yhi = spread(carry, mass, uy, flags)
     y_above, y_below = exchange(ylo, yhi, "by")
-    rows, carry, sx, xlo, xhi = first(parity, own, bits, below, above, carry)
+    rows, carry, ux, xlo, xhi = first(carry, ux, mass, allow, bits, below, above)
     received = sum_over_devices(rows)
     x_above, x_below = exchange(xlo, xhi, "bx")
-    uy, y_weights, y_mass = join(parity, sy, y_below, y_above, Y_LEFT, "by")
-    ux, x_weights, x_mass = join(parity, sx, x_below, x_above, X_LEFT, "bx")
+    received, carry, uy = lax.optimization_barrier((received, carry, uy))
+    uy, y_weights = join(carry, uy, y_mass, y_bits, y_below, y_above, Y_LEFT, 1)
     for step in range(1, STEPS):
         if step % 2 == 0:
-            ux, rows, carry = collide(step, received, carry, ux, x_weights, x_mass)
+            ux, rows, carry = collide(step, received, carry, ux, x_weights, mass)
         else:
             uy, rows, carry = collide(step, received, carry, uy, y_weights, y_mass)
         received = sum_over_devices(rows)
+        if step == 1:
+            received, carry, ux = lax.optimization_barrier((received, carry, ux))
+            ux, x_weights = join(carry, ux, mass, bits, x_below, x_above, X_LEFT, 2)
         if step == TURN_STEP:
-            received, shifts = lax.optimization_barrier((received, shifts))
-            w = turn(shifts, v, counts, spin)
+            received, carry = lax.optimization_barrier((received, carry))
+            w = turn(carry, v, counts, spin)
             received, w = lax.optimization_barrier((received, w))
-    return finish(received, carry, ux, uy, uz, own, w)
+    return finish(received, carry, ux, uy, uz, mass, w)
 
 
 def solution(mesh):

time: 203 us -> 198 us (0.975)
  blocking collectives: 138 us -> 171 us
  waiting for transfers between devices: 17.1 us -> 2 us
  starting transfers between devices: 27.8 us -> 13.4 us
  Pallas kernels: 15.4 us -> 11.1 us
  local copies, waits for them, and re-layouts: 3.69 us -> 0.01 us
    all_to_all x10 -> x12, blocking collectives: 138 us -> 171 us  [sum_over_devices(): return lax.all_to_all(rows, ('bx', 'by'), 0, 0, tiled=True)]
    all_to_all x2 -> x0, waiting for transfers between devices: 15.1 us -> none  [sum_over_devices(): return lax.all_to_all(rows, ('bx', 'by'), 0, 0, tiled=True)]
    all_to_all x2 -> x0, starting transfers between devices: 14.4 us -> none  [sum_over_devices(): return lax.all_to_all(rows, ('bx', 'by'), 0, 0, tiled=True)]
    pallas_call x7, Pallas kernels: 12.7 us -> 8.9 us  [the longest x1 3.04 us: turn(): pl.pallas_call(turn_kernel, in_specs=[VMEM] * 4, out_specs=VMEM, out_shap...]
    unnamed x20 -> x8, local copies, waits for them, and re-layouts: 3.69 us -> 0.01 us
  transfers between devices with their start and end apart: 8 -> 6, of which waited for: 4 -> 2; matrix products, arithmetic and copies ran while one was open for 0% -> 0% of each run, Pallas kernels for 2% -> 0%
where the time goes in v5:
time: 198 us
  blocking collectives  171 us (86%)
  starting transfers between devices  13.4 us (7%)
  Pallas kernels  11.1 us (6%)
  waiting for transfers between devices  2 us (1%)
    all_to_all x12, blocking collectives, sum_over_devices(): return lax.all_to_all(rows, ('bx', 'by'), 0, 0, tiled=True)  171 us
    ppermute x3, starting transfers between devices, exchange(): lax.ppermute(high_edge, axis, up)  7.97 us
    ppermute x3, starting transfers between devices, exchange(): lax.ppermute(low_edge, axis, down)  5.4 us
  transfers between devices with their start and end apart: 6, of which 2 were waited for; matrix products, arithmetic and copies ran while one was open for 0% of the time, Pallas kernels for 0%

profile of v5, /device:TPU:1, one launch (start us, length us, event | category | flops | bytes accessed | tf_op | source)
XLA Modules:
  0.0 197.7 jit_solution(9104844738841094744)
XLA Ops:
  0.0 2.3 %prep.1 = (f32[15,16,128]{2,1,0:T(8,128)S(1)}, f32[15,16,128]{2,1,0:T(8,128)S(1)}, f32[15,16,128]{2,1,0:T(8,128)S(1)}, f32[16,16,128]{2,1,0:T(8,128)S(1)}, f32[1...) custom-call(s32[12]{0:T(128)} %shift_hbm.1, ...), custom_call_target="tpu_custom_call" | custom-call | tf_op jit(solution)/shard_map/prep/pallas_call | solution.py:152
  2.3 0.6 spread.1
  2.9 3.1 %collective-permute-start.2 = (f32[33,16,128]{2,1,0:T(8,128)S(1)}, f32[33,16,128]{2,1,0:T(8,128)S(1)}, u32[]{:S(2)}, u32[]{:S(2)}) collective-permute-start(f32[33,16,128]{2,1,0:T(8,128)S(1)} %get-tuple-element.87), channel_id=1, source_target_pairs={{0,1},{1,2},{2,3},{3,4},{4,5},{5,6},{6,7},{7,8},{8,9},{9,10},{10,1... | collective-permute-start | bytes 811016 | tf_op jit(solution)/shard_map/ppermute | solution.py:501
  6.0 2.7 %collective-permute-start = (f32[3,16,128]{2,1,0:T(8,128)S(1)}, f32[3,16,128]{2,1,0:T(8,128)S(1)}, u32[]{:S(2)}, u32[]{:S(2)}) collective-permute-start(f32[3,16,128]{2,1,0:T(8,128)S(1)} %get-tuple-element.77), channel_id=1, source_target_pairs={{0,16},{16,32},{32,48},{48,64},{64,80},{80,96},{96,112},{112,0},{1... | collective-permute-start | bytes 73736 | tf_op jit(solution)/shard_map/ppermute | solution.py:501
  8.7 2.5 %collective-permute-start.1 = (f32[3,16,128]{2,1,0:T(8,128)S(1)}, f32[3,16,128]{2,1,0:T(8,128)S(1)}, u32[]{:S(2)}, u32[]{:S(2)}) collective-permute-start(f32[3,16,128]{2,1,0:T(8,128)S(1)} %get-tuple-element.78), channel_id=1, source_target_pairs={{0,112},{16,0},{32,16},{48,32},{64,48},{80,64},{96,80},{112,96},{1... | collective-permute-start | bytes 73736 | tf_op jit(solution)/shard_map/ppermute | solution.py:501
  11.2 1.2 collective-permute-done.below_ref
  12.4 0.8 collective-permute-done.1.above_ref
  13.2 0.2 first.1
  13.4 2.1 %collective-permute-start.4 = (f32[25,16,128]{2,1,0:T(8,128)S(1)}, f32[25,16,128]{2,1,0:T(8,128)S(1)}, u32[]{:S(2)}, u32[]{:S(2)}) collective-permute-start(f32[25,16,128]{2,1,0:T(8,128)S(1)} %get-tuple-element.97), channel_id=1, source_target_pairs={{0,16},{16,32},{32,48},{48,64},{64,80},{80,96},{96,112},{112,0},{1... | collective-permute-start | bytes 614408 | tf_op jit(solution)/shard_map/ppermute | solution.py:501
  15.5 2.9 %collective-permute-start.5 = (f32[25,16,128]{2,1,0:T(8,128)S(1)}, f32[25,16,128]{2,1,0:T(8,128)S(1)}, u32[]{:S(2)}, u32[]{:S(2)}) collective-permute-start(f32[25,16,128]{2,1,0:T(8,128)S(1)} %get-tuple-element.98), channel_id=1, source_target_pairs={{0,112},{16,0},{32,16},{48,32},{64,48},{80,64},{96,80},{112,96},{1... | collective-permute-start | bytes 614408 | tf_op jit(solution)/shard_map/ppermute | solution.py:501
  18.5 18.8 %all_to_all.135 = f32[128,1,128]{2,1,0:T(1,128)S(1)} all-to-all(f32[128,1,128]{2,1,0:T(1,128)S(1)} %bitcast.64), channel_id=1, replica_groups=mesh['bx'=8,'by'=16] {'bx','by'}, dimensions={0} | all-to-all | bytes 131072 | tf_op jit(solution)/shard_map/all_to_all | solution.py:505
  37.3 0.3 join.2
  37.6 0.2 collide.11
  37.8 13.8 %all_to_all.136 = f32[128,1,128]{2,1,0:T(1,128)S(1)} all-to-all(f32[128,1,128]{2,1,0:T(1,128)S(1)} %bitcast.67), channel_id=1, replica_groups=mesh['bx'=8,'by'=16] {'bx','by'}, dimensions={0} | all-to-all | bytes 131072 | tf_op jit(solution)/shard_map/all_to_all | solution.py:505
  51.7 0.3 join.3
  51.9 0.2 collide.12
  52.1 13.8 %all_to_all.137 = f32[128,1,128]{2,1,0:T(1,128)S(1)} all-to-all(f32[128,1,128]{2,1,0:T(1,128)S(1)} %bitcast.68), channel_id=1, replica_groups=mesh['bx'=8,'by'=16] {'bx','by'}, dimensions={0} | all-to-all | bytes 131072 | tf_op jit(solution)/shard_map/all_to_all | solution.py:505
  66.2 13.8 %all_to_all.138 = f32[128,1,128]{2,1,0:T(1,128)S(1)} all-to-all(f32[128,1,128]{2,1,0:T(1,128)S(1)} %bitcast.69), channel_id=1, replica_groups=mesh['bx'=8,'by'=16] {'bx','by'}, dimensions={0} | all-to-all | bytes 131072 | tf_op jit(solution)/shard_map/all_to_all | solution.py:505
  80.2 13.8 %all_to_all.139 = f32[128,1,128]{2,1,0:T(1,128)S(1)} all-to-all(f32[128,1,128]{2,1,0:T(1,128)S(1)} %bitcast.70), channel_id=1, replica_groups=mesh['bx'=8,'by'=16] {'bx','by'}, dimensions={0} | all-to-all | bytes 131072 | tf_op jit(solution)/shard_map/all_to_all | solution.py:505
  94.3 13.8 %all_to_all.140 = f32[128,1,128]{2,1,0:T(1,128)S(1)} all-to-all(f32[128,1,128]{2,1,0:T(1,128)S(1)} %bitcast.71), channel_id=1, replica_groups=mesh['bx'=8,'by'=16] {'bx','by'}, dimensions={0} | all-to-all | bytes 131072 | tf_op jit(solution)/shard_map/all_to_all | solution.py:505
  108.1 3.0 %turn.1.w_ref = f32[3,6,15,15,128]{4,3,2,1,0:T(8,128)S(1)} custom-call(f32[56,128]{1,0:T(8,128)S(1)} %get-tuple-element.113.carry_ref.refs_1_, f32[3,6,15,15,128]{4,3,2,1,0:T(8,128)S(1)} %copy-done, s32[15,15,128]{2,1,0:T(8,128)S(1)} %copy-done.3, s32[12,15,15,128]{3,2,1,0:T(8,128)S(1)} %copy-done.2), custom_call_target="tpu_custom_call" | custom-call | tf_op jit(solution)/shard_map/turn/pallas_call | solution.py:449
  111.2 0.2 collide.16
  111.4 13.8 %all_to_all.141 = f32[128,1,128]{2,1,0:T(1,128)S(1)} all-to-all(f32[128,1,128]{2,1,0:T(1,128)S(1)} %bitcast.72), channel_id=1, replica_groups=mesh['bx'=8,'by'=16] {'bx','by'}, dimensions={0} | all-to-all | bytes 131072 | tf_op jit(solution)/shard_map/all_to_all | solution.py:505
  125.4 13.8 %all_to_all.142 = f32[128,1,128]{2,1,0:T(1,128)S(1)} all-to-all(f32[128,1,128]{2,1,0:T(1,128)S(1)} %bitcast.73), channel_id=1, replica_groups=mesh['bx'=8,'by'=16] {'bx','by'}, dimensions={0} | all-to-all | bytes 131072 | tf_op jit(solution)/shard_map/all_to_all | solution.py:505
  139.3 0.2 collide.18
  139.5 13.8 %all_to_all.143 = f32[128,1,128]{2,1,0:T(1,128)S(1)} all-to-all(f32[128,1,128]{2,1,0:T(1,128)S(1)} %bitcast.74), channel_id=1, replica_groups=mesh['bx'=8,'by'=16] {'bx','by'}, dimensions={0} | all-to-all | bytes 131072 | tf_op jit(solution)/shard_map/all_to_all | solution.py:505
  153.5 13.8 %all_to_all.144 = f32[128,1,128]{2,1,0:T(1,128)S(1)} all-to-all(f32[128,1,128]{2,1,0:T(1,128)S(1)} %bitcast.75), channel_id=1, replica_groups=mesh['bx'=8,'by'=16] {'bx','by'}, dimensions={0} | all-to-all | bytes 131072 | tf_op jit(solution)/shard_map/all_to_all | solution.py:505
  167.4 0.2 collide.20
  167.6 13.8 %all_to_all.145 = f32[128,1,128]{2,1,0:T(1,128)S(1)} all-to-all(f32[128,1,128]{2,1,0:T(1,128)S(1)} %bitcast.66), channel_id=1, replica_groups=mesh['bx'=8,'by'=16] {'bx','by'}, dimensions={0} | all-to-all | bytes 131072 | tf_op jit(solution)/shard_map/all_to_all | solution.py:505
  181.4 0.2 collide.21
  181.6 13.8 %all_to_all.146 = f32[128,1,128]{2,1,0:T(1,128)S(1)} all-to-all(f32[128,1,128]{2,1,0:T(1,128)S(1)} %bitcast.65), channel_id=1, replica_groups=mesh['bx'=8,'by'=16] {'bx','by'}, dimensions={0} | all-to-all | bytes 131072 | tf_op jit(solution)/shard_map/all_to_all | solution.py:505
  195.5 2.2 %finish.1 = f32[3,6,15,15,128]{4,3,2,1,0:T(8,128)} custom-call(f32[128,128]{1,0:T(8,128)S(1)} %bitcast.50, f32[56,128]{1,0:T(8,128)S(1)} %get-tuple-element.132.carry_ref, f32[25,16,128]{2,1,0:T(8,128)S(1)} %get-tuple-element.133.ux_ref, f32[432,128]{1,0:T(8,128)S(1)} %bitcast.62, f32[15,16,128]{2,1,0:T(8,128)S(1)} %get-tuple-element.135.uz_ref, ...), custom_call_target="tpu_custom_call" | custom-call | tf_op jit(solution)/shard_map/finish/pallas_call | solution.py:486
  (18 shorter events, 1.0 us)
Async XLA Ops:
  0.0 2.3 %copy-start.1 = (s32[12,15,15,128]{3,2,1,0:T(8,128)S(1)}, s32[12,15,15,128]{3,2,1,0:T(8,128)}, u32[]{:S(2)}) copy-start(s32[12,15,15,128]{3,2,1,0:T(8,128)} %flag_ref.1) | copy-start | bytes 4147204
  2.9 34.4 %collective-permute-start.2 = (f32[33,16,128]{2,1,0:T(8,128)S(1)}, f32[33,16,128]{2,1,0:T(8,128)S(1)}, u32[]{:S(2)}, u32[]{:S(2)}) collective-permute-start(f32[33,16,128]{2,1,0:T(8,128)S(1)} %get-tuple-element.87), channel_id=1, source_target_pairs={{0,1},{1,2},{2,3},{3,4},{4,5},{5,6},{6,7},{7,8},{8,9},{9,10},{10,1... | collective-permute-start | bytes 811016 | tf_op jit(solution)/shard_map/ppermute | solution.py:501
  6.0 31.3 %collective-permute-start.3 = (f32[33,16,128]{2,1,0:T(8,128)S(1)}, f32[33,16,128]{2,1,0:T(8,128)S(1)}, u32[]{:S(2)}, u32[]{:S(2)}) collective-permute-start(f32[33,16,128]{2,1,0:T(8,128)S(1)} %get-tuple-element.88), channel_id=1, source_target_pairs={{0,15},{1,0},{2,1},{3,2},{4,3},{5,4},{6,5},{7,6},{8,7},{9,8},{10,9... | collective-permute-start | bytes 811016 | tf_op jit(solution)/shard_map/ppermute | solution.py:501
  6.0 6.4 %collective-permute-start = (f32[3,16,128]{2,1,0:T(8,128)S(1)}, f32[3,16,128]{2,1,0:T(8,128)S(1)}, u32[]{:S(2)}, u32[]{:S(2)}) collective-permute-start(f32[3,16,128]{2,1,0:T(8,128)S(1)} %get-tuple-element.77), channel_id=1, source_target_pairs={{0,16},{16,32},{32,48},{48,64},{64,80},{80,96},{96,112},{112,0},{1... | collective-permute-start | bytes 73736 | tf_op jit(solution)/shard_map/ppermute | solution.py:501
  8.7 4.4 %collective-permute-start.1 = (f32[3,16,128]{2,1,0:T(8,128)S(1)}, f32[3,16,128]{2,1,0:T(8,128)S(1)}, u32[]{:S(2)}, u32[]{:S(2)}) collective-permute-start(f32[3,16,128]{2,1,0:T(8,128)S(1)} %get-tuple-element.78), channel_id=1, source_target_pairs={{0,112},{16,0},{32,16},{48,32},{64,48},{80,64},{96,80},{112,96},{1... | collective-permute-start | bytes 73736 | tf_op jit(solution)/shard_map/ppermute | solution.py:501
  13.4 38.3 %collective-permute-start.4 = (f32[25,16,128]{2,1,0:T(8,128)S(1)}, f32[25,16,128]{2,1,0:T(8,128)S(1)}, u32[]{:S(2)}, u32[]{:S(2)}) collective-permute-start(f32[25,16,128]{2,1,0:T(8,128)S(1)} %get-tuple-element.97), channel_id=1, source_target_pairs={{0,16},{16,32},{32,48},{48,64},{64,80},{80,96},{96,112},{112,0},{1... | collective-permute-start | bytes 614408 | tf_op jit(solution)/shard_map/ppermute | solution.py:501
  15.5 36.1 %collective-permute-start.5 = (f32[25,16,128]{2,1,0:T(8,128)S(1)}, f32[25,16,128]{2,1,0:T(8,128)S(1)}, u32[]{:S(2)}, u32[]{:S(2)}) collective-permute-start(f32[25,16,128]{2,1,0:T(8,128)S(1)} %get-tuple-element.98), channel_id=1, source_target_pairs={{0,112},{16,0},{32,16},{48,32},{64,48},{80,64},{96,80},{112,96},{1... | collective-permute-start | bytes 614408 | tf_op jit(solution)/shard_map/ppermute | solution.py:501
  66.0 42.1 %copy-start = (f32[3,6,15,15,128]{4,3,2,1,0:T(8,128)S(1)}, f32[3,6,15,15,128]{4,3,2,1,0:T(8,128)}, u32[]{:S(2)}) copy-start(f32[3,6,15,15,128]{4,3,2,1,0:T(8,128)} %v_ref.1) | copy-start | bytes 6220804
  66.0 42.1 %copy-start.2 = (s32[12,15,15,128]{3,2,1,0:T(8,128)S(1)}, s32[12,15,15,128]{3,2,1,0:T(8,128)}, u32[]{:S(2)}) copy-start(s32[12,15,15,128]{3,2,1,0:T(8,128)} %spin_ref.1) | copy-start | bytes 4147204
  66.0 42.1 %copy-start.3 = (s32[15,15,128]{2,1,0:T(8,128)S(1)}, s32[15,15,128]{2,1,0:T(8,128)}, u32[]{:S(2)}) copy-start(s32[15,15,128]{2,1,0:T(8,128)} %count_ref.1) | copy-start | bytes 345604

commit v6 on v5

--- a/solution.py
+++ b/solution.py
@@ -13,7 +13,6 @@
 EXT = 15
 PAD = 16
 CHUNK = 3
-TURN_STEP = 5
 NZ = 128
 DEVICES = 128
 X_LEFT = HALF - 1
@@ -39,6 +38,10 @@
 
 def shape(*dims):
     return jax.ShapeDtypeStruct(dims, f32)
+
+
+def far(*dims):
+    return pltpu.HBM(dims, f32)
 
 
 def later_shifts(shift_ref, step):
@@ -217,7 +220,7 @@
 
 def first_kernel(
     carry_ref, own_ref, own_mass_ref, own_allow_ref, bits_ref, below_ref, above_ref,
-    rows_ref, out_ref, next_ref, xlo_ref, xhi_ref, u_ref, mass_ref, allow_ref,
+    rows_ref, out_ref, next_ref, xlo_hbm, xhi_hbm, u_ref, mass_ref, allow_ref, xlo_ref, xhi_ref, sems,
 ):
     for field, (all_ref, mine_ref) in enumerate(
         ((u_ref, own_ref), (mass_ref, own_mass_ref), (allow_ref, own_allow_ref))
@@ -237,11 +240,8 @@
         push = allowed * closing * jnp.tanh(wide * closing)
         u_ref[plane] = low - weight_low * push
         u_ref[plane + 1] = high + weight_high * push
-    energy = jnp.zeros((PAD, NZ), f32)
     for k in range(EXT):
-        u = u_ref[1 + k]
-        energy = energy + own_mass_ref[k] * u * u
-        next_ref[k] = u
+        next_ref[k] = u_ref[1 + k]
     for field, (place, planes) in enumerate(edge_layout(X_LEFT)[0]):
         for k in range(planes):
             for edge_ref, plane in ((xlo_ref, k), (xhi_ref, EXT - planes + k)):
@@ -251,6 +251,16 @@
                     edge_ref[place + k] = own_mass_ref[plane]
                 else:
                     edge_ref[place + k] = bits_ref[field - 2, plane]
+    sends = [
+        pltpu.make_async_copy(xlo_ref, xlo_hbm, sems.at[0]),
+        pltpu.make_async_copy(xhi_ref, xhi_hbm, sems.at[1]),
+    ]
+    for send in sends:
+        send.start()
+    energy = jnp.zeros((PAD, NZ), f32)
+    for k in range(EXT):
+        u = next_ref[k]
+        energy = energy + own_mass_ref[k] * u * u
     mine = fold(energy)
     half = NZ // 2
     lane = lax.broadcasted_iota(jnp.int32, (1, NZ), 1)
@@ -260,16 +270,20 @@
     out_ref[...] = carry_ref[...]
     out_ref[3:4, :] = mine
     rows_ref[...] = jnp.broadcast_to(local, (DEVICES, NZ))
+    for send in sends:
+        send.wait()
 
 
 def first(carry, own, mass, allow, bits, below, above):
-    edge = shape(edge_layout(X_LEFT)[1], PAD, NZ)
+    edge = (edge_layout(X_LEFT)[1], PAD, NZ)
     return pl.pallas_call(
         first_kernel,
         in_specs=[VMEM] * 7,
-        out_specs=[VMEM] * 5,
-        out_shape=[shape(DEVICES, NZ), shape(CARRY, NZ), shape(EXT, PAD, NZ), edge, edge],
-        scratch_shapes=[pltpu.VMEM((EXT + 2, PAD, NZ), f32)] * 3,
+        out_specs=[VMEM] * 3 + [ANY] * 2,
+        out_shape=[shape(DEVICES, NZ), shape(CARRY, NZ), shape(EXT, PAD, NZ), far(*edge), far(*edge)],
+        scratch_shapes=[pltpu.VMEM((EXT + 2, PAD, NZ), f32)] * 3
+        + [pltpu.VMEM(edge, f32)] * 2
+        + [pltpu.SemaphoreType.DMA((2,))],
         compiler_params=GRANT,
         name="first",
     )(carry, own, mass, allow, bits, below, above)
@@ -392,7 +406,7 @@
     )(received, carry, u, weight, mass)
 
 
-def turn_kernel(carry_ref, v_ref, count_ref, spin_ref, w_ref):
+def turn_kernel(carry_ref, v_ref, count_ref, spin_ref, w_hbm, w_ref, sems):
     shifts = [whole(carry_ref, SHIFT_ROW + step) for step in range(STEPS)]
 
     def plane(i, carry):
@@ -440,17 +454,25 @@
             for member in range(3):
                 turned = rows[member][0] * rest[0] + rows[member][1] * rest[1] + rows[member][2] * rest[2]
                 w_ref[member, slot, i] = turned
+        send(i).start()
         return carry
 
+    def send(i):
+        part = pl.ds(i, 1)
+        return pltpu.make_async_copy(w_ref.at[:, :, part], w_hbm.at[:, :, part], sems.at[i])
+
     lax.fori_loop(0, EXT, plane, 0)
+    for i in range(EXT):
+        send(i).wait()
 
 
 def turn(carry, v, counts, spin):
     return pl.pallas_call(
         turn_kernel,
         in_specs=[VMEM] * 4,
-        out_specs=VMEM,
-        out_shape=shape(3, SLOTS, EXT, EXT, NZ),
+        out_specs=ANY,
+        out_shape=far(3, SLOTS, EXT, EXT, NZ),
+        scratch_shapes=[pltpu.VMEM((3, SLOTS, EXT, EXT, NZ), f32), pltpu.SemaphoreType.DMA((EXT,))],
         compiler_params=GRANT,
         name="turn",
     )(carry, v, counts, spin)
@@ -507,9 +529,12 @@
 
 def per_device(v, counts, spin, flags, parity, shifts, heat):
     ux, mass, allow, uy, uz, low, high, carry = prep(shifts, parity, heat, v, counts, flags)
+    carry, v, counts, spin, flags = lax.optimization_barrier((carry, v, counts, spin, flags))
     above, below = exchange(low, high, "bx")
     bits, uy, y_mass, y_bits, ylo, yhi = spread(carry, mass, uy, flags)
     y_above, y_below = exchange(ylo, yhi, "by")
+    w = turn(carry, v, counts, spin)
+    below, above, w = lax.optimization_barrier((below, above, w))
     rows, carry, ux, xlo, xhi = first(carry, ux, mass, allow, bits, below, above)
     received = sum_over_devices(rows)
     x_above, x_below = exchange(xlo, xhi, "bx")
@@ -524,10 +549,6 @@
         if step == 1:
             received, carry, ux = lax.optimization_barrier((received, carry, ux))
             ux, x_weights = join(carry, ux, mass, bits, x_below, x_above, X_LEFT, 2)
-        if step == TURN_STEP:
-            received, carry = lax.optimization_barrier((received, carry))
-            w = turn(carry, v, counts, spin)
-            received, w = lax.optimization_barrier((received, w))
     return finish(received, carry, ux, uy, uz, mass, w)
 
 

time: 198 us -> 196 us (0.990)
  blocking collectives: 171 us -> 169 us
  waiting for transfers between devices: 2 us -> 0.02 us
  transfers between devices with their start and end apart: 6 -> 6, of which waited for: 2 -> 0; matrix products, arithmetic and copies ran while one was open for 0% -> 0% of each run, Pallas kernels for 0% -> 3%
where the time goes in v6:
time: 196 us; the launch traced here: 195 us
  blocking collectives  169 us (86%)
  starting transfers between devices  13.4 us (7%)
  Pallas kernels  12.6 us (6%)
    all_to_all x12, blocking collectives, sum_over_devices(): return lax.all_to_all(rows, ('bx', 'by'), 0, 0, tiled=True)  169 us
    ppermute x3, starting transfers between devices, exchange(): lax.ppermute(low_edge, axis, down)  7.02 us
    ppermute x3, starting transfers between devices, exchange(): lax.ppermute(high_edge, axis, up)  6.41 us
  transfers between devices with their start and end apart: 6, of which 0 were waited for; matrix products, arithmetic and copies ran while one was open for 0% of the time, Pallas kernels for 3%

profile of v6, /device:TPU:1, one launch (start us, length us, event | category | flops | bytes accessed | tf_op | source)
XLA Modules:
  0.0 195.4 jit_solution(6265971252247162139)
XLA Ops:
  0.0 2.3 %prep.1 = (f32[15,16,128]{2,1,0:T(8,128)S(1)}, f32[15,16,128]{2,1,0:T(8,128)S(1)}, f32[15,16,128]{2,1,0:T(8,128)S(1)}, f32[16,16,128]{2,1,0:T(8,128)S(1)}, f32[1...) custom-call(s32[12]{0:T(128)} %shift_hbm.1, ...), custom_call_target="tpu_custom_call" | custom-call | tf_op jit(solution)/shard_map/prep/pallas_call | solution.py:155
  2.3 0.6 spread.1
  3.0 3.1 %collective-permute-start.2 = (f32[33,16,128]{2,1,0:T(8,128)S(1)}, f32[33,16,128]{2,1,0:T(8,128)S(1)}, u32[]{:S(2)}, u32[]{:S(2)}) collective-permute-start(f32[33,16,128]{2,1,0:T(8,128)S(1)} %get-tuple-element.98), channel_id=1, source_target_pairs={{0,1},{1,2},{2,3},{3,4},{4,5},{5,6},{6,7},{7,8},{8,9},{9,10},{10,1... | collective-permute-start | bytes 811016 | tf_op jit(solution)/shard_map/ppermute | solution.py:523
  6.0 2.7 %collective-permute-start = (f32[3,16,128]{2,1,0:T(8,128)S(1)}, f32[3,16,128]{2,1,0:T(8,128)S(1)}, u32[]{:S(2)}, u32[]{:S(2)}) collective-permute-start(f32[3,16,128]{2,1,0:T(8,128)S(1)} %get-tuple-element.83), channel_id=1, source_target_pairs={{0,16},{16,32},{32,48},{48,64},{64,80},{80,96},{96,112},{112,0},{1... | collective-permute-start | bytes 73736 | tf_op jit(solution)/shard_map/ppermute | solution.py:523
  8.8 2.5 %collective-permute-start.1 = (f32[3,16,128]{2,1,0:T(8,128)S(1)}, f32[3,16,128]{2,1,0:T(8,128)S(1)}, u32[]{:S(2)}, u32[]{:S(2)}) collective-permute-start(f32[3,16,128]{2,1,0:T(8,128)S(1)} %get-tuple-element.84), channel_id=1, source_target_pairs={{0,112},{16,0},{32,16},{48,32},{64,48},{80,64},{96,80},{112,96},{1... | collective-permute-start | bytes 73736 | tf_op jit(solution)/shard_map/ppermute | solution.py:523
  11.3 3.8 %turn.1.w_ref = f32[3,6,15,15,128]{4,3,2,1,0:T(8,128)} custom-call(f32[56,128]{1,0:T(8,128)S(1)} %get-tuple-element.76.carry_ref, f32[3,6,15,15,128]{4,3,2,1,0:T(8,128)S(1)} %copy-done, s32[15,15,128]{2,1,0:T(8,128)S(1)} %copy-done.4, s32[12,15,15,128]{3,2,1,0:T(8,128)S(1)} %copy-done.3), custom_call_target="tpu_custom_call" | custom-call | tf_op jit(solution)/shard_map/turn/pallas_call | solution.py:470
  15.1 0.9 first.1
  16.1 0.6 collective-permute-start.4
  16.6 4.6 %collective-permute-start.5 = (f32[25,16,128]{2,1,0:T(8,128)}, f32[25,16,128]{2,1,0:T(8,128)S(1)}, u32[]{:S(2)}, u32[]{:S(2)}) collective-permute-start(f32[25,16,128]{2,1,0:T(8,128)} %get-tuple-element.109), channel_id=1, source_target_pairs={{0,112},{16,0},{32,16},{48,32},{64,48},{80,64},{96,80},{112,96},{1... | collective-permute-start | bytes 614408 | tf_op jit(solution)/shard_map/ppermute | solution.py:523
  21.2 16.9 %all_to_all.134 = f32[128,1,128]{2,1,0:T(1,128)S(1)} all-to-all(f32[128,1,128]{2,1,0:T(1,128)S(1)} %bitcast.64), channel_id=1, replica_groups=mesh['bx'=8,'by'=16] {'bx','by'}, dimensions={0} | all-to-all | bytes 131072 | tf_op jit(solution)/shard_map/all_to_all | solution.py:527
  38.1 0.3 join.2
  38.4 0.2 collide.11
  38.6 13.8 %all_to_all.135 = f32[128,1,128]{2,1,0:T(1,128)S(1)} all-to-all(f32[128,1,128]{2,1,0:T(1,128)S(1)} %bitcast.67), channel_id=1, replica_groups=mesh['bx'=8,'by'=16] {'bx','by'}, dimensions={0} | all-to-all | bytes 131072 | tf_op jit(solution)/shard_map/all_to_all | solution.py:527
  52.5 0.3 join.3
  52.8 0.2 collide.12
  53.0 13.8 %all_to_all.136 = f32[128,1,128]{2,1,0:T(1,128)S(1)} all-to-all(f32[128,1,128]{2,1,0:T(1,128)S(1)} %bitcast.68), channel_id=1, replica_groups=mesh['bx'=8,'by'=16] {'bx','by'}, dimensions={0} | all-to-all | bytes 131072 | tf_op jit(solution)/shard_map/all_to_all | solution.py:527
  66.8 0.2 collide.13
  67.0 13.8 %all_to_all.137 = f32[128,1,128]{2,1,0:T(1,128)S(1)} all-to-all(f32[128,1,128]{2,1,0:T(1,128)S(1)} %bitcast.69), channel_id=1, replica_groups=mesh['bx'=8,'by'=16] {'bx','by'}, dimensions={0} | all-to-all | bytes 131072 | tf_op jit(solution)/shard_map/all_to_all | solution.py:527
  81.1 13.8 %all_to_all.138 = f32[128,1,128]{2,1,0:T(1,128)S(1)} all-to-all(f32[128,1,128]{2,1,0:T(1,128)S(1)} %bitcast.70), channel_id=1, replica_groups=mesh['bx'=8,'by'=16] {'bx','by'}, dimensions={0} | all-to-all | bytes 131072 | tf_op jit(solution)/shard_map/all_to_all | solution.py:527
  94.9 0.2 collide.15
  95.1 13.8 %all_to_all.139 = f32[128,1,128]{2,1,0:T(1,128)S(1)} all-to-all(f32[128,1,128]{2,1,0:T(1,128)S(1)} %bitcast.71), channel_id=1, replica_groups=mesh['bx'=8,'by'=16] {'bx','by'}, dimensions={0} | all-to-all | bytes 131072 | tf_op jit(solution)/shard_map/all_to_all | solution.py:527
  109.1 13.8 %all_to_all.140 = f32[128,1,128]{2,1,0:T(1,128)S(1)} all-to-all(f32[128,1,128]{2,1,0:T(1,128)S(1)} %bitcast.72), channel_id=1, replica_groups=mesh['bx'=8,'by'=16] {'bx','by'}, dimensions={0} | all-to-all | bytes 131072 | tf_op jit(solution)/shard_map/all_to_all | solution.py:527
  123.0 0.2 collide.17
  123.2 13.8 %all_to_all.141 = f32[128,1,128]{2,1,0:T(1,128)S(1)} all-to-all(f32[128,1,128]{2,1,0:T(1,128)S(1)} %bitcast.73), channel_id=1, replica_groups=mesh['bx'=8,'by'=16] {'bx','by'}, dimensions={0} | all-to-all | bytes 131072 | tf_op jit(solution)/shard_map/all_to_all | solution.py:527
  137.2 13.8 %all_to_all.142 = f32[128,1,128]{2,1,0:T(1,128)S(1)} all-to-all(f32[128,1,128]{2,1,0:T(1,128)S(1)} %bitcast.74), channel_id=1, replica_groups=mesh['bx'=8,'by'=16] {'bx','by'}, dimensions={0} | all-to-all | bytes 131072 | tf_op jit(solution)/shard_map/all_to_all | solution.py:527
  151.1 0.2 collide.19
  151.3 13.9 %all_to_all.143 = f32[128,1,128]{2,1,0:T(1,128)S(1)} all-to-all(f32[128,1,128]{2,1,0:T(1,128)S(1)} %bitcast.75), channel_id=1, replica_groups=mesh['bx'=8,'by'=16] {'bx','by'}, dimensions={0} | all-to-all | bytes 131072 | tf_op jit(solution)/shard_map/all_to_all | solution.py:527
  165.1 0.2 collide.20
  165.3 13.8 %all_to_all.144 = f32[128,1,128]{2,1,0:T(1,128)S(1)} all-to-all(f32[128,1,128]{2,1,0:T(1,128)S(1)} %bitcast.66), channel_id=1, replica_groups=mesh['bx'=8,'by'=16] {'bx','by'}, dimensions={0} | all-to-all | bytes 131072 | tf_op jit(solution)/shard_map/all_to_all | solution.py:527
  179.2 0.2 collide.21
  179.4 13.8 %all_to_all.145 = f32[128,1,128]{2,1,0:T(1,128)S(1)} all-to-all(f32[128,1,128]{2,1,0:T(1,128)S(1)} %bitcast.65), channel_id=1, replica_groups=mesh['bx'=8,'by'=16] {'bx','by'}, dimensions={0} | all-to-all | bytes 131072 | tf_op jit(solution)/shard_map/all_to_all | solution.py:527
  193.2 2.2 %finish.1 = f32[3,6,15,15,128]{4,3,2,1,0:T(8,128)} custom-call(f32[128,128]{1,0:T(8,128)S(1)} %bitcast.50, f32[56,128]{1,0:T(8,128)S(1)} %get-tuple-element.140.carry_ref, f32[25,16,128]{2,1,0:T(8,128)S(1)} %get-tuple-element.141.ux_ref, f32[432,128]{1,0:T(8,128)S(1)} %bitcast.62, f32[15,16,128]{2,1,0:T(8,128)S(1)} %get-tuple-element.143.uz_ref, ...), custom_call_target="tpu_custom_call" | custom-call | tf_op jit(solution)/shard_map/finish/pallas_call | solution.py:508
  (20 shorter events, 0.6 us)
Async XLA Ops:
  0.0 2.3 %copy-start.2 = (s32[12,15,15,128]{3,2,1,0:T(8,128)S(1)}, s32[12,15,15,128]{3,2,1,0:T(8,128)}, u32[]{:S(2)}) copy-start(s32[12,15,15,128]{3,2,1,0:T(8,128)} %flag_ref) | copy-start | bytes 4147204
  0.0 11.2 %copy-start.4 = (s32[15,15,128]{2,1,0:T(8,128)S(1)}, s32[15,15,128]{2,1,0:T(8,128)}, u32[]{:S(2)}) copy-start(s32[15,15,128]{2,1,0:T(8,128)} %count_ref) | copy-start | bytes 345604
  0.0 11.2 %copy-start = (f32[3,6,15,15,128]{4,3,2,1,0:T(8,128)S(1)}, f32[3,6,15,15,128]{4,3,2,1,0:T(8,128)}, u32[]{:S(2)}) copy-start(f32[3,6,15,15,128]{4,3,2,1,0:T(8,128)} %v_ref) | copy-start | bytes 6220804
  0.0 11.2 %copy-start.3 = (s32[12,15,15,128]{3,2,1,0:T(8,128)S(1)}, s32[12,15,15,128]{3,2,1,0:T(8,128)}, u32[]{:S(2)}) copy-start(s32[12,15,15,128]{3,2,1,0:T(8,128)} %spin_ref) | copy-start | bytes 4147204
  3.0 35.2 %collective-permute-start.2 = (f32[33,16,128]{2,1,0:T(8,128)S(1)}, f32[33,16,128]{2,1,0:T(8,128)S(1)}, u32[]{:S(2)}, u32[]{:S(2)}) collective-permute-start(f32[33,16,128]{2,1,0:T(8,128)S(1)} %get-tuple-element.98), channel_id=1, source_target_pairs={{0,1},{1,2},{2,3},{3,4},{4,5},{5,6},{6,7},{7,8},{8,9},{9,10},{10,1... | collective-permute-start | bytes 811016 | tf_op jit(solution)/shard_map/ppermute | solution.py:523
  6.0 32.1 %collective-permute-start.3 = (f32[33,16,128]{2,1,0:T(8,128)S(1)}, f32[33,16,128]{2,1,0:T(8,128)S(1)}, u32[]{:S(2)}, u32[]{:S(2)}) collective-permute-start(f32[33,16,128]{2,1,0:T(8,128)S(1)} %get-tuple-element.99), channel_id=1, source_target_pairs={{0,15},{1,0},{2,1},{3,2},{4,3},{5,4},{6,5},{7,6},{8,7},{9,8},{10,9... | collective-permute-start | bytes 811016 | tf_op jit(solution)/shard_map/ppermute | solution.py:523
  6.0 9.1 %collective-permute-start = (f32[3,16,128]{2,1,0:T(8,128)S(1)}, f32[3,16,128]{2,1,0:T(8,128)S(1)}, u32[]{:S(2)}, u32[]{:S(2)}) collective-permute-start(f32[3,16,128]{2,1,0:T(8,128)S(1)} %get-tuple-element.83), channel_id=1, source_target_pairs={{0,16},{16,32},{32,48},{48,64},{64,80},{80,96},{96,112},{112,0},{1... | collective-permute-start | bytes 73736 | tf_op jit(solution)/shard_map/ppermute | solution.py:523
  8.8 6.3 %collective-permute-start.1 = (f32[3,16,128]{2,1,0:T(8,128)S(1)}, f32[3,16,128]{2,1,0:T(8,128)S(1)}, u32[]{:S(2)}, u32[]{:S(2)}) collective-permute-start(f32[3,16,128]{2,1,0:T(8,128)S(1)} %get-tuple-element.84), channel_id=1, source_target_pairs={{0,112},{16,0},{32,16},{48,32},{64,48},{80,64},{96,80},{112,96},{1... | collective-permute-start | bytes 73736 | tf_op jit(solution)/shard_map/ppermute | solution.py:523
  16.1 36.4 %collective-permute-start.4 = (f32[25,16,128]{2,1,0:T(8,128)}, f32[25,16,128]{2,1,0:T(8,128)S(1)}, u32[]{:S(2)}, u32[]{:S(2)}) collective-permute-start(f32[25,16,128]{2,1,0:T(8,128)} %get-tuple-element.108), channel_id=1, source_target_pairs={{0,16},{16,32},{32,48},{48,64},{64,80},{80,96},{96,112},{112,0},{1... | collective-permute-start | bytes 614408 | tf_op jit(solution)/shard_map/ppermute | solution.py:523
  16.6 35.9 %collective-permute-start.5 = (f32[25,16,128]{2,1,0:T(8,128)}, f32[25,16,128]{2,1,0:T(8,128)S(1)}, u32[]{:S(2)}, u32[]{:S(2)}) collective-permute-start(f32[25,16,128]{2,1,0:T(8,128)} %get-tuple-element.109), channel_id=1, source_target_pairs={{0,112},{16,0},{32,16},{48,32},{64,48},{80,64},{96,80},{112,96},{1... | collective-permute-start | bytes 614408 | tf_op jit(solution)/shard_map/ppermute | solution.py:523
  151.1 42.1 %copy-start.1 = (f32[3,6,15,15,128]{4,3,2,1,0:T(8,128)S(1)}, f32[3,6,15,15,128]{4,3,2,1,0:T(8,128)}, u32[]{:S(2)}) copy-start(f32[3,6,15,15,128]{4,3,2,1,0:T(8,128)} %turn.1.w_ref) | copy-start | bytes 6220804

commit v7 on v6

--- a/solution.py
+++ b/solution.py
@@ -13,6 +13,7 @@
 EXT = 15
 PAD = 16
 CHUNK = 3
+TURN_UNROLL = 5
 NZ = 128
 DEVICES = 128
 X_LEFT = HALF - 1
@@ -222,6 +223,19 @@
     carry_ref, own_ref, own_mass_ref, own_allow_ref, bits_ref, below_ref, above_ref,
     rows_ref, out_ref, next_ref, xlo_hbm, xhi_hbm, u_ref, mass_ref, allow_ref, xlo_ref, xhi_ref, sems,
 ):
+    layout, edge_count = edge_layout(X_LEFT)
+    edges = ((xlo_ref, xlo_hbm, 0), (xhi_ref, xhi_hbm, 1))
+    for field, (place, planes) in enumerate(layout):
+        for k in range(planes):
+            for edge_ref, plane in ((xlo_ref, k), (xhi_ref, EXT - planes + k)):
+                if field == 1:
+                    edge_ref[place + k] = own_mass_ref[plane]
+                elif field > 1:
+                    edge_ref[place + k] = bits_ref[field - 2, plane]
+    fixed, moved = pl.ds(X_LEFT, edge_count - X_LEFT), pl.ds(0, X_LEFT)
+    sends = [pltpu.make_async_copy(src.at[fixed], dst.at[fixed], sems.at[k]) for src, dst, k in edges]
+    for send in sends:
+        send.start()
     for field, (all_ref, mine_ref) in enumerate(
         ((u_ref, own_ref), (mass_ref, own_mass_ref), (allow_ref, own_allow_ref))
     ):
@@ -242,21 +256,12 @@
         u_ref[plane + 1] = high + weight_high * push
     for k in range(EXT):
         next_ref[k] = u_ref[1 + k]
-    for field, (place, planes) in enumerate(edge_layout(X_LEFT)[0]):
-        for k in range(planes):
-            for edge_ref, plane in ((xlo_ref, k), (xhi_ref, EXT - planes + k)):
-                if field == 0:
-                    edge_ref[place + k] = next_ref[plane]
-                elif field == 1:
-                    edge_ref[place + k] = own_mass_ref[plane]
-                else:
-                    edge_ref[place + k] = bits_ref[field - 2, plane]
-    sends = [
-        pltpu.make_async_copy(xlo_ref, xlo_hbm, sems.at[0]),
-        pltpu.make_async_copy(xhi_ref, xhi_hbm, sems.at[1]),
-    ]
-    for send in sends:
-        send.start()
+    for k in range(X_LEFT):
+        xlo_ref[k] = u_ref[1 + k]
+        xhi_ref[k] = u_ref[1 + EXT - X_LEFT + k]
+    for src, dst, k in edges:
+        sends.append(pltpu.make_async_copy(src.at[moved], dst.at[moved], sems.at[2 + k]))
+        sends[-1].start()
     energy = jnp.zeros((PAD, NZ), f32)
     for k in range(EXT):
         u = next_ref[k]
@@ -283,7 +288,7 @@
         out_shape=[shape(DEVICES, NZ), shape(CARRY, NZ), shape(EXT, PAD, NZ), far(*edge), far(*edge)],
         scratch_shapes=[pltpu.VMEM((EXT + 2, PAD, NZ), f32)] * 3
         + [pltpu.VMEM(edge, f32)] * 2
-        + [pltpu.SemaphoreType.DMA((2,))],
+        + [pltpu.SemaphoreType.DMA((4,))],
         compiler_params=GRANT,
         name="first",
     )(carry, own, mass, allow, bits, below, above)
@@ -461,7 +466,7 @@
         part = pl.ds(i, 1)
         return pltpu.make_async_copy(w_ref.at[:, :, part], w_hbm.at[:, :, part], sems.at[i])
 
-    lax.fori_loop(0, EXT, plane, 0)
+    lax.fori_loop(0, EXT, plane, 0, unroll=TURN_UNROLL)
     for i in range(EXT):
         send(i).wait()
 
@@ -478,39 +483,36 @@
     )(carry, v, counts, spin)
 
 
-def finish_kernel(received_ref, carry_ref, ux_ref, uy_ref, uz_ref, mass_ref, w_ref, v_ref):
-    member = pl.program_id(0)
+def finish_kernel(received_ref, carry_ref, ux_ref, uy_ref, uz_ref, mass_ref, w_ref, v_hbm, v_ref, sems):
     scale, _ = next_scale(received_ref, carry_ref, STEPS - 1)
     wide = jnp.broadcast_to(scale, (EXT, NZ))
-
-    def write(mean_of):
-        for i in range(EXT):
-            counts = mass_ref[i, 0:EXT, :]
-            mean = mean_of(i)
-            for slot in range(SLOTS):
-                v_ref[0, slot, i] = jnp.where(counts > slot, wide * (mean + w_ref[0, slot, i]), 0.0)
-
-    @pl.when(member == 0)
-    def _():
-        write(lambda i: ux_ref[X_LEFT + i, 0:EXT, :])
-
-    @pl.when(member == 1)
-    def _():
-        write(lambda i: uy_ref[pl.ds(Y_LEFT * PAD + i, EXT, stride=PAD), :])
-
-    @pl.when(member == 2)
-    def _():
-        write(lambda i: uz_ref[i, 0:EXT, :])
+    sends = []
+    for i in range(EXT):
+        counts = mass_ref[i, 0:EXT, :]
+        means = [
+            ux_ref[X_LEFT + i, 0:EXT, :],
+            uy_ref[pl.ds(Y_LEFT * PAD + i, EXT, stride=PAD), :],
+            uz_ref[i, 0:EXT, :],
+        ]
+        for slot in range(SLOTS):
+            live = counts > slot
+            for member in range(3):
+                v_ref[member, slot, i] = jnp.where(live, wide * (means[member] + w_ref[member, slot, i]), 0.0)
+        if i % CHUNK == CHUNK - 1:
+            part = pl.ds(i - (CHUNK - 1), CHUNK)
+            sends.append(pltpu.make_async_copy(v_ref.at[:, :, part], v_hbm.at[:, :, part], sems.at[i // CHUNK]))
+            sends[-1].start()
+    for send in sends:
+        send.wait()
 
 
 def finish(received, carry, ux, uy, uz, mass, w):
-    part = pl.BlockSpec((1, SLOTS, EXT, EXT, NZ), lambda c: (c, 0, 0, 0, 0))
     return pl.pallas_call(
         finish_kernel,
-        grid=(3,),
-        in_specs=[VMEM] * 6 + [part],
-        out_specs=part,
-        out_shape=shape(3, SLOTS, EXT, EXT, NZ),
+        in_specs=[VMEM] * 7,
+        out_specs=ANY,
+        out_shape=far(3, SLOTS, EXT, EXT, NZ),
+        scratch_shapes=[pltpu.VMEM((3, SLOTS, EXT, EXT, NZ), f32), pltpu.SemaphoreType.DMA((EXT // CHUNK,))],
         compiler_params=GRANT,
         name="finish",
     )(received, carry, ux, uy.reshape(full_planes(Y_LEFT) * PAD, NZ), uz, mass, w)

time: 196 us -> 195 us (level)
  transfers between devices with their start and end apart: 6 -> 6, of which waited for: 0 -> 0; matrix products, arithmetic and copies ran while one was open for 0% -> 0% of each run, Pallas kernels for 3% -> 2%
where the time goes in v7:
time: 195 us
  blocking collectives  170 us (87%)
  starting transfers between devices  13.4 us (7%)
  Pallas kernels  11 us (6%)
    all_to_all x12, blocking collectives, sum_over_devices(): return lax.all_to_all(rows, ('bx', 'by'), 0, 0, tiled=True)  170 us
    ppermute x3, starting transfers between devices, exchange(): lax.ppermute(high_edge, axis, up)  6.97 us
    ppermute x3, starting transfers between devices, exchange(): lax.ppermute(low_edge, axis, down)  6.46 us
  transfers between devices with their start and end apart: 6, of which 0 were waited for; matrix products, arithmetic and copies ran while one was open for 0% of the time, Pallas kernels for 2%

profile of v7, /device:TPU:1, one launch (start us, length us, event | category | flops | bytes accessed | tf_op | source)
XLA Modules:
  0.0 194.8 jit_solution(10932735681193212537)
XLA Ops:
  0.0 2.3 %prep.1 = (f32[15,16,128]{2,1,0:T(8,128)S(1)}, f32[15,16,128]{2,1,0:T(8,128)S(1)}, f32[15,16,128]{2,1,0:T(8,128)S(1)}, f32[16,16,128]{2,1,0:T(8,128)S(1)}, f32[1...) custom-call(s32[12]{0:T(128)} %shift_hbm.1, ...), custom_call_target="tpu_custom_call" | custom-call | tf_op jit(solution)/shard_map/prep/pallas_call | solution.py:156
  2.3 0.6 spread.1
  3.0 3.1 %collective-permute-start.2 = (f32[33,16,128]{2,1,0:T(8,128)S(1)}, f32[33,16,128]{2,1,0:T(8,128)S(1)}, u32[]{:S(2)}, u32[]{:S(2)}) collective-permute-start(f32[33,16,128]{2,1,0:T(8,128)S(1)} %get-tuple-element.98), channel_id=1, source_target_pairs={{0,1},{1,2},{2,3},{3,4},{4,5},{5,6},{6,7},{7,8},{8,9},{9,10},{10,1... | collective-permute-start | bytes 811016 | tf_op jit(solution)/shard_map/ppermute | solution.py:525
  6.0 2.7 %collective-permute-start = (f32[3,16,128]{2,1,0:T(8,128)S(1)}, f32[3,16,128]{2,1,0:T(8,128)S(1)}, u32[]{:S(2)}, u32[]{:S(2)}) collective-permute-start(f32[3,16,128]{2,1,0:T(8,128)S(1)} %get-tuple-element.83), channel_id=1, source_target_pairs={{0,16},{16,32},{32,48},{48,64},{64,80},{80,96},{96,112},{112,0},{1... | collective-permute-start | bytes 73736 | tf_op jit(solution)/shard_map/ppermute | solution.py:525
  8.8 2.5 %collective-permute-start.1 = (f32[3,16,128]{2,1,0:T(8,128)S(1)}, f32[3,16,128]{2,1,0:T(8,128)S(1)}, u32[]{:S(2)}, u32[]{:S(2)}) collective-permute-start(f32[3,16,128]{2,1,0:T(8,128)S(1)} %get-tuple-element.84), channel_id=1, source_target_pairs={{0,112},{16,0},{32,16},{48,32},{64,48},{80,64},{96,80},{112,96},{1... | collective-permute-start | bytes 73736 | tf_op jit(solution)/shard_map/ppermute | solution.py:525
  11.3 3.0 %turn.1.w_ref = f32[3,6,15,15,128]{4,3,2,1,0:T(8,128)} custom-call(f32[56,128]{1,0:T(8,128)S(1)} %get-tuple-element.76.carry_ref, f32[3,6,15,15,128]{4,3,2,1,0:T(8,128)S(1)} %copy-done, s32[15,15,128]{2,1,0:T(8,128)S(1)} %copy-done.4, s32[12,15,15,128]{3,2,1,0:T(8,128)S(1)} %copy-done.3), custom_call_target="tpu_custom_call" | custom-call | tf_op jit(solution)/shard_map/turn/pallas_call | solution.py:475
  14.3 0.8 first.1
  15.1 1.1 collective-permute-start.4
  16.3 4.0 %collective-permute-start.5 = (f32[25,16,128]{2,1,0:T(8,128)}, f32[25,16,128]{2,1,0:T(8,128)S(1)}, u32[]{:S(2)}, u32[]{:S(2)}) collective-permute-start(f32[25,16,128]{2,1,0:T(8,128)} %get-tuple-element.109), channel_id=1, source_target_pairs={{0,112},{16,0},{32,16},{48,32},{64,48},{80,64},{96,80},{112,96},{1... | collective-permute-start | bytes 614408 | tf_op jit(solution)/shard_map/ppermute | solution.py:525
  20.3 17.7 %all_to_all.134 = f32[128,1,128]{2,1,0:T(1,128)S(1)} all-to-all(f32[128,1,128]{2,1,0:T(1,128)S(1)} %bitcast.64), channel_id=1, replica_groups=mesh['bx'=8,'by'=16] {'bx','by'}, dimensions={0} | all-to-all | bytes 131072 | tf_op jit(solution)/shard_map/all_to_all | solution.py:529
  38.0 0.3 join.2
  38.3 0.2 collide.11
  38.5 13.8 %all_to_all.135 = f32[128,1,128]{2,1,0:T(1,128)S(1)} all-to-all(f32[128,1,128]{2,1,0:T(1,128)S(1)} %bitcast.67), channel_id=1, replica_groups=mesh['bx'=8,'by'=16] {'bx','by'}, dimensions={0} | all-to-all | bytes 131072 | tf_op jit(solution)/shard_map/all_to_all | solution.py:529
  52.4 0.3 join.3
  52.7 0.2 collide.12
  52.9 13.8 %all_to_all.136 = f32[128,1,128]{2,1,0:T(1,128)S(1)} all-to-all(f32[128,1,128]{2,1,0:T(1,128)S(1)} %bitcast.68), channel_id=1, replica_groups=mesh['bx'=8,'by'=16] {'bx','by'}, dimensions={0} | all-to-all | bytes 131072 | tf_op jit(solution)/shard_map/all_to_all | solution.py:529
  66.7 0.2 collide.13
  66.9 13.8 %all_to_all.137 = f32[128,1,128]{2,1,0:T(1,128)S(1)} all-to-all(f32[128,1,128]{2,1,0:T(1,128)S(1)} %bitcast.69), channel_id=1, replica_groups=mesh['bx'=8,'by'=16] {'bx','by'}, dimensions={0} | all-to-all | bytes 131072 | tf_op jit(solution)/shard_map/all_to_all | solution.py:529
  81.0 13.8 %all_to_all.138 = f32[128,1,128]{2,1,0:T(1,128)S(1)} all-to-all(f32[128,1,128]{2,1,0:T(1,128)S(1)} %bitcast.70), channel_id=1, replica_groups=mesh['bx'=8,'by'=16] {'bx','by'}, dimensions={0} | all-to-all | bytes 131072 | tf_op jit(solution)/shard_map/all_to_all | solution.py:529
  94.8 0.2 collide.15
  95.0 13.8 %all_to_all.139 = f32[128,1,128]{2,1,0:T(1,128)S(1)} all-to-all(f32[128,1,128]{2,1,0:T(1,128)S(1)} %bitcast.71), channel_id=1, replica_groups=mesh['bx'=8,'by'=16] {'bx','by'}, dimensions={0} | all-to-all | bytes 131072 | tf_op jit(solution)/shard_map/all_to_all | solution.py:529
  109.0 13.8 %all_to_all.140 = f32[128,1,128]{2,1,0:T(1,128)S(1)} all-to-all(f32[128,1,128]{2,1,0:T(1,128)S(1)} %bitcast.72), channel_id=1, replica_groups=mesh['bx'=8,'by'=16] {'bx','by'}, dimensions={0} | all-to-all | bytes 131072 | tf_op jit(solution)/shard_map/all_to_all | solution.py:529
  122.9 0.2 collide.17
  123.1 13.8 %all_to_all.141 = f32[128,1,128]{2,1,0:T(1,128)S(1)} all-to-all(f32[128,1,128]{2,1,0:T(1,128)S(1)} %bitcast.73), channel_id=1, replica_groups=mesh['bx'=8,'by'=16] {'bx','by'}, dimensions={0} | all-to-all | bytes 131072 | tf_op jit(solution)/shard_map/all_to_all | solution.py:529
  137.1 13.8 %all_to_all.142 = f32[128,1,128]{2,1,0:T(1,128)S(1)} all-to-all(f32[128,1,128]{2,1,0:T(1,128)S(1)} %bitcast.74), channel_id=1, replica_groups=mesh['bx'=8,'by'=16] {'bx','by'}, dimensions={0} | all-to-all | bytes 131072 | tf_op jit(solution)/shard_map/all_to_all | solution.py:529
  151.0 0.2 collide.19
  151.2 13.8 %all_to_all.143 = f32[128,1,128]{2,1,0:T(1,128)S(1)} all-to-all(f32[128,1,128]{2,1,0:T(1,128)S(1)} %bitcast.75), channel_id=1, replica_groups=mesh['bx'=8,'by'=16] {'bx','by'}, dimensions={0} | all-to-all | bytes 131072 | tf_op jit(solution)/shard_map/all_to_all | solution.py:529
  165.0 0.2 collide.20
  165.2 13.8 %all_to_all.144 = f32[128,1,128]{2,1,0:T(1,128)S(1)} all-to-all(f32[128,1,128]{2,1,0:T(1,128)S(1)} %bitcast.66), channel_id=1, replica_groups=mesh['bx'=8,'by'=16] {'bx','by'}, dimensions={0} | all-to-all | bytes 131072 | tf_op jit(solution)/shard_map/all_to_all | solution.py:529
  179.1 0.2 collide.21
  179.3 13.8 %all_to_all.145 = f32[128,1,128]{2,1,0:T(1,128)S(1)} all-to-all(f32[128,1,128]{2,1,0:T(1,128)S(1)} %bitcast.65), channel_id=1, replica_groups=mesh['bx'=8,'by'=16] {'bx','by'}, dimensions={0} | all-to-all | bytes 131072 | tf_op jit(solution)/shard_map/all_to_all | solution.py:529
  193.1 1.5 finish.1
  (20 shorter events, 0.6 us)
Async XLA Ops:
  0.0 2.3 %copy-start.2 = (s32[12,15,15,128]{3,2,1,0:T(8,128)S(1)}, s32[12,15,15,128]{3,2,1,0:T(8,128)}, u32[]{:S(2)}) copy-start(s32[12,15,15,128]{3,2,1,0:T(8,128)} %flag_ref) | copy-start | bytes 4147204
  0.0 11.2 %copy-start.4 = (s32[15,15,128]{2,1,0:T(8,128)S(1)}, s32[15,15,128]{2,1,0:T(8,128)}, u32[]{:S(2)}) copy-start(s32[15,15,128]{2,1,0:T(8,128)} %count_ref) | copy-start | bytes 345604
  0.0 11.2 %copy-start = (f32[3,6,15,15,128]{4,3,2,1,0:T(8,128)S(1)}, f32[3,6,15,15,128]{4,3,2,1,0:T(8,128)}, u32[]{:S(2)}) copy-start(f32[3,6,15,15,128]{4,3,2,1,0:T(8,128)} %v_ref) | copy-start | bytes 6220804
  0.0 11.2 %copy-start.3 = (s32[12,15,15,128]{3,2,1,0:T(8,128)S(1)}, s32[12,15,15,128]{3,2,1,0:T(8,128)}, u32[]{:S(2)}) copy-start(s32[12,15,15,128]{3,2,1,0:T(8,128)} %spin_ref) | copy-start | bytes 4147204
  3.0 35.1 %collective-permute-start.2 = (f32[33,16,128]{2,1,0:T(8,128)S(1)}, f32[33,16,128]{2,1,0:T(8,128)S(1)}, u32[]{:S(2)}, u32[]{:S(2)}) collective-permute-start(f32[33,16,128]{2,1,0:T(8,128)S(1)} %get-tuple-element.98), channel_id=1, source_target_pairs={{0,1},{1,2},{2,3},{3,4},{4,5},{5,6},{6,7},{7,8},{8,9},{9,10},{10,1... | collective-permute-start | bytes 811016 | tf_op jit(solution)/shard_map/ppermute | solution.py:525
  6.0 32.0 %collective-permute-start.3 = (f32[33,16,128]{2,1,0:T(8,128)S(1)}, f32[33,16,128]{2,1,0:T(8,128)S(1)}, u32[]{:S(2)}, u32[]{:S(2)}) collective-permute-start(f32[33,16,128]{2,1,0:T(8,128)S(1)} %get-tuple-element.99), channel_id=1, source_target_pairs={{0,15},{1,0},{2,1},{3,2},{4,3},{5,4},{6,5},{7,6},{8,7},{9,8},{10,9... | collective-permute-start | bytes 811016 | tf_op jit(solution)/shard_map/ppermute | solution.py:525
  6.0 8.2 %collective-permute-start = (f32[3,16,128]{2,1,0:T(8,128)S(1)}, f32[3,16,128]{2,1,0:T(8,128)S(1)}, u32[]{:S(2)}, u32[]{:S(2)}) collective-permute-start(f32[3,16,128]{2,1,0:T(8,128)S(1)} %get-tuple-element.83), channel_id=1, source_target_pairs={{0,16},{16,32},{32,48},{48,64},{64,80},{80,96},{96,112},{112,0},{1... | collective-permute-start | bytes 73736 | tf_op jit(solution)/shard_map/ppermute | solution.py:525
  8.8 5.5 %collective-permute-start.1 = (f32[3,16,128]{2,1,0:T(8,128)S(1)}, f32[3,16,128]{2,1,0:T(8,128)S(1)}, u32[]{:S(2)}, u32[]{:S(2)}) collective-permute-start(f32[3,16,128]{2,1,0:T(8,128)S(1)} %get-tuple-element.84), channel_id=1, source_target_pairs={{0,112},{16,0},{32,16},{48,32},{64,48},{80,64},{96,80},{112,96},{1... | collective-permute-start | bytes 73736 | tf_op jit(solution)/shard_map/ppermute | solution.py:525
  15.1 37.3 %collective-permute-start.4 = (f32[25,16,128]{2,1,0:T(8,128)}, f32[25,16,128]{2,1,0:T(8,128)S(1)}, u32[]{:S(2)}, u32[]{:S(2)}) collective-permute-start(f32[25,16,128]{2,1,0:T(8,128)} %get-tuple-element.108), channel_id=1, source_target_pairs={{0,16},{16,32},{32,48},{48,64},{64,80},{80,96},{96,112},{112,0},{1... | collective-permute-start | bytes 614408 | tf_op jit(solution)/shard_map/ppermute | solution.py:525
  16.3 36.1 %collective-permute-start.5 = (f32[25,16,128]{2,1,0:T(8,128)}, f32[25,16,128]{2,1,0:T(8,128)S(1)}, u32[]{:S(2)}, u32[]{:S(2)}) collective-permute-start(f32[25,16,128]{2,1,0:T(8,128)} %get-tuple-element.109), channel_id=1, source_target_pairs={{0,112},{16,0},{32,16},{48,32},{64,48},{80,64},{96,80},{112,96},{1... | collective-permute-start | bytes 614408 | tf_op jit(solution)/shard_map/ppermute | solution.py:525
  151.0 42.1 %copy-start.1 = (f32[3,6,15,15,128]{4,3,2,1,0:T(8,128)S(1)}, f32[3,6,15,15,128]{4,3,2,1,0:T(8,128)}, u32[]{:S(2)}) copy-start(f32[3,6,15,15,128]{4,3,2,1,0:T(8,128)} %turn.1.w_ref) | copy-start | bytes 6220804

commit v8 on v7

--- a/solution.py
+++ b/solution.py
@@ -411,7 +411,7 @@
     )(received, carry, u, weight, mass)
 
 
-def turn_kernel(carry_ref, v_ref, count_ref, spin_ref, w_hbm, w_ref, sems):
+def turn_kernel(carry_ref, v_ref, ux_ref, uy_ref, uz_ref, spin_ref, w_hbm, w_ref, sems):
     shifts = [whole(carry_ref, SHIFT_ROW + step) for step in range(STEPS)]
 
     def plane(i, carry):
@@ -439,23 +439,9 @@
             [2.0 * (x * z - real * y), 2.0 * (y * z + real * x), (rr + zz) - (xx + yy)],
         ]
         rows = [[unit * value for value in row] for row in rows]
-        counts = pltpu.roll(count_ref[i], shifts[0], 1)
-        inverse = 1.0 / jnp.maximum(counts.astype(f32), 1.0)
-        values = [
-            [
-                jnp.where(counts > slot, pltpu.roll(v_ref[member, slot, i], shifts[0], 1), 0.0)
-                for slot in range(SLOTS)
-            ]
-            for member in range(3)
-        ]
-        mean = []
-        for member in range(3):
-            moment = values[member][0]
-            for slot in range(1, SLOTS):
-                moment = moment + values[member][slot]
-            mean.append(moment * inverse)
+        mean = [mean_ref[i, 0:EXT, :] * (1.0 / BIG) for mean_ref in (ux_ref, uy_ref, uz_ref)]
         for slot in range(SLOTS):
-            rest = [values[member][slot] - mean[member] for member in range(3)]
+            rest = [pltpu.roll(v_ref[member, slot, i], shifts[0], 1) - mean[member] for member in range(3)]
             for member in range(3):
                 turned = rows[member][0] * rest[0] + rows[member][1] * rest[1] + rows[member][2] * rest[2]
                 w_ref[member, slot, i] = turned
@@ -471,16 +457,16 @@
         send(i).wait()
 
 
-def turn(carry, v, counts, spin):
+def turn(carry, v, ux, uy, uz, spin):
     return pl.pallas_call(
         turn_kernel,
-        in_specs=[VMEM] * 4,
+        in_specs=[VMEM] * 6,
         out_specs=ANY,
         out_shape=far(3, SLOTS, EXT, EXT, NZ),
         scratch_shapes=[pltpu.VMEM((3, SLOTS, EXT, EXT, NZ), f32), pltpu.SemaphoreType.DMA((EXT,))],
         compiler_params=GRANT,
         name="turn",
-    )(carry, v, counts, spin)
+    )(carry, v, ux, uy, uz, spin)
 
 
 def finish_kernel(received_ref, carry_ref, ux_ref, uy_ref, uz_ref, mass_ref, w_ref, v_hbm, v_ref, sems):
@@ -531,11 +517,12 @@
 
 def per_device(v, counts, spin, flags, parity, shifts, heat):
     ux, mass, allow, uy, uz, low, high, carry = prep(shifts, parity, heat, v, counts, flags)
-    carry, v, counts, spin, flags = lax.optimization_barrier((carry, v, counts, spin, flags))
+    carry, v, spin, flags = lax.optimization_barrier((carry, v, spin, flags))
+    mean_y = uy
     above, below = exchange(low, high, "bx")
     bits, uy, y_mass, y_bits, ylo, yhi = spread(carry, mass, uy, flags)
     y_above, y_below = exchange(ylo, yhi, "by")
-    w = turn(carry, v, counts, spin)
+    w = turn(carry, v, ux, mean_y, uz, spin)
     below, above, w = lax.optimization_barrier((below, above, w))
     rows, carry, ux, xlo, xhi = first(carry, ux, mass, allow, bits, below, above)
     received = sum_over_devices(rows)

time: 195 us -> 195 us (level)
  no operation moved by 1% of the time
where the time goes in v8:
time: 195 us
  blocking collectives  170 us (87%)
  starting transfers between devices  13.4 us (7%)
  Pallas kernels  10.8 us (6%)
    all_to_all x12, blocking collectives, sum_over_devices(): return lax.all_to_all(rows, ('bx', 'by'), 0, 0, tiled=True)  170 us
    ppermute x3, starting transfers between devices, exchange(): lax.ppermute(high_edge, axis, up)  7.11 us
    ppermute x3, starting transfers between devices, exchange(): lax.ppermute(low_edge, axis, down)  6.33 us
  transfers between devices with their start and end apart: 6, of which 0 were waited for; matrix products, arithmetic and copies ran while one was open for 0% of the time, Pallas kernels for 2%

profile of v8, /device:TPU:1, one launch (start us, length us, event | category | flops | bytes accessed | tf_op | source)
XLA Modules:
  0.0 194.8 jit_solution(14758000011744015886)
XLA Ops:
  0.0 2.3 %prep.1 = (f32[15,16,128]{2,1,0:T(8,128)S(1)}, f32[15,16,128]{2,1,0:T(8,128)S(1)}, f32[15,16,128]{2,1,0:T(8,128)S(1)}, f32[16,16,128]{2,1,0:T(8,128)S(1)}, f32[1...) custom-call(s32[12]{0:T(128)} %shift_hbm.1, ...), custom_call_target="tpu_custom_call" | custom-call | tf_op jit(solution)/shard_map/prep/pallas_call | solution.py:156
  2.3 0.6 spread.1
  2.9 3.1 %collective-permute-start.2 = (f32[33,16,128]{2,1,0:T(8,128)S(1)}, f32[33,16,128]{2,1,0:T(8,128)S(1)}, u32[]{:S(2)}, u32[]{:S(2)}) collective-permute-start(f32[33,16,128]{2,1,0:T(8,128)S(1)} %get-tuple-element.97), channel_id=1, source_target_pairs={{0,1},{1,2},{2,3},{3,4},{4,5},{5,6},{6,7},{7,8},{8,9},{9,10},{10,1... | collective-permute-start | bytes 811016 | tf_op jit(solution)/shard_map/ppermute | solution.py:511
  6.0 2.7 %collective-permute-start = (f32[3,16,128]{2,1,0:T(8,128)S(1)}, f32[3,16,128]{2,1,0:T(8,128)S(1)}, u32[]{:S(2)}, u32[]{:S(2)}) collective-permute-start(f32[3,16,128]{2,1,0:T(8,128)S(1)} %get-tuple-element.82), channel_id=1, source_target_pairs={{0,16},{16,32},{32,48},{48,64},{64,80},{80,96},{96,112},{112,0},{1... | collective-permute-start | bytes 73736 | tf_op jit(solution)/shard_map/ppermute | solution.py:511
  8.8 2.5 %collective-permute-start.1 = (f32[3,16,128]{2,1,0:T(8,128)S(1)}, f32[3,16,128]{2,1,0:T(8,128)S(1)}, u32[]{:S(2)}, u32[]{:S(2)}) collective-permute-start(f32[3,16,128]{2,1,0:T(8,128)S(1)} %get-tuple-element.83), channel_id=1, source_target_pairs={{0,112},{16,0},{32,16},{48,32},{64,48},{80,64},{96,80},{112,96},{1... | collective-permute-start | bytes 73736 | tf_op jit(solution)/shard_map/ppermute | solution.py:511
  11.2 2.9 %turn.1.w_ref = f32[3,6,15,15,128]{4,3,2,1,0:T(8,128)} custom-call(f32[56,128]{1,0:T(8,128)S(1)} %get-tuple-element.75.carry_ref, f32[3,6,15,15,128]{4,3,2,1,0:T(8,128)S(1)} %copy-done, f32[15,16,128]{2,1,0:T(8,128)S(1)} %get-tuple-element.76.ux_ref.own_ref, f32[16,16,128]{2,1,0:T(8,128)S(1)} %get-tuple-element.79.uy_ref, ...), custom_call_target="tpu_custom_call" | custom-call | tf_op jit(solution)/shard_map/turn/pallas_call | solution.py:461
  14.1 0.8 first.1
  15.0 1.3 collective-permute-start.4
  16.3 3.9 %collective-permute-start.5 = (f32[25,16,128]{2,1,0:T(8,128)}, f32[25,16,128]{2,1,0:T(8,128)S(1)}, u32[]{:S(2)}, u32[]{:S(2)}) collective-permute-start(f32[25,16,128]{2,1,0:T(8,128)} %get-tuple-element.108), channel_id=1, source_target_pairs={{0,112},{16,0},{32,16},{48,32},{64,48},{80,64},{96,80},{112,96},{1... | collective-permute-start | bytes 614408 | tf_op jit(solution)/shard_map/ppermute | solution.py:511
  20.1 17.9 %all_to_all.134 = f32[128,1,128]{2,1,0:T(1,128)S(1)} all-to-all(f32[128,1,128]{2,1,0:T(1,128)S(1)} %bitcast.64), channel_id=1, replica_groups=mesh['bx'=8,'by'=16] {'bx','by'}, dimensions={0} | all-to-all | bytes 131072 | tf_op jit(solution)/shard_map/all_to_all | solution.py:515
  38.0 0.3 join.2
  38.3 0.2 collide.11
  38.5 13.8 %all_to_all.135 = f32[128,1,128]{2,1,0:T(1,128)S(1)} all-to-all(f32[128,1,128]{2,1,0:T(1,128)S(1)} %bitcast.67), channel_id=1, replica_groups=mesh['bx'=8,'by'=16] {'bx','by'}, dimensions={0} | all-to-all | bytes 131072 | tf_op jit(solution)/shard_map/all_to_all | solution.py:515
  52.4 0.3 join.3
  52.7 0.2 collide.12
  52.8 13.8 %all_to_all.136 = f32[128,1,128]{2,1,0:T(1,128)S(1)} all-to-all(f32[128,1,128]{2,1,0:T(1,128)S(1)} %bitcast.68), channel_id=1, replica_groups=mesh['bx'=8,'by'=16] {'bx','by'}, dimensions={0} | all-to-all | bytes 131072 | tf_op jit(solution)/shard_map/all_to_all | solution.py:515
  66.7 0.2 collide.13
  66.9 13.8 %all_to_all.137 = f32[128,1,128]{2,1,0:T(1,128)S(1)} all-to-all(f32[128,1,128]{2,1,0:T(1,128)S(1)} %bitcast.69), channel_id=1, replica_groups=mesh['bx'=8,'by'=16] {'bx','by'}, dimensions={0} | all-to-all | bytes 131072 | tf_op jit(solution)/shard_map/all_to_all | solution.py:515
  80.9 13.8 %all_to_all.138 = f32[128,1,128]{2,1,0:T(1,128)S(1)} all-to-all(f32[128,1,128]{2,1,0:T(1,128)S(1)} %bitcast.70), channel_id=1, replica_groups=mesh['bx'=8,'by'=16] {'bx','by'}, dimensions={0} | all-to-all | bytes 131072 | tf_op jit(solution)/shard_map/all_to_all | solution.py:515
  94.8 0.2 collide.15
  95.0 13.8 %all_to_all.139 = f32[128,1,128]{2,1,0:T(1,128)S(1)} all-to-all(f32[128,1,128]{2,1,0:T(1,128)S(1)} %bitcast.71), channel_id=1, replica_groups=mesh['bx'=8,'by'=16] {'bx','by'}, dimensions={0} | all-to-all | bytes 131072 | tf_op jit(solution)/shard_map/all_to_all | solution.py:515
  109.0 13.8 %all_to_all.140 = f32[128,1,128]{2,1,0:T(1,128)S(1)} all-to-all(f32[128,1,128]{2,1,0:T(1,128)S(1)} %bitcast.72), channel_id=1, replica_groups=mesh['bx'=8,'by'=16] {'bx','by'}, dimensions={0} | all-to-all | bytes 131072 | tf_op jit(solution)/shard_map/all_to_all | solution.py:515
  122.9 0.2 collide.17
  123.1 13.8 %all_to_all.141 = f32[128,1,128]{2,1,0:T(1,128)S(1)} all-to-all(f32[128,1,128]{2,1,0:T(1,128)S(1)} %bitcast.73), channel_id=1, replica_groups=mesh['bx'=8,'by'=16] {'bx','by'}, dimensions={0} | all-to-all | bytes 131072 | tf_op jit(solution)/shard_map/all_to_all | solution.py:515
  136.9 0.2 collide.18
  137.1 13.8 %all_to_all.142 = f32[128,1,128]{2,1,0:T(1,128)S(1)} all-to-all(f32[128,1,128]{2,1,0:T(1,128)S(1)} %bitcast.74), channel_id=1, replica_groups=mesh['bx'=8,'by'=16] {'bx','by'}, dimensions={0} | all-to-all | bytes 131072 | tf_op jit(solution)/shard_map/all_to_all | solution.py:515
  151.0 0.2 collide.19
  151.2 13.8 %all_to_all.143 = f32[128,1,128]{2,1,0:T(1,128)S(1)} all-to-all(f32[128,1,128]{2,1,0:T(1,128)S(1)} %bitcast.75), channel_id=1, replica_groups=mesh['bx'=8,'by'=16] {'bx','by'}, dimensions={0} | all-to-all | bytes 131072 | tf_op jit(solution)/shard_map/all_to_all | solution.py:515
  165.2 13.8 %all_to_all.144 = f32[128,1,128]{2,1,0:T(1,128)S(1)} all-to-all(f32[128,1,128]{2,1,0:T(1,128)S(1)} %bitcast.66), channel_id=1, replica_groups=mesh['bx'=8,'by'=16] {'bx','by'}, dimensions={0} | all-to-all | bytes 131072 | tf_op jit(solution)/shard_map/all_to_all | solution.py:515
  179.1 0.2 collide.21
  179.3 13.8 %all_to_all.145 = f32[128,1,128]{2,1,0:T(1,128)S(1)} all-to-all(f32[128,1,128]{2,1,0:T(1,128)S(1)} %bitcast.65), channel_id=1, replica_groups=mesh['bx'=8,'by'=16] {'bx','by'}, dimensions={0} | all-to-all | bytes 131072 | tf_op jit(solution)/shard_map/all_to_all | solution.py:515
  193.1 1.5 finish.1
  (18 shorter events, 0.6 us)
Async XLA Ops:
  0.0 2.3 %copy-start.2 = (s32[12,15,15,128]{3,2,1,0:T(8,128)S(1)}, s32[12,15,15,128]{3,2,1,0:T(8,128)}, u32[]{:S(2)}) copy-start(s32[12,15,15,128]{3,2,1,0:T(8,128)} %flag_ref) | copy-start | bytes 4147204
  0.0 11.2 %copy-start = (f32[3,6,15,15,128]{4,3,2,1,0:T(8,128)S(1)}, f32[3,6,15,15,128]{4,3,2,1,0:T(8,128)}, u32[]{:S(2)}) copy-start(f32[3,6,15,15,128]{4,3,2,1,0:T(8,128)} %v_ref) | copy-start | bytes 6220804
  0.0 11.2 %copy-start.3 = (s32[12,15,15,128]{3,2,1,0:T(8,128)S(1)}, s32[12,15,15,128]{3,2,1,0:T(8,128)}, u32[]{:S(2)}) copy-start(s32[12,15,15,128]{3,2,1,0:T(8,128)} %spin_ref) | copy-start | bytes 4147204
  2.9 35.1 %collective-permute-start.2 = (f32[33,16,128]{2,1,0:T(8,128)S(1)}, f32[33,16,128]{2,1,0:T(8,128)S(1)}, u32[]{:S(2)}, u32[]{:S(2)}) collective-permute-start(f32[33,16,128]{2,1,0:T(8,128)S(1)} %get-tuple-element.97), channel_id=1, source_target_pairs={{0,1},{1,2},{2,3},{3,4},{4,5},{5,6},{6,7},{7,8},{8,9},{9,10},{10,1... | collective-permute-start | bytes 811016 | tf_op jit(solution)/shard_map/ppermute | solution.py:511
  6.0 32.0 %collective-permute-start.3 = (f32[33,16,128]{2,1,0:T(8,128)S(1)}, f32[33,16,128]{2,1,0:T(8,128)S(1)}, u32[]{:S(2)}, u32[]{:S(2)}) collective-permute-start(f32[33,16,128]{2,1,0:T(8,128)S(1)} %get-tuple-element.98), channel_id=1, source_target_pairs={{0,15},{1,0},{2,1},{3,2},{4,3},{5,4},{6,5},{7,6},{8,7},{9,8},{10,9... | collective-permute-start | bytes 811016 | tf_op jit(solution)/shard_map/ppermute | solution.py:511
  6.0 8.1 %collective-permute-start = (f32[3,16,128]{2,1,0:T(8,128)S(1)}, f32[3,16,128]{2,1,0:T(8,128)S(1)}, u32[]{:S(2)}, u32[]{:S(2)}) collective-permute-start(f32[3,16,128]{2,1,0:T(8,128)S(1)} %get-tuple-element.82), channel_id=1, source_target_pairs={{0,16},{16,32},{32,48},{48,64},{64,80},{80,96},{96,112},{112,0},{1... | collective-permute-start | bytes 73736 | tf_op jit(solution)/shard_map/ppermute | solution.py:511
  8.8 5.4 %collective-permute-start.1 = (f32[3,16,128]{2,1,0:T(8,128)S(1)}, f32[3,16,128]{2,1,0:T(8,128)S(1)}, u32[]{:S(2)}, u32[]{:S(2)}) collective-permute-start(f32[3,16,128]{2,1,0:T(8,128)S(1)} %get-tuple-element.83), channel_id=1, source_target_pairs={{0,112},{16,0},{32,16},{48,32},{64,48},{80,64},{96,80},{112,96},{1... | collective-permute-start | bytes 73736 | tf_op jit(solution)/shard_map/ppermute | solution.py:511
  15.0 37.4 %collective-permute-start.4 = (f32[25,16,128]{2,1,0:T(8,128)}, f32[25,16,128]{2,1,0:T(8,128)S(1)}, u32[]{:S(2)}, u32[]{:S(2)}) collective-permute-start(f32[25,16,128]{2,1,0:T(8,128)} %get-tuple-element.107), channel_id=1, source_target_pairs={{0,16},{16,32},{32,48},{48,64},{64,80},{80,96},{96,112},{112,0},{1... | collective-permute-start | bytes 614408 | tf_op jit(solution)/shard_map/ppermute | solution.py:511
  16.3 36.1 %collective-permute-start.5 = (f32[25,16,128]{2,1,0:T(8,128)}, f32[25,16,128]{2,1,0:T(8,128)S(1)}, u32[]{:S(2)}, u32[]{:S(2)}) collective-permute-start(f32[25,16,128]{2,1,0:T(8,128)} %get-tuple-element.108), channel_id=1, source_target_pairs={{0,112},{16,0},{32,16},{48,32},{64,48},{80,64},{96,80},{112,96},{1... | collective-permute-start | bytes 614408 | tf_op jit(solution)/shard_map/ppermute | solution.py:511
  151.0 42.1 %copy-start.1 = (f32[3,6,15,15,128]{4,3,2,1,0:T(8,128)S(1)}, f32[3,6,15,15,128]{4,3,2,1,0:T(8,128)}, u32[]{:S(2)}) copy-start(f32[3,6,15,15,128]{4,3,2,1,0:T(8,128)} %turn.1.w_ref) | copy-start | bytes 6220804
